TPU v7x, 128 devices: a whole 4x4x4 slice. The times are simulated.
128 devices in a mesh: dp: 16 (over z, y), ep: 8 (over x, core).
Axes of the slice: x: 4, y: 4, z: 4, core: 2. Of those that a mesh axis runs over, the one named last changes fastest.
Arguments:
- tok_x: bfloat16 [32768, 4096], P(('dp', 'ep'))
- tok_dy: bfloat16 [32768, 4096], P(('dp', 'ep'))
- exp_first: int32 [32768], P(('dp', 'ep'))
- exp_second: int32 [32768], P(('dp', 'ep'))
- eligible: int32 [32768, 16], P(('dp', 'ep'))
- slot_first: int32 [32768], P(('dp', 'ep'))
- slot_second: int32 [32768], P(('dp', 'ep'))
- ln_weight: bfloat16 [4096], replicated
- ln_bias: bfloat16 [4096], replicated
- router: bfloat16 [4096, 16], replicated
- w_gate: bfloat16 [16, 4096, 448], P('ep')
- w_up: bfloat16 [16, 4096, 448], P('ep')
- w_down: bfloat16 [16, 448, 4096], P('ep')
Outputs:
- output 1: bfloat16 [32768, 4096], P(('dp', 'ep'))
- output 2: bfloat16 [32768, 4096], P(('dp', 'ep'))
- output 3: float32 [16, 4096, 448], P('ep')
- output 4: float32 [16, 4096, 448], P('ep')
- output 5: float32 [16, 448, 4096], P('ep')
- output 6: float32 [4096, 16], replicated
- output 7: float32 [4096], replicated
- output 8: float32 [4096], replicated
All inputs are finite; a program needn't handle non-finite values.
Results may differ from a plain program's by a relative error of at most 0.00505461.
Values are sent between devices in bfloat16 or wider.
A program may use at most 1 GiB of HBM per device.

v0:
```python
import functools

import jax
import jax.numpy as jnp
from jax import lax
from jax.experimental import pallas as pl
from jax.experimental.pallas import tpu as pltpu
from jax.sharding import PartitionSpec as P


LN_EPS = 1e-5
CORES = 2
UNITS = 4
F32 = jnp.float32
BF16 = jnp.bfloat16
MESH_ID = pl.DeviceIdType.MESH
NT = (((1,), (1,)), ((), ()))


def layer_norm(x_rows, ln_weight, ln_bias):
    x_float = x_rows.astype(F32)
    centered = x_float - jnp.mean(x_float, axis=-1, keepdims=True)
    inv_std = lax.rsqrt(jnp.mean(centered * centered, axis=-1, keepdims=True) + LN_EPS)
    x_hat = centered * inv_std
    hidden = (x_hat * ln_weight.astype(F32) + ln_bias.astype(F32)).astype(BF16)
    return hidden, x_hat, inv_std


def layer_norm_back(grad_h, x_hat, inv_std, ln_weight):
    scaled = grad_h * ln_weight.astype(F32)
    return inv_std * (scaled - jnp.mean(scaled, axis=-1, keepdims=True)
                      - x_hat * jnp.mean(scaled * x_hat, axis=-1, keepdims=True))


def masked_gate(logits, allowed, choice):
    expert_ids = jnp.arange(logits.shape[-1])
    prob_all = jax.nn.softmax(jnp.where(allowed, logits, -1e30), axis=-1)
    picked = (choice[:, None] == expert_ids[None, :]).astype(F32)
    return jnp.sum(prob_all * picked, axis=-1), prob_all, picked


def ring_offsets(n_x):
    near = [d for d in (1, n_x - 1) if 0 < d < n_x]
    near = list(dict.fromkeys(near))
    far = [d for d in range(2, n_x - 1)]
    out = [(0, 1)]
    for group in (near, far):
        for core in range(CORES):
            out += [(d, core) for d in group]
    return out


class Place:
    def __init__(self, n_ep, grid):
        self.n_x, self.grid = n_ep // CORES, grid
        self.ep, self.dp = lax.axis_index('ep'), lax.axis_index('dp')
        self.x, self.core = self.ep // CORES, self.ep % CORES
        self.z, self.y = self.dp // grid, self.dp % grid
        self.offsets = ring_offsets(self.n_x)

    def ep_to(self, k):
        dx, dc = self.offsets[k]
        return lax.rem(self.x + dx, self.n_x) * CORES + lax.rem(self.core + dc, CORES)

    def ep_from(self, k):
        dx, dc = self.offsets[k]
        return lax.rem(self.x + (self.n_x - dx), self.n_x) * CORES + lax.rem(self.core + dc, CORES)

    def step(self, axis, k):
        here = self.y if axis == 'y' else self.z
        return lax.rem(here + k + self.grid, self.grid)

    def device(self, axis, k):
        if axis == 'y':
            return (self.z * self.grid + self.step('y', k), self.ep)
        return (self.step('z', k) * self.grid + self.y, self.ep)

    def flip(self, axis, bits):
        if axis == 'y':
            return (self.z * self.grid + (self.y ^ bits), self.ep)
        return ((self.z ^ bits) * self.grid + self.y, self.ep)

    def barrier(self):
        sem = pltpu.get_barrier_semaphore()
        peers = [(self.dp, self.ep_to(k)) for k in range(len(self.offsets))]
        for k in range(1, self.grid):
            peers += [self.device('y', k), self.device('z', k)]
        for peer in peers:
            pl.semaphore_signal(sem, inc=1, device_id=peer, device_id_type=MESH_ID)
        pl.semaphore_wait(sem, len(peers))


def rows_at(start, size, unit):
    return pl.ds(pl.multiple_of(start, unit), size)


class Spread:
    STAGES = ((0,), (1, 2), (3, 4, 5, 6), tuple(range(7, 15)))

    def __init__(self, here, own, held, send, recv):
        self.here, self.own, self.held, self.sems = here, own, held, (send, recv)

    def plan(self, unit, index):
        axes = ('y', 'z') if unit < UNITS // 2 else ('z', 'y')
        one, two = (1, 3) if unit % 2 == 0 else (3, 1)
        line = (0, one, two, one ^ two)
        if index < 1:
            return axes, (axes[0], one), (0, 0)
        if index < 3:
            return axes, (axes[0], two), (line[index - 1], 0)
        if index < 7:
            return axes, (axes[1], one), (line[index - 3], 0)
        return axes, (axes[1], two), (line[(index - 7) % 4], (0, one)[(index - 7) // 4])

    def copy(self, unit, index):
        axes, (axis, flip), offsets = self.plan(unit, index)
        at = dict(zip(axes, offsets))
        owner = (self.here.z ^ at['z']) * self.here.grid + (self.here.y ^ at['y'])
        held = self.held.at[owner, unit]
        source = self.own.at[unit] if self.own is not None and offsets == (0, 0) else held
        return pltpu.make_async_remote_copy(src_ref=source, dst_ref=held, send_sem=self.sems[0].at[unit, index],
                                            recv_sem=self.sems[1].at[unit, index], device_id=self.here.flip(axis, flip),
                                            device_id_type=MESH_ID)

    def each(self, stage, picks=None):
        ids = self.STAGES[stage]
        for index in ids if picks is None else [ids[p] for p in picks]:
            for unit in range(UNITS):
                yield self.copy(unit, index)

    def send(self, stage, picks=None):
        for c in self.each(stage, picks):
            c.start()

    def receive(self, stage):
        for c in self.each(stage):
            c.wait_recv()

    def sent(self, stage):
        for c in self.each(stage):
            c.wait_send()


def spread_kernel(grid, cap, held_in, o_in, dh_in, held, o_out, dh_out, sp_s, sp_r, ba_s, ba_r, loc):
    rows = o_in.shape[0]
    here = Place(rows // cap, grid)
    n_peer = len(here.offsets)
    here.barrier()
    spread = Spread(here, None, held, sp_s, sp_r)
    spread.send(3)
    pairs = ((o_in, o_out), (dh_in, dh_out))

    def block(e):
        return rows_at(e * cap, cap, 16)

    def back(j, k):
        src, dst = pairs[j]
        return pltpu.make_async_remote_copy(src_ref=src.at[block(here.ep_to(k)), :], dst_ref=dst.at[block(here.ep), :],
                                            send_sem=ba_s.at[j, k], recv_sem=ba_r.at[j, k], device_id=(here.dp, here.ep_to(k)),
                                            device_id_type=MESH_ID)

    own = [pltpu.make_async_copy(src.at[block(here.ep), :], dst.at[block(here.ep), :], loc.at[j]) for j, (src, dst) in enumerate(pairs)]
    for j in range(2):
        for k in range(n_peer):
            back(j, k).start()
        own[j].start()
    for j in range(2):
        for k in range(n_peer):
            back(j, k).wait()
        own[j].wait()
    spread.receive(3)
    spread.sent(3)


def spread_call(held, o, dh, cap, grid, collective_id):
    dma = pltpu.SemaphoreType.DMA
    n_peer = o.shape[0] // cap - 1
    hbm = pl.BlockSpec(memory_space=pl.ANY)
    return pl.pallas_call(
        functools.partial(spread_kernel, grid, cap),
        out_shape=tuple(jax.ShapeDtypeStruct(x.shape, x.dtype) for x in (held, o, dh)),
        in_specs=[hbm] * 3, out_specs=(hbm,) * 3, input_output_aliases={0: 0},
        scratch_shapes=[dma((UNITS, 15)), dma((UNITS, 15)), dma((2, n_peer)), dma((2, n_peer)), dma((2,))],
        compiler_params=pltpu.CompilerParams(collective_id=collective_id, has_side_effects=True),
        cost_estimate=pl.CostEstimate(flops=1_000_000_000, bytes_accessed=30_000_000, transcendentals=0),
        name='spread',
    )(held, o, dh)


def expert_kernel(dims, *refs):
    expert, grid, chunk, cap, first = dims
    refs = list(refs)
    take = lambda n: [refs.pop(0) for _ in range(n)]
    if first:
        sel_in, wg_h, wu_h, wd_h = take(6), *take(3)
        o_h, dh_h, sh_h, h_next, q_next, hsl_next, qsl_next = take(7)
    else:
        h_next, q_next, hsl_next, qsl_next, wg_h, wu_h, wd_h, *carry = take(9)
        done_h, = take(1)
        o_h, dh_h, sh_h, *carry_out = take(5)
        all_h, = take(1)
    h_recv, q_recv, wg, wu, wd, a_t, b_t, d_t, u_all, da_all, db_all, h_sl, q_sl, dw, rsb, act, act_b, eye = take(18)
    loc, hs_s, hs_r, qs_s, qs_r, ga_s, ga_r, rs_s, rs_r = take(9)
    if first:
        sel_h, sel_q, sel_h_next, sel_q_next, hidden, pair, h_send, q_send, h_send_next, q_send_next = take(10)
        xh_s, xh_r, xq_s, xq_r, nh_s, nh_r, nq_s, nq_r, ns_h_s, ns_h_r, ns_q_s, ns_q_r, lin = take(13)
        o_v, dh_v = h_send, q_send
    else:
        o_v, dh_v = take(2)
        ba_s, ba_r, ba_l, lin, sp_s, sp_r = take(6)
    rows, d_model = h_recv.shape
    ff = wg.shape[0]
    quarter = d_model // grid
    share = ff // grid
    here = Place(rows // cap, grid)
    n_peer = len(here.offsets)
    ep = here.ep
    remote = functools.partial(pltpu.make_async_remote_copy, device_id_type=MESH_ID)
    wide = chunk // 2

    def spot(axis):
        return here.y if axis == 'y' else here.z

    def block(e):
        return rows_at(e * cap, cap, 16)

    weights = [pltpu.make_async_copy(src.at[expert], dst, loc.at[i]) for i, (src, dst) in enumerate(((wg_h, wg), (wu_h, wu), (wd_h, wd)))]

    def x_copy(src, dst, send, recv, k):
        return remote(src_ref=src.at[block(here.ep_to(k)), :], dst_ref=dst.at[block(ep), :],
                      send_sem=send.at[k], recv_sem=recv.at[k], device_id=(here.dp, here.ep_to(k)))

    def slice_copy(axis, buf, sl, send, recv, src_ep, k):
        return remote(src_ref=buf.at[block(src_ep), rows_at(here.step(axis, k) * quarter, quarter, 128)],
                      dst_ref=sl.at[rows_at(spot(axis) * rows + src_ep * cap, cap, 16), :],
                      send_sem=send.at[k], recv_sem=recv.at[k], device_id=here.device(axis, k))

    def slices(axis, buf, sl, send, recv, k):
        return remote(src_ref=buf.at[:, pl.ds(0, quarter)], dst_ref=sl.at[pl.ds(0, rows), :],
                      send_sem=send.at[k], recv_sem=recv.at[k], device_id=here.device(axis, k))

    half = ff // 2
    gathers = [(u_all, pl.ds(0, half), 'z', 1, 3), (u_all, pl.ds(half, half), 'z', 3, 1),
               (da_all, pl.ds(0, ff), 'y', 1, 3), (db_all, pl.ds(0, ff), 'y', 3, 1)]

    def share_t(g, j):
        ref, part, axis, one, two = gathers[g]
        flip = two if j else one
        owner = spot(axis) ^ (one if j == 2 else 0)
        view = ref.at[part, rows_at(owner * rows, rows, 128)]
        return remote(src_ref=view, dst_ref=view, send_sem=ga_s.at[g, j], recv_sem=ga_r.at[g, j], device_id=here.flip(axis, flip))

    def share_on(units):
        for g in units:
            share_t(g, 0).wait_recv()
            for j in (1, 2):
                share_t(g, j).start()

    def share_done(units):
        for g in units:
            for j in (1, 2):
                share_t(g, j).wait_recv()

    reduces = [(0, pl.ds(0, quarter), 'z', 1, 3), (1, pl.ds(0, quarter), 'z', 3, 1),
               (2, pl.ds(0, quarter // 2), 'y', 1, 3), (2, pl.ds(quarter // 2, quarter // 2), 'y', 3, 1)]

    def part_at(i):
        return rows_at(i * share, share, 8)

    def reduce_copy(r, j):
        t, cols, axis, one, two = reduces[r]
        here_at = spot(axis)
        flip, chunk_at = ((one, here_at ^ one), (one, here_at ^ one ^ two), (two, here_at ^ two))[j]
        return remote(src_ref=dw.at[t, part_at(chunk_at), cols], dst_ref=rsb.at[t, j, :, cols],
                      send_sem=rs_s.at[r, j], recv_sem=rs_r.at[r, j], device_id=here.flip(axis, flip))

    def reduce_start(units):
        for r in units:
            for j in (0, 1):
                reduce_copy(r, j).start()

    def reduce_on(units):
        for r in units:
            t, cols, axis, _, two = reduces[r]
            reduce_copy(r, 0).wait_recv()
            reduce_copy(r, 1).wait_recv()
            on = part_at(spot(axis) ^ two)
            dw[t, on, cols] = dw[t, on, cols] + rsb[t, 1, :, cols]
            reduce_copy(r, 2).start()

    def reduce_end(t):
        units = [r for r in range(len(reduces)) if reduces[r][0] == t]
        axis = reduces[units[0]][2]
        for r in units:
            reduce_copy(r, 2).wait_recv()
        rsb[t, 0] = dw[t, part_at(spot(axis)), :] + rsb[t, 0] + rsb[t, 2]
        unit = quarter // UNITS
        outs = [pltpu.make_async_copy(rsb.at[t, 0, :, pl.ds(i * unit, unit)], sh_h.at[i, t], loc.at[5 + t * UNITS + i]) for i in range(UNITS)]
        for c in outs:
            c.start()
        return outs

    def own_slice(axis, buf, sl):
        sl[rows_at(spot(axis) * rows, rows, 16), :] = buf[:, rows_at(spot(axis) * quarter, quarter, 128)]

    strip = ff // 7
    u_cols = rows_at(here.z * rows, rows, 128)
    g_cols = rows_at(here.y * rows, rows, 128)

    def forward_pass():
        a_t[...] = jnp.zeros_like(a_t)
        b_t[...] = jnp.zeros_like(b_t)

        @pl.loop(0, d_model // chunk)
        def _(i):
            cols = rows_at(i * chunk, chunk, 128)
            a_t[...] += lax.dot_general(wg[:, cols], h_recv[:, cols], NT, preferred_element_type=F32)
            b_t[...] += lax.dot_general(wu[:, cols], h_recv[:, cols], NT, preferred_element_type=F32)

        @pl.loop(0, 7)
        def _(i):
            r = rows_at(i * strip, strip, 16)
            a = a_t[r, :]
            u_all[r, u_cols] = (a * jax.nn.sigmoid(a) * b_t[r, :]).astype(BF16)

    def backward_pass():
        d_t[...] = jnp.zeros_like(d_t)

        @pl.loop(0, d_model // chunk)
        def _(i):
            cols = rows_at(i * chunk, chunk, 128)
            d_t[...] += lax.dot_general(wd[:, cols], q_recv[:, cols], NT, preferred_element_type=F32)

        @pl.loop(0, 7)
        def _(i):
            r = rows_at(i * strip, strip, 16)
            a, b, du = a_t[r, :], b_t[r, :], d_t[r, :]
            sig = jax.nn.sigmoid(a)
            silu = a * sig
            da_all[r, g_cols] = (du * b * sig * (1.0 + a * (1.0 - sig))).astype(BF16)
            db_all[r, g_cols] = (du * silu).astype(BF16)

    def untranspose(out, ref, cols):
        out[...] = lax.dot_general(eye[...], ref[:, cols], NT, preferred_element_type=F32).astype(BF16)

    def o_pass():
        @pl.loop(0, d_model // wide)
        def _(i):
            cols = rows_at(i * wide, wide, 128)
            o_v[:, cols] = jnp.dot(act[...], wd[:, cols], preferred_element_type=F32).astype(BF16)

    def dh_pass():
        @pl.loop(0, d_model // wide)
        def _(i):
            cols = rows_at(i * wide, wide, 128)
            dh_v[:, cols] = (jnp.dot(act[...], wg[:, cols], preferred_element_type=F32)
                             + jnp.dot(act_b[...], wu[:, cols], preferred_element_type=F32)).astype(BF16)

    def weight_grad(t, left, right):
        @pl.loop(0, quarter // wide)
        def _(i):
            cols = rows_at(i * wide, wide, 128)
            dw[t, :, cols] = jnp.dot(left[...], right[:, cols], preferred_element_type=F32)

    def make_eye():
        eye[...] = (lax.broadcasted_iota(jnp.int32, (rows, rows), 0)
                    == lax.broadcasted_iota(jnp.int32, (rows, rows), 1)).astype(F32).astype(BF16)

    if first:
        inputs = [pltpu.make_async_copy(src, dst, lin.at[i])
                  for i, (src, dst) in enumerate(zip(sel_in, (sel_h, hidden, sel_q, pair, sel_h_next, sel_q_next)))]
        for c in inputs:
            c.start()
        here.barrier()
        for c in inputs:
            c.wait()

        def gather(sel, source, out, e):
            @pl.loop(0, d_model // chunk)
            def _(i):
                cols = rows_at(i * chunk, chunk, 128)
                out[block(e), cols] = jnp.dot(sel[block(e), :], source[:, cols], preferred_element_type=F32).astype(BF16)

        now = ((sel_h, hidden, h_send, h_recv, xh_s, xh_r), (sel_q, pair, q_send, q_recv, xq_s, xq_r))
        later = ((sel_h_next, hidden, h_send_next, h_next, nh_s, nh_r), (sel_q_next, pair, q_send_next, q_next, nq_s, nq_r))

        def copy_of(what, k):
            _, _, out, recv_buf, send, recv = what
            return x_copy(out, recv_buf, send, recv, k)

        pending = []

        def dispatch(what, k):
            gather(what[0], what[1], what[2], here.ep_to(k))
            pending.append(copy_of(what, k))
            if len(pending) > 1:
                pending.pop(0).start()

        for k in range(n_peer):
            for what in now:
                dispatch(what, k)
        for what in now:
            gather(what[0], what[1], what[3], ep)
        while pending:
            pending.pop(0).start()
        for c in weights:
            c.start()
        make_eye()

        spread = (('y', h_recv, h_sl, hs_s, hs_r), ('z', q_recv, q_sl, qs_s, qs_r))
        spread_next = (('y', h_next, hsl_next, ns_h_s, ns_h_r), ('z', q_next, qsl_next, ns_q_s, ns_q_r))

        def forward_own(spread, bufs):
            for (axis, _, sl, send, recv), buf in zip(spread, bufs):
                for k in range(1, grid):
                    slice_copy(axis, buf, sl, send, recv, ep, k).start()

        def forward(group, spread, p):
            for what, (axis, buf, sl, send, recv) in zip(group, spread):
                copy_of(what, p).wait_recv()
                for k in range(1, grid):
                    slice_copy(axis, buf, sl, send, recv, here.ep_from(p), k).start()

        forward_own(spread, (h_recv, q_recv))
        for what in later:
            gather(what[0], what[1], what[2], ep)
        own_next = [pltpu.make_async_copy(what[2].at[block(ep), :], what[3].at[block(ep), :], lin.at[6 + i]) for i, what in enumerate(later)]
        for p in range(n_peer):
            forward(now, spread, p)
            for what in later:
                dispatch(what, p)
        while pending:
            pending.pop(0).start()
        for c in own_next:
            c.start()
        own_slice('y', h_recv, h_sl)
        own_slice('z', q_recv, q_sl)
        for c in weights:
            c.wait()
        for k in range(n_peer):
            for what in now:
                copy_of(what, k).wait_send()
    else:
        loads = [pltpu.make_async_copy(h_next, h_recv, lin.at[0]), weights[0], weights[1],
                 pltpu.make_async_copy(q_next, q_recv, lin.at[1]), weights[2]]
        for i, (axis, src, dst) in enumerate((('z', qsl_next, q_sl), ('y', hsl_next, h_sl))):
            for k in range(1, grid):
                part = rows_at(here.step(axis, k) * rows, rows, 16)
                loads.append(pltpu.make_async_copy(src.at[part, :], dst.at[part, :], lin.at[2 + i * grid + k]))
        for c in loads:
            c.start()
        here.barrier()
        back = list(zip(carry, carry_out))
        spread_unit = Spread(here, done_h, all_h, sp_s, sp_r)
        own_unit = pltpu.make_async_copy(done_h, all_h.at[here.dp], lin.at[1])
        spread_unit.send(0)

        def back_copy(j, k):
            src, dst = back[j]
            return remote(src_ref=src.at[block(here.ep_to(k)), :], dst_ref=dst.at[block(ep), :],
                          send_sem=ba_s.at[j, k], recv_sem=ba_r.at[j, k], device_id=(here.dp, here.ep_to(k)))

        def back_own(j):
            src, dst = back[j]
            return pltpu.make_async_copy(src.at[block(ep), :], dst.at[block(ep), :], ba_l.at[j])

        def send_back(j):
            for k in range(n_peer):
                back_copy(j, k).start()
            back_own(j).start()

        for j in range(len(carry)):
            send_back(j)
        make_eye()
        for c in loads:
            c.wait()
        own_unit.start()
        own_slice('y', h_recv, h_sl)
        own_slice('z', q_recv, q_sl)

    forward_pass()
    share_t(0, 0).start()
    share_t(1, 0).start()
    if not first:
        spread_unit.receive(0)
        spread_unit.send(1)
    backward_pass()
    share_t(2, 0).start()
    share_t(3, 0).start()
    untranspose(act, u_all, u_cols)
    share_on((0, 1))
    o_pass()
    o_out = pltpu.make_async_copy(o_v, o_h, loc.at[3])
    o_out.start()
    untranspose(act, da_all, g_cols)
    untranspose(act_b, db_all, g_cols)
    share_on((2, 3))
    dh_pass()
    dh_out = pltpu.make_async_copy(dh_v, dh_h, loc.at[4])
    dh_out.start()
    if first:
        forward_own(spread_next, (h_send_next, q_send_next))
        forward(later, spread_next, 0)
        for k in range(1, grid):
            slices('z', q_recv, q_sl, qs_s, qs_r, k).wait_recv()
    else:
        spread_unit.receive(1)
        spread_unit.send(2, (0,))
    share_done((0, 1))
    weight_grad(2, u_all, q_sl)
    reduce_start((2, 3))
    if first:
        for k in range(1, grid):
            slices('y', h_recv, h_sl, hs_s, hs_r, k).wait_recv()
    share_done((2,))
    weight_grad(0, da_all, h_sl)
    reduce_start((0,))
    share_done((3,))
    weight_grad(1, db_all, h_sl)
    reduce_start((1,))
    if first:
        for p in range(1, (n_peer + 1) // 2):
            forward(later, spread_next, p)
    else:
        spread_unit.send(2, (1,))
    reduce_on((2, 3))
    if first:
        for p in range((n_peer + 1) // 2, n_peer - 2):
            forward(later, spread_next, p)
    reduce_on((0, 1))
    if not first:
        spread_unit.send(2, (2, 3))
    if first:
        for p in range(max((n_peer + 1) // 2, n_peer - 2), n_peer):
            forward(later, spread_next, p)
    ends = reduce_end(2) + reduce_end(0) + reduce_end(1)

    for j in range(3):
        for g in range(4):
            share_t(g, j).wait_send()
        for r in range(4):
            reduce_copy(r, j).wait_send()
    if first:
        for k in range(1, grid):
            for axis, buf, sl, send, recv in spread:
                slices(axis, buf, sl, send, recv, k).wait_send()
            for axis, buf, sl, send, recv in spread_next:
                slices(axis, buf, sl, send, recv, k).wait()
        for k in range(n_peer):
            for what in later:
                copy_of(what, k).wait_send()
        for c in own_next:
            c.wait()
    else:
        for j in range(len(back)):
            for k in range(n_peer):
                back_copy(j, k).wait()
            back_own(j).wait()
        spread_unit.receive(2)
        for stage in range(3):
            spread_unit.sent(stage)
        own_unit.wait()
    for c in ends + [o_out, dh_out]:
        c.wait()


def expert_call(inputs, w_gate, w_up, w_down, expert, cap, grid):
    first = expert == 0
    d_model = w_gate.shape[2]
    ff = w_gate.shape[1]
    rows = inputs[0].shape[0]
    quarter, share = d_model // grid, ff // grid
    n_peer = rows // cap - 1
    chunk = min(1024, d_model)
    vmem, dma = pltpu.VMEM, pltpu.SemaphoreType.DMA
    hbm = pl.BlockSpec(memory_space=pl.ANY)
    row_block, slice_block = (rows, d_model), (grid * rows, quarter)
    scratch = [
        vmem(row_block, BF16), vmem(row_block, BF16),
        vmem((ff, d_model), BF16), vmem((ff, d_model), BF16), vmem((ff, d_model), BF16),
        vmem((ff, rows), F32), vmem((ff, rows), F32), vmem((ff, rows), F32),
        vmem((ff, grid * rows), BF16), vmem((ff, grid * rows), BF16), vmem((ff, grid * rows), BF16),
        vmem(slice_block, BF16), vmem(slice_block, BF16),
        vmem((3, ff, quarter), F32), vmem((3, 3, share, quarter), F32),
        vmem((rows, ff), BF16), vmem((rows, ff), BF16), vmem((rows, rows), BF16), dma((5 + 3 * UNITS,)),
    ] + [dma((grid,))] * 4 + [dma((4, 3))] * 4
    out = lambda shape, dtype=BF16: jax.ShapeDtypeStruct(shape, dtype)
    share_block = (UNITS, 3, share, quarter // UNITS)
    outs = [out(row_block), out(row_block), out(share_block, F32)]
    if first:
        sel_h, hidden, sel_q, pair, sel_h_next, sel_q_next = inputs
        scratch += [vmem(x.shape, BF16) for x in (sel_h, sel_q, sel_h_next, sel_q_next, hidden, pair)]
        scratch += [vmem(row_block, BF16)] * 4 + [dma((n_peer,))] * 8 + [dma((grid,))] * 4 + [dma((8,))]
        operands = (*inputs, w_gate, w_up, w_down)
        outs += [out(row_block), out(row_block), out(slice_block), out(slice_block)]
    else:
        h_next, q_next, hsl_next, qsl_next, *carry, done = inputs
        scratch += [vmem(row_block, BF16)] * 2 + [dma((2, n_peer)), dma((2, n_peer)), dma((2,)), dma((2 + 2 * grid,))]
        scratch += [dma((UNITS, 15)), dma((UNITS, 15))]
        operands = (h_next, q_next, hsl_next, qsl_next, w_gate, w_up, w_down, *carry, done)
        outs += [out(row_block), out(row_block), out((grid * grid,) + share_block, F32)]
    return pl.pallas_call(
        functools.partial(expert_kernel, (expert, grid, chunk, cap, first)),
        out_shape=tuple(outs), in_specs=[hbm] * len(operands), out_specs=(hbm,) * len(outs), scratch_shapes=scratch,
        compiler_params=pltpu.CompilerParams(collective_id=expert, has_side_effects=True, vmem_limit_bytes=63 * 2 ** 20),
        cost_estimate=pl.CostEstimate(flops=2 * rows * d_model * ff * 9, bytes_accessed=30_000_000, transcendentals=0),
    )(*operands)


def small_sum_kernel(grid, val, out, first, second, third, c_one, c_two, c_three, s_one, r_one, s_two, r_two, s_three, r_three, s_four, r_four):
    n_ep, _, width = first.shape
    here = Place(n_ep, grid)
    n_peer = len(here.offsets)
    ep = here.ep
    remote = functools.partial(pltpu.make_async_remote_copy, device_id_type=MESH_ID)
    here.barrier()

    def cols(e):
        return rows_at(e * width, width, 128)

    def scatter(k):
        to = here.ep_to(k)
        return remote(src_ref=val.at[:, cols(to)], dst_ref=first.at[ep], send_sem=s_one.at[k], recv_sem=r_one.at[k],
                      device_id=(here.dp, to))

    def along(axis, src, dst, send, recv, k):
        mine = here.y if axis == 'y' else here.z
        return remote(src_ref=src, dst_ref=dst.at[mine], send_sem=send.at[k], recv_sem=recv.at[k], device_id=here.device(axis, k))

    def gather(k):
        return remote(src_ref=c_three, dst_ref=out.at[:, cols(ep)], send_sem=s_four.at[k], recv_sem=r_four.at[k],
                      device_id=(here.dp, here.ep_to(k)))

    def add_up(ref, n):
        total = ref[0]
        for i in range(1, n):
            total = total + ref[i]
        return total

    for k in range(n_peer):
        scatter(k).start()
    first[ep] = val[:, cols(ep)]
    for k in range(n_peer):
        scatter(k).wait_recv()
    c_one[...] = add_up(first, n_ep)
    second[here.y] = c_one[...]
    for k in range(1, grid):
        along('y', c_one, second, s_two, r_two, k).start()
    for k in range(1, grid):
        along('y', c_one, second, s_two, r_two, k).wait_recv()
    c_two[...] = add_up(second, grid)
    third[here.z] = c_two[...]
    for k in range(1, grid):
        along('z', c_two, third, s_three, r_three, k).start()
    for k in range(1, grid):
        along('z', c_two, third, s_three, r_three, k).wait_recv()
    c_three[...] = add_up(third, grid)
    for k in range(n_peer):
        gather(k).start()
    out[:, cols(ep)] = c_three[...]
    for k in range(n_peer):
        gather(k).wait_recv()
    for k in range(n_peer):
        scatter(k).wait_send()
        gather(k).wait_send()
    for k in range(1, grid):
        along('y', c_one, second, s_two, r_two, k).wait_send()
        along('z', c_two, third, s_three, r_three, k).wait_send()


def small_sum(val, n_ep, grid, collective_id):
    rows, d_model = val.shape
    width = d_model // n_ep
    vmem, dma = pltpu.VMEM, pltpu.SemaphoreType.DMA
    return pl.pallas_call(
        functools.partial(small_sum_kernel, grid),
        out_shape=jax.ShapeDtypeStruct(val.shape, F32),
        in_specs=[pl.BlockSpec(memory_space=pltpu.VMEM)], out_specs=pl.BlockSpec(memory_space=pltpu.VMEM),
        scratch_shapes=[vmem((n_ep, rows, width), F32), vmem((grid, rows, width), F32), vmem((grid, rows, width), F32),
                        vmem((rows, width), F32), vmem((rows, width), F32), vmem((rows, width), F32),
                        dma((n_ep - 1,)), dma((n_ep - 1,)), dma((grid,)), dma((grid,)), dma((grid,)), dma((grid,)),
                        dma((n_ep - 1,)), dma((n_ep - 1,))],
        compiler_params=pltpu.CompilerParams(collective_id=collective_id, has_side_effects=True),
        name='small_sum',
    )(val)


def assemble_kernel(gate, up, down, *refs):
    outs = refs[-3:]
    grid, unit = gate.shape[1], gate.shape[-1]
    for c in range(grid):
        for i in range(UNITS):
            at = (c * UNITS + i) * unit
            outs[0][0, :, at:at + unit] = gate[0, c, i, 0]
            outs[1][0, :, at:at + unit] = up[0, c, i, 0]
            outs[2][0, :, at:at + unit] = down[c, 0, i, 0]


def assemble(gathered, expert, n_expert, into):
    grid, _, _, _, share, unit = gathered.shape
    cut = 2
    part = share // cut
    row_first = pl.BlockSpec((1, grid, UNITS, 1, part, unit), lambda r, h: (r, 0, 0, 0, h, 0))
    up_first = pl.BlockSpec((1, grid, UNITS, 1, part, unit), lambda r, h: (r, 0, 0, 1, h, 0))
    col_first = pl.BlockSpec((grid, 1, UNITS, 1, part, unit), lambda r, h: (0, r, 0, 2, h, 0))
    out_spec = pl.BlockSpec((1, part, grid * UNITS * unit), lambda r, h: (expert, r * cut + h, 0))
    whole = jax.ShapeDtypeStruct((n_expert, grid * share, grid * UNITS * unit), F32)
    return pl.pallas_call(
        assemble_kernel, grid=(grid, cut), out_shape=(whole,) * 3,
        in_specs=[row_first, up_first, col_first] + [pl.BlockSpec(memory_space=pl.ANY)] * len(into),
        out_specs=(out_spec,) * 3, input_output_aliases={3 + i: i for i in range(len(into))},
        compiler_params=pltpu.CompilerParams(vmem_limit_bytes=40 * 2 ** 20),
        cost_estimate=pl.CostEstimate(flops=1_000_000, bytes_accessed=44_000_000, transcendentals=0),
    )(gathered, gathered, gathered, *into)


def solution(mesh):
    n_ep = mesh.shape['ep']
    grid = round(mesh.shape['dp'] ** 0.5)
    tok_spec = P(('dp', 'ep'), None)
    row_spec = P(('dp', 'ep'))
    exp_spec = P('ep', None, None)

    def local_step(tok_x, tok_dy, exp_first, exp_second, eligible, slot_first, slot_second,
                   ln_weight, ln_bias, router, w_gate, w_up, w_down):
        n_local, d_model = tok_x.shape
        n_exp = eligible.shape[1]
        local_exp = w_gate.shape[0]
        slot_cap = 3 * n_local // n_exp
        hidden, x_hat, inv_std = layer_norm(tok_x, ln_weight, ln_bias)
        logits = jnp.dot(hidden, router, preferred_element_type=F32)
        expert_ids = jnp.arange(n_exp)
        allowed = eligible > 0
        gate_one, prob_one, pick_one = masked_gate(logits, allowed, exp_first)
        gate_two, prob_two, pick_two = masked_gate(logits, allowed & (expert_ids[None, :] != exp_first[:, None]), exp_second)
        per = n_ep * slot_cap
        row_ids = jnp.arange(n_exp * slot_cap)

        def place(expert, slot):
            pos = (expert % local_exp) * per + (expert // local_exp) * slot_cap + slot
            return jnp.where(slot >= 0, pos, -1)

        pos_one = place(exp_first, slot_first)
        pos_two = place(exp_second, slot_second)
        sel_one = (pos_one[:, None] == row_ids[None, :]).astype(BF16)
        sel_two = (pos_two[:, None] == row_ids[None, :]).astype(BF16)
        sel_both = sel_one + sel_two
        dy_float = tok_dy.astype(F32)
        grad_one = (gate_one[:, None] * dy_float).astype(BF16)
        grad_two = (gate_two[:, None] * dy_float).astype(BF16)
        pair = jnp.concatenate([grad_one, grad_two], axis=0)
        pos_pair = jnp.concatenate([pos_one, pos_two])
        wg_t, wu_t = jnp.swapaxes(w_gate, 1, 2), jnp.swapaxes(w_up, 1, 2)
        cuts = [slice(e * per, (e + 1) * per) for e in range(local_exp)]
        sels = []
        for e in range(local_exp):
            ids = row_ids[cuts[e]][:, None]
            sels.append(jnp.logical_or(ids == pos_one[None, :], ids == pos_two[None, :]).astype(BF16))
            sels.append((ids == pos_pair[None, :]).astype(BF16))
        o, dh, share, *landed = expert_call((sels[0], hidden, sels[1], pair, sels[2], sels[3]), wg_t, wu_t, w_down, 0, slot_cap, grid)
        o_next, dh_next, share, o, dh, held = expert_call((*landed, o, dh, share), wg_t, wu_t, w_down, 1, slot_cap, grid)
        gathered_next = lax.all_gather(share, 'dp')
        held, o_next, dh_next = spread_call(held, o_next, dh_next, slot_cap, grid, local_exp + 1)
        gathered = [x.reshape((grid, grid) + share.shape) for x in (held, gathered_next)]
        outs, grads = [o, o_next], [dh, dh_next]
        sel_cat = [sel_one, sel_two]
        out_one, out_two = [sum(jnp.dot(s[:, c], o, preferred_element_type=F32) for c, o in zip(cuts, outs)) for s in sel_cat]
        y_mix = gate_one[:, None] * out_one + gate_two[:, None] * out_two
        out_tok = (tok_x.astype(F32) + y_mix).astype(BF16)
        grad_exp = sum(jnp.dot(sel_both[:, c], g, preferred_element_type=F32) for c, g in zip(cuts, grads))
        dgate_one = jnp.sum(dy_float * out_one, axis=-1)
        dgate_two = jnp.sum(dy_float * out_two, axis=-1)
        d_logits = ((dgate_one * gate_one)[:, None] * (pick_one - prob_one)
                    + (dgate_two * gate_two)[:, None] * (pick_two - prob_two)).astype(BF16)
        d_router = jnp.einsum('te,td->ed', d_logits, hidden, preferred_element_type=F32)
        grad_h = jnp.einsum('te,de->td', d_logits, router, preferred_element_type=F32) + grad_exp
        d_ln_weight = jnp.sum(grad_h * x_hat, axis=0)
        d_ln_bias = jnp.sum(grad_h, axis=0)
        dx_tok = (dy_float + layer_norm_back(grad_h, x_hat, inv_std, ln_weight)).astype(BF16)
        small = jnp.concatenate([d_router, d_ln_weight[None], d_ln_bias[None], jnp.zeros((6, d_model), F32)], axis=0)
        small = small_sum(small, n_ep, grid, local_exp)
        d_router, d_ln_weight, d_ln_bias = small[:n_exp].T, small[n_exp], small[n_exp + 1]

        weights = ()
        for e in range(local_exp):
            weights = assemble(gathered[e], e, local_exp, weights)
        dw_gate, dw_up, dw_down = jnp.swapaxes(weights[0], 1, 2), jnp.swapaxes(weights[1], 1, 2), weights[2]
        return out_tok, dx_tok, dw_gate, dw_up, dw_down, d_router, d_ln_weight, d_ln_bias

    return jax.shard_map(
        local_step, mesh=mesh,
        in_specs=(tok_spec, tok_spec, row_spec, row_spec, tok_spec, row_spec, row_spec,
                  P(), P(), P(), exp_spec, exp_spec, exp_spec),
        out_specs=(tok_spec, tok_spec, exp_spec, exp_spec, exp_spec, P(), P(), P()),
        check_vma=False)
```

profile of v0, /device:TPU:1, one launch (start us, length us, event | category | flops | bytes accessed | tf_op | source)
XLA Modules:
  0.0 515.2 jit_solution(7212106624135724587)
XLA Ops:
  7.3 2.1 convert_reduce_fusion
  9.4 2.3 fusion.13
  11.9 0.9 or_convert_fusion
  12.8 1.1 compare_convert_fusion
  13.9 1.0 fusion.8.refs_1_
  14.9 1.3 copy-done.7
  16.2 0.7 fusion.35
  17.0 1.2 fusion.15
  18.2 2.5 pad_maximum_fusion.refs_3_
  20.8 177.8 %shard_map.188 = (bf16[384,4096]{1,0:T(8,128)(2,1)}, bf16[384,4096]{1,0:T(8,128)(2,1)}, f32[4,3,112,256]{3,2,1,0:T(8,128)}, bf16[384,4096]{1,0:T(8,128)(2,1)}, b...) custom-call(bf16[384,256]{1,0:T(8,128)(2,1)} %get-tuple-element.72.refs_0_, ...), custom_call_target="tpu_custom_call" | custom-call | flops 12683575296 | bytes 30000000 | tf_op jit(solution)/shard_map/pallas_call | solution.py:602
  198.6 112.0 %shard_map.189 = (bf16[384,4096]{1,0:T(8,128)(2,1)}, bf16[384,4096]{1,0:T(8,128)(2,1)}, f32[4,3,112,256]{3,2,1,0:T(8,128)}, bf16[384,4096]{1,0:T(8,128)(2,1)}, b...) custom-call(bf16[384,4096]{1,0:T(8,128)(2,1)} %get-tuple-element.30.refs_0_, ...), custom_call_target="tpu_custom_call" | custom-call | flops 12683575296 | bytes 30000000 | tf_op jit(solution)/shard_map/pallas_call | solution.py:602
  310.6 105.6 %spread.1 = (f32[16,4,3,112,256]{4,3,2,1,0:T(8,128)}, bf16[384,4096]{1,0:T(8,128)(2,1)}, bf16[384,4096]{1,0:T(8,128)(2,1)}) custom-call(f32[16,4,3,112,256]{4,3,2,1,0:T(8,128)} %get-tuple-element.38.held_in, bf16[384,4096]{1,0:T(8,128)(2,1)} %get-tuple-element.39.o_in, bf16[384,4096]{1,0:T(8,128)(2,1)} %get-tuple-element.40.dh_in), custom_call_target="tpu_custom_call", output_to_operand_aliasing={{0}: (0, {})} | custom-call | flops 1000000000 | bytes 30000000 | tf_op jit(solution)/shard_map/spread/pallas_call | solution.py:179
  416.6 1.3 fusion.21
  417.8 1.3 fusion.24
  419.1 0.7 copy-done.11
  419.8 1.4 convolution_add_fusion.1
  421.4 0.6 copy-done.5
  422.1 4.1 fusion.17
  426.3 0.2 convert_add_fusion.2
  426.5 0.4 fusion.43
  426.9 0.7 fusion.44
  427.6 0.5 copy-done.12
  428.1 1.2 fusion.27
  429.3 0.3 copy-done.13
  429.6 4.6 fusion.12
  434.2 0.8 maximum_maximum_fusion.val
  435.0 34.3 %small_sum.1 = f32[24,4096]{1,0:T(8,128)} custom-call(f32[24,4096]{1,0:T(8,128)} %maximum_maximum_fusion.val), custom_call_target="tpu_custom_call" | custom-call | tf_op jit(solution)/shard_map/small_sum/pallas_call | solution.py:675
  469.4 17.8 %shard_map.190 = (f32[2,448,4096]{2,1,0:T(8,128)}, f32[2,448,4096]{2,1,0:T(8,128)}, f32[2,448,4096]{2,1,0:T(8,128)}) custom-call(f32[4,4,4,3,112,256]{5,4,3,2,1,0:T(8,128)} %bitcast.22, f32[4,4,4,3,112,256]{5,4,3,2,1,0:T(8,128)} %bitcast.23, f32[4,4,4,3,112,256]{5,4,3,2,1,0:T(8,128)} %bitcast.24), custom_call_target="tpu_custom_call" | custom-call | flops 1000000 | bytes 44000000 | tf_op jit(solution)/shard_map/pallas_call | solution.py:708
  487.2 0.6 fusion.45
  487.8 0.7 slice_bitcast_fusion
  488.5 3.4 fusion.19
  491.9 16.5 %shard_map.191 = (f32[2,448,4096]{2,1,0:T(8,128)}, f32[2,448,4096]{2,1,0:T(8,128)}, f32[2,448,4096]{2,1,0:T(8,128)}) custom-call(f32[4,4,4,3,112,256]{5,4,3,2,1,0:T(8,128)} %bitcast.25, f32[4,4,4,3,112,256]{5,4,3,2,1,0:T(8,128)} %bitcast.26, f32[4,4,4,3,112,256]{5,4,3,2,1,0:T(8,128)} %bitcast.27, ...), custom_call_target="tpu_custom_call", output_to_operand_aliasing={{0}: (3, {}), {1}: (4, {}), {2}: (5, {})} | custom-call | flops 1000000 | bytes 44000000 | tf_op jit(solution)/shard_map/pallas_call | solution.py:708
  (63 shorter events, 0.9 us)
Async XLA Ops:
  7.2 9.1 %copy-start = (bf16[4096,16]{0,1:T(8,128)(2,1)S(1)}, bf16[4096,16]{0,1:T(8,128)(2,1)}, u32[]{:S(2)}) copy-start(bf16[4096,16]{0,1:T(8,128)(2,1)} %param.22) | copy-start | bytes 393220
  7.2 6.7 %copy-start.2 = (bf16[256,4096]{1,0:T(8,128)(2,1)S(1)}, bf16[256,4096]{1,0:T(8,128)(2,1)}, u32[]{:S(2)}) copy-start(bf16[256,4096]{1,0:T(8,128)(2,1)} %param.13) | copy-start | bytes 6291460
  7.2 4.6 copy-start.18
  7.2 4.6 copy-start.19
  7.2 4.6 copy-start.15
  7.2 4.6 copy-start.17
  7.2 4.6 copy-start.20
  7.2 4.6 copy-start.21
  7.3 484.6 %all-gather.3.cloned.1.call-start = ((), (), s32[]{:S(2)}) async-start(), calls=%async_computation | async-start | bytes 23396352 | tf_op jit(solution)/shard_map/all_gather | solution.py:762
  9.4 6.8 %copy-start.16 = (s32[256,16]{0,1:T(8,128)S(1)}, s32[256,16]{0,1:T(8,128)}, u32[]{:S(2)}) copy-start(s32[256,16]{0,1:T(8,128)} %param.17) | copy-start | bytes 49156
  11.7 5.3 %copy-start.4 = (bf16[256,4096]{1,0:T(8,128)(2,1)S(1)}, bf16[256,4096]{1,0:T(8,128)(2,1)}, u32[]{:S(2)}) copy-start(bf16[256,4096]{1,0:T(8,128)(2,1)} %param.14) | copy-start | bytes 6291460
  14.9 1.3 copy-start.7
  310.6 106.0 %copy-start.10 = (bf16[384,4096]{1,0:T(8,128)(2,1)S(1)}, bf16[384,4096]{1,0:T(8,128)(2,1)}, u32[]{:S(2)}) copy-start(bf16[384,4096]{1,0:T(8,128)(2,1)} %get-tuple-element.37) | copy-start | bytes 9437188
  417.8 2.0 copy-start.11
  419.8 1.6 copy-start.3
  419.8 2.2 copy-start.5
  422.1 4.4 copy-start.8
  426.2 1.9 copy-start.12
  427.6 2.0 copy-start.13
  469.3 17.8 %copy-start.14 = (f32[24,4096]{1,0:T(8,128)S(1)}, f32[24,4096]{1,0:T(8,128)}, u32[]{:S(2)}) copy-start(f32[24,4096]{1,0:T(8,128)} %small_sum.1) | copy-start | bytes 1179652
  469.4 19.2 %copy-start.6 = (bf16[256,4096]{1,0:T(8,128)(2,1)S(1)}, bf16[256,4096]{1,0:T(8,128)(2,1)}, u32[]{:S(2)}) copy-start(bf16[256,4096]{1,0:T(8,128)(2,1)} %param.14) | copy-start | bytes 6291460
  469.4 19.2 %copy-start.9 = (f32[256,4096]{1,0:T(8,128)S(1)}, f32[256,4096]{1,0:T(8,128)}, u32[]{:S(2)}) copy-start(f32[256,4096]{1,0:T(8,128)} %get-tuple-element.74) | copy-start | bytes 12582916
  491.9 16.5 %copy-start.1 = (bf16[4096,16]{0,1:T(8,128)(2,1)S(1)}, bf16[4096,16]{0,1:T(8,128)(2,1)}, u32[]{:S(2)}) copy-start(bf16[4096,16]{0,1:T(8,128)(2,1)} %param.22) | copy-start | bytes 393220
Sparse Core Ops, SparseCore 0:
  310.7 180.9 all-gather.2
where the time goes:
time: 516 us; the launch traced here: 515 us
  Pallas kernels  464 us (90%)
  other arithmetic  16 us (3%)
  matrix products  15.7 us (3%)
  between operations  14.5 us (3%)
    pallas_call x2, Pallas kernels, expert_call(): pl.pallas_call(functools.partial(expert_kernel, (expert, grid, chunk, cap...  290 us
    pallas_call x1, Pallas kernels, spread_call(): pl.pallas_call(functools.partial(spread_kernel, grid, cap), out_shape=tup...  106 us
    pallas_call x1, Pallas kernels, small_sum(): pl.pallas_call(functools.partial(small_sum_kernel, grid), out_shape=jax.S...  34.3 us
    pallas_call x2, Pallas kernels, assemble(): pl.pallas_call(assemble_kernel, grid=(grid, cut), out_shape=(whole,) * 3,...  34.3 us
  transfers between devices with their start and end apart: 1, of which 0 were waited for; matrix products, arithmetic and copies ran while one was open for 4% of the time, Pallas kernels for 31%

commit v1 on v0

--- a/solution.py
+++ b/solution.py
@@ -23,13 +23,7 @@
     inv_std = lax.rsqrt(jnp.mean(centered * centered, axis=-1, keepdims=True) + LN_EPS)
     x_hat = centered * inv_std
     hidden = (x_hat * ln_weight.astype(F32) + ln_bias.astype(F32)).astype(BF16)
-    return hidden, x_hat, inv_std
-
-
-def layer_norm_back(grad_h, x_hat, inv_std, ln_weight):
-    scaled = grad_h * ln_weight.astype(F32)
-    return inv_std * (scaled - jnp.mean(scaled, axis=-1, keepdims=True)
-                      - x_hat * jnp.mean(scaled * x_hat, axis=-1, keepdims=True))
+    return hidden, jnp.mean(x_float, axis=-1, keepdims=True), inv_std
 
 
 def masked_gate(logits, allowed, choice):
@@ -141,50 +135,180 @@
             c.wait_send()
 
 
-def spread_kernel(grid, cap, held_in, o_in, dh_in, held, o_out, dh_out, sp_s, sp_r, ba_s, ba_r, loc):
-    rows = o_in.shape[0]
-    here = Place(rows // cap, grid)
+def tail_kernel(grid, cap, *refs):
+    refs = list(refs)
+    take = lambda n: [refs.pop(0) for _ in range(n)]
+    _, o_next_h, dh_next_h, x_h, dy_h, hid_h, o_h, dh_h, stats, err_one, err_two, places, lnw, router = take(14)
+    held, out, dx, small = take(4)
+    x_v, dy_v, hid_v, o_v, dh_v, sel_one, sel_two, grad_h, val = take(9)
+    first, second, third, c_one, c_two, c_three = take(6)
+    loc, sp_s, sp_r, ba_s, ba_r, s_one, r_one, s_two, r_two, s_three, r_three, s_four, r_four = take(13)
+    n_tok, d_model = x_v.shape
+    rows = o_next_h.shape[0]
+    n_ep, _, width = first.shape
+    wide = min(512, d_model)
+    here = Place(n_ep, grid)
     n_peer = len(here.offsets)
+    ep = here.ep
+    remote = functools.partial(pltpu.make_async_remote_copy, device_id_type=MESH_ID)
     here.barrier()
     spread = Spread(here, None, held, sp_s, sp_r)
     spread.send(3)
-    pairs = ((o_in, o_out), (dh_in, dh_out))
-
-    def block(e):
-        return rows_at(e * cap, cap, 16)
+
+    def block(e, base=0):
+        return rows_at(base + e * cap, cap, 16)
+
+    pairs = ((o_next_h, o_v), (dh_next_h, dh_v))
 
     def back(j, k):
         src, dst = pairs[j]
-        return pltpu.make_async_remote_copy(src_ref=src.at[block(here.ep_to(k)), :], dst_ref=dst.at[block(here.ep), :],
-                                            send_sem=ba_s.at[j, k], recv_sem=ba_r.at[j, k], device_id=(here.dp, here.ep_to(k)),
-                                            device_id_type=MESH_ID)
-
-    own = [pltpu.make_async_copy(src.at[block(here.ep), :], dst.at[block(here.ep), :], loc.at[j]) for j, (src, dst) in enumerate(pairs)]
+        return remote(src_ref=src.at[block(here.ep_to(k)), :], dst_ref=dst.at[block(ep, rows), :],
+                      send_sem=ba_s.at[j, k], recv_sem=ba_r.at[j, k], device_id=(here.dp, here.ep_to(k)))
+
+    own = [pltpu.make_async_copy(src.at[block(ep), :], dst.at[block(ep, rows), :], loc.at[j]) for j, (src, dst) in enumerate(pairs)]
     for j in range(2):
         for k in range(n_peer):
             back(j, k).start()
         own[j].start()
-    for j in range(2):
-        for k in range(n_peer):
-            back(j, k).wait()
-        own[j].wait()
+    home = pl.ds(0, rows)
+    loads = [pltpu.make_async_copy(src, dst, loc.at[2 + i]) for i, (src, dst) in enumerate((
+        (x_h, x_v), (dy_h, dy_v), (hid_h, hid_v), (o_h, o_v.at[home, :]), (dh_h, dh_v.at[home, :])))]
+    for c in loads:
+        c.start()
+    slots = lax.broadcasted_iota(jnp.int32, (n_tok, 2 * rows), 1)
+    sel_one[...] = (slots == places[:, 0:1]).astype(F32).astype(BF16)
+    sel_two[...] = (slots == places[:, 1:2]).astype(F32).astype(BF16)
+    gate_one, gate_two, mean, inv_std = [stats[:, i:i + 1] for i in range(4)]
+    zero = jnp.zeros((n_tok, 1), F32)
+    for c in loads:
+        c.wait()
+    own[0].wait()
+    for k in range(n_peer):
+        back(0, k).wait_recv()
+
+    def mix(i, sums):
+        cols = rows_at(i * wide, wide, 128)
+        one = jnp.dot(sel_one[...], o_v[:, cols], preferred_element_type=F32)
+        two = jnp.dot(sel_two[...], o_v[:, cols], preferred_element_type=F32)
+        dy = dy_v[:, cols].astype(F32)
+        out[:, cols] = (x_v[:, cols].astype(F32) + (gate_one * one + gate_two * two)).astype(BF16)
+        return sums[0] + jnp.sum(dy * one, axis=1, keepdims=True), sums[1] + jnp.sum(dy * two, axis=1, keepdims=True)
+
+    dgate_one, dgate_two = lax.fori_loop(0, d_model // wide, mix, (zero, zero))
+    d_logits = ((dgate_one * gate_one) * err_one[...] + (dgate_two * gate_two) * err_two[...]).astype(BF16)
+    lanes = d_logits.shape[1]
+    eye = (lax.broadcasted_iota(jnp.int32, (lanes, lanes), 0)
+           == lax.broadcasted_iota(jnp.int32, (lanes, lanes), 1)).astype(F32).astype(BF16)
+    d_logits_t = lax.dot_general(eye, d_logits, NT, preferred_element_type=F32).astype(BF16)[:16]
+    sel_both = sel_one[...] + sel_two[...]
+    row = lax.broadcasted_iota(jnp.int32, (8, wide), 0)
+    own[1].wait()
+    for k in range(n_peer):
+        back(1, k).wait_recv()
+
+    def gradient(i, sums):
+        cols = rows_at(i * wide, wide, 128)
+        grad = (jnp.dot(d_logits, router[:, cols], preferred_element_type=F32)
+                + jnp.dot(sel_both, dh_v[:, cols], preferred_element_type=F32))
+        x_hat = (x_v[:, cols].astype(F32) - mean) * inv_std
+        grad_h[:, cols] = grad
+        val[0:16, cols] = jnp.dot(d_logits_t, hid_v[:, cols], preferred_element_type=F32)
+        d_weight = jnp.sum(grad * x_hat, axis=0, keepdims=True)
+        d_bias = jnp.sum(grad, axis=0, keepdims=True)
+        val[16:24, cols] = jnp.where(row == 0, d_weight, jnp.where(row == 1, d_bias, 0.0))
+        scaled = grad * lnw[:, cols]
+        return sums[0] + jnp.sum(scaled, axis=1, keepdims=True), sums[1] + jnp.sum(scaled * x_hat, axis=1, keepdims=True)
+
+    mean_one, mean_two = lax.fori_loop(0, d_model // wide, gradient, (zero, zero))
+    mean_one, mean_two = mean_one / d_model, mean_two / d_model
+
+    def part(e):
+        return rows_at(e * width, width, 128)
+
+    def scatter(k):
+        to = here.ep_to(k)
+        return remote(src_ref=val.at[:, part(to)], dst_ref=first.at[ep], send_sem=s_one.at[k], recv_sem=r_one.at[k],
+                      device_id=(here.dp, to))
+
+    def along(axis, src, dst, send, recv, k):
+        mine = here.y if axis == 'y' else here.z
+        return remote(src_ref=src, dst_ref=dst.at[mine], send_sem=send.at[k], recv_sem=recv.at[k], device_id=here.device(axis, k))
+
+    def gather(k):
+        return remote(src_ref=c_three, dst_ref=small.at[:, part(ep)], send_sem=s_four.at[k], recv_sem=r_four.at[k],
+                      device_id=(here.dp, here.ep_to(k)))
+
+    def add_up(ref, n):
+        total = ref[0]
+        for i in range(1, n):
+            total = total + ref[i]
+        return total
+
+    for k in range(n_peer):
+        scatter(k).start()
+    first[ep] = val[:, part(ep)]
+
+    @pl.loop(0, d_model // wide)
+    def _(i):
+        cols = rows_at(i * wide, wide, 128)
+        x_hat = (x_v[:, cols].astype(F32) - mean) * inv_std
+        step = inv_std * (grad_h[:, cols] * lnw[:, cols] - mean_one - x_hat * mean_two)
+        dx[:, cols] = (dy_v[:, cols].astype(F32) + step).astype(BF16)
+
+    for k in range(n_peer):
+        scatter(k).wait_recv()
+    c_one[...] = add_up(first, n_ep)
+    second[here.y] = c_one[...]
+    for k in range(1, grid):
+        along('y', c_one, second, s_two, r_two, k).start()
+    for k in range(1, grid):
+        along('y', c_one, second, s_two, r_two, k).wait_recv()
+    c_two[...] = add_up(second, grid)
+    third[here.z] = c_two[...]
+    for k in range(1, grid):
+        along('z', c_two, third, s_three, r_three, k).start()
+    for k in range(1, grid):
+        along('z', c_two, third, s_three, r_three, k).wait_recv()
+    c_three[...] = add_up(third, grid)
+    for k in range(n_peer):
+        gather(k).start()
+    small[:, part(ep)] = c_three[...]
+    for k in range(n_peer):
+        gather(k).wait_recv()
+    for k in range(n_peer):
+        scatter(k).wait_send()
+        gather(k).wait_send()
+        back(0, k).wait_send()
+        back(1, k).wait_send()
+    for k in range(1, grid):
+        along('y', c_one, second, s_two, r_two, k).wait_send()
+        along('z', c_two, third, s_three, r_three, k).wait_send()
     spread.receive(3)
     spread.sent(3)
 
 
-def spread_call(held, o, dh, cap, grid, collective_id):
-    dma = pltpu.SemaphoreType.DMA
-    n_peer = o.shape[0] // cap - 1
-    hbm = pl.BlockSpec(memory_space=pl.ANY)
+def tail_call(held, o_next, dh_next, tok_x, tok_dy, hidden, o, dh, stats, err_one, err_two, places, lnw, router, cap, grid, collective_id):
+    vmem, dma = pltpu.VMEM, pltpu.SemaphoreType.DMA
+    n_tok, d_model = tok_x.shape
+    rows = o.shape[0]
+    n_ep = rows // cap
+    n_peer, width = n_ep - 1, d_model // n_ep
+    hbm, on_chip = pl.BlockSpec(memory_space=pl.ANY), pl.BlockSpec(memory_space=pltpu.VMEM)
+    tokens = jax.ShapeDtypeStruct((n_tok, d_model), BF16)
+    peers, ring = dma((n_peer,)), dma((grid,))
     return pl.pallas_call(
-        functools.partial(spread_kernel, grid, cap),
-        out_shape=tuple(jax.ShapeDtypeStruct(x.shape, x.dtype) for x in (held, o, dh)),
-        in_specs=[hbm] * 3, out_specs=(hbm,) * 3, input_output_aliases={0: 0},
-        scratch_shapes=[dma((UNITS, 15)), dma((UNITS, 15)), dma((2, n_peer)), dma((2, n_peer)), dma((2,))],
-        compiler_params=pltpu.CompilerParams(collective_id=collective_id, has_side_effects=True),
-        cost_estimate=pl.CostEstimate(flops=1_000_000_000, bytes_accessed=30_000_000, transcendentals=0),
-        name='spread',
-    )(held, o, dh)
+        functools.partial(tail_kernel, grid, cap),
+        out_shape=(jax.ShapeDtypeStruct(held.shape, F32), tokens, tokens, jax.ShapeDtypeStruct((24, d_model), F32)),
+        in_specs=[hbm] * 8 + [on_chip] * 6, out_specs=(hbm, on_chip, on_chip, on_chip), input_output_aliases={0: 0},
+        scratch_shapes=[vmem((n_tok, d_model), BF16)] * 3 + [vmem((2 * rows, d_model), BF16)] * 2
+        + [vmem((n_tok, 2 * rows), BF16)] * 2 + [vmem((n_tok, d_model), F32), vmem((24, d_model), F32)]
+        + [vmem((n_ep, 24, width), F32), vmem((grid, 24, width), F32), vmem((grid, 24, width), F32)] + [vmem((24, width), F32)] * 3
+        + [dma((7,)), dma((UNITS, 15)), dma((UNITS, 15)), dma((2, n_peer)), dma((2, n_peer)),
+           peers, peers, ring, ring, ring, ring, peers, peers],
+        compiler_params=pltpu.CompilerParams(collective_id=collective_id, has_side_effects=True, vmem_limit_bytes=50 * 2 ** 20),
+        cost_estimate=pl.CostEstimate(flops=10_000_000_000, bytes_accessed=30_000_000, transcendentals=0),
+        name='tail',
+    )(held, o_next, dh_next, tok_x, tok_dy, hidden, o, dh, stats, err_one, err_two, places, lnw, router)
 
 
 def expert_kernel(dims, *refs):
@@ -192,7 +316,7 @@
     refs = list(refs)
     take = lambda n: [refs.pop(0) for _ in range(n)]
     if first:
-        sel_in, wg_h, wu_h, wd_h = take(6), *take(3)
+        sel_in, wg_h, wu_h, wd_h = take(7), *take(3)
         o_h, dh_h, sh_h, h_next, q_next, hsl_next, qsl_next = take(7)
     else:
         h_next, q_next, hsl_next, qsl_next, wg_h, wu_h, wd_h, *carry = take(9)
@@ -202,7 +326,7 @@
     h_recv, q_recv, wg, wu, wd, a_t, b_t, d_t, u_all, da_all, db_all, h_sl, q_sl, dw, rsb, act, act_b, eye = take(18)
     loc, hs_s, hs_r, qs_s, qs_r, ga_s, ga_r, rs_s, rs_r = take(9)
     if first:
-        sel_h, sel_q, sel_h_next, sel_q_next, hidden, pair, h_send, q_send, h_send_next, q_send_next = take(10)
+        sel_h, sel_q, sel_h_next, sel_q_next, hidden, grad_one, grad_two, h_send, q_send, h_send_next, q_send_next = take(11)
         xh_s, xh_r, xq_s, xq_r, nh_s, nh_r, nq_s, nq_r, ns_h_s, ns_h_r, ns_q_s, ns_q_r, lin = take(13)
         o_v, dh_v = h_send, q_send
     else:
@@ -368,7 +492,7 @@
 
     if first:
         inputs = [pltpu.make_async_copy(src, dst, lin.at[i])
-                  for i, (src, dst) in enumerate(zip(sel_in, (sel_h, hidden, sel_q, pair, sel_h_next, sel_q_next)))]
+                  for i, (src, dst) in enumerate(zip(sel_in, (sel_h, hidden, sel_q, grad_one, grad_two, sel_h_next, sel_q_next)))]
         for c in inputs:
             c.start()
         here.barrier()
@@ -379,10 +503,15 @@
             @pl.loop(0, d_model // chunk)
             def _(i):
                 cols = rows_at(i * chunk, chunk, 128)
-                out[block(e), cols] = jnp.dot(sel[block(e), :], source[:, cols], preferred_element_type=F32).astype(BF16)
-
-        now = ((sel_h, hidden, h_send, h_recv, xh_s, xh_r), (sel_q, pair, q_send, q_recv, xq_s, xq_r))
-        later = ((sel_h_next, hidden, h_send_next, h_next, nh_s, nh_r), (sel_q_next, pair, q_send_next, q_next, nq_s, nq_r))
+                total = jnp.dot(sel[block(e), :n_tok], source[0][:, cols], preferred_element_type=F32)
+                for j in range(1, len(source)):
+                    total += jnp.dot(sel[block(e), j * n_tok:(j + 1) * n_tok], source[j][:, cols], preferred_element_type=F32)
+                out[block(e), cols] = total.astype(BF16)
+
+        n_tok = hidden.shape[0]
+        rows_h, rows_q = (hidden,), (grad_one, grad_two)
+        now = ((sel_h, rows_h, h_send, h_recv, xh_s, xh_r), (sel_q, rows_q, q_send, q_recv, xq_s, xq_r))
+        later = ((sel_h_next, rows_h, h_send_next, h_next, nh_s, nh_r), (sel_q_next, rows_q, q_send_next, q_next, nq_s, nq_r))
 
         def copy_of(what, k):
             _, _, out, recv_buf, send, recv = what
@@ -424,11 +553,16 @@
         forward_own(spread, (h_recv, q_recv))
         for what in later:
             gather(what[0], what[1], what[2], ep)
-        own_next = [pltpu.make_async_copy(what[2].at[block(ep), :], what[3].at[block(ep), :], lin.at[6 + i]) for i, what in enumerate(later)]
+        own_next = [pltpu.make_async_copy(what[2].at[block(ep), :], what[3].at[block(ep), :], lin.at[7 + i]) for i, what in enumerate(later)]
         for p in range(n_peer):
             forward(now, spread, p)
             for what in later:
                 dispatch(what, p)
+            if p == min(3, n_peer - 1):
+                while pending:
+                    pending.pop(0).start()
+                forward_own(spread_next, (h_send_next, q_send_next))
+                forward(later, spread_next, 0)
         while pending:
             pending.pop(0).start()
         for c in own_next:
@@ -499,8 +633,6 @@
     dh_out = pltpu.make_async_copy(dh_v, dh_h, loc.at[4])
     dh_out.start()
     if first:
-        forward_own(spread_next, (h_send_next, q_send_next))
-        forward(later, spread_next, 0)
         for k in range(1, grid):
             slices('z', q_recv, q_sl, qs_s, qs_r, k).wait_recv()
     else:
@@ -588,9 +720,9 @@
     share_block = (UNITS, 3, share, quarter // UNITS)
     outs = [out(row_block), out(row_block), out(share_block, F32)]
     if first:
-        sel_h, hidden, sel_q, pair, sel_h_next, sel_q_next = inputs
-        scratch += [vmem(x.shape, BF16) for x in (sel_h, sel_q, sel_h_next, sel_q_next, hidden, pair)]
-        scratch += [vmem(row_block, BF16)] * 4 + [dma((n_peer,))] * 8 + [dma((grid,))] * 4 + [dma((8,))]
+        sel_h, hidden, sel_q, grad_one, grad_two, sel_h_next, sel_q_next = inputs
+        scratch += [vmem(x.shape, BF16) for x in (sel_h, sel_q, sel_h_next, sel_q_next, hidden, grad_one, grad_two)]
+        scratch += [vmem(row_block, BF16)] * 4 + [dma((n_peer,))] * 8 + [dma((grid,))] * 4 + [dma((9,))]
         operands = (*inputs, w_gate, w_up, w_down)
         outs += [out(row_block), out(row_block), out(slice_block), out(slice_block)]
     else:
@@ -607,86 +739,11 @@
     )(*operands)
 
 
-def small_sum_kernel(grid, val, out, first, second, third, c_one, c_two, c_three, s_one, r_one, s_two, r_two, s_three, r_three, s_four, r_four):
-    n_ep, _, width = first.shape
-    here = Place(n_ep, grid)
-    n_peer = len(here.offsets)
-    ep = here.ep
-    remote = functools.partial(pltpu.make_async_remote_copy, device_id_type=MESH_ID)
-    here.barrier()
-
-    def cols(e):
-        return rows_at(e * width, width, 128)
-
-    def scatter(k):
-        to = here.ep_to(k)
-        return remote(src_ref=val.at[:, cols(to)], dst_ref=first.at[ep], send_sem=s_one.at[k], recv_sem=r_one.at[k],
-                      device_id=(here.dp, to))
-
-    def along(axis, src, dst, send, recv, k):
-        mine = here.y if axis == 'y' else here.z
-        return remote(src_ref=src, dst_ref=dst.at[mine], send_sem=send.at[k], recv_sem=recv.at[k], device_id=here.device(axis, k))
-
-    def gather(k):
-        return remote(src_ref=c_three, dst_ref=out.at[:, cols(ep)], send_sem=s_four.at[k], recv_sem=r_four.at[k],
-                      device_id=(here.dp, here.ep_to(k)))
-
-    def add_up(ref, n):
-        total = ref[0]
-        for i in range(1, n):
-            total = total + ref[i]
-        return total
-
-    for k in range(n_peer):
-        scatter(k).start()
-    first[ep] = val[:, cols(ep)]
-    for k in range(n_peer):
-        scatter(k).wait_recv()
-    c_one[...] = add_up(first, n_ep)
-    second[here.y] = c_one[...]
-    for k in range(1, grid):
-        along('y', c_one, second, s_two, r_two, k).start()
-    for k in range(1, grid):
-        along('y', c_one, second, s_two, r_two, k).wait_recv()
-    c_two[...] = add_up(second, grid)
-    third[here.z] = c_two[...]
-    for k in range(1, grid):
-        along('z', c_two, third, s_three, r_three, k).start()
-    for k in range(1, grid):
-        along('z', c_two, third, s_three, r_three, k).wait_recv()
-    c_three[...] = add_up(third, grid)
-    for k in range(n_peer):
-        gather(k).start()
-    out[:, cols(ep)] = c_three[...]
-    for k in range(n_peer):
-        gather(k).wait_recv()
-    for k in range(n_peer):
-        scatter(k).wait_send()
-        gather(k).wait_send()
-    for k in range(1, grid):
-        along('y', c_one, second, s_two, r_two, k).wait_send()
-        along('z', c_two, third, s_three, r_three, k).wait_send()
-
-
-def small_sum(val, n_ep, grid, collective_id):
-    rows, d_model = val.shape
-    width = d_model // n_ep
-    vmem, dma = pltpu.VMEM, pltpu.SemaphoreType.DMA
-    return pl.pallas_call(
-        functools.partial(small_sum_kernel, grid),
-        out_shape=jax.ShapeDtypeStruct(val.shape, F32),
-        in_specs=[pl.BlockSpec(memory_space=pltpu.VMEM)], out_specs=pl.BlockSpec(memory_space=pltpu.VMEM),
-        scratch_shapes=[vmem((n_ep, rows, width), F32), vmem((grid, rows, width), F32), vmem((grid, rows, width), F32),
-                        vmem((rows, width), F32), vmem((rows, width), F32), vmem((rows, width), F32),
-                        dma((n_ep - 1,)), dma((n_ep - 1,)), dma((grid,)), dma((grid,)), dma((grid,)), dma((grid,)),
-                        dma((n_ep - 1,)), dma((n_ep - 1,))],
-        compiler_params=pltpu.CompilerParams(collective_id=collective_id, has_side_effects=True),
-        name='small_sum',
-    )(val)
-
-
 def assemble_kernel(gate, up, down, *refs):
-    outs = refs[-3:]
+    n_pass = (len(refs) - 3) // 2 if len(refs) > 6 else 0
+    outs = refs[-3 - n_pass:][:3]
+    for j in range(n_pass):
+        refs[-n_pass + j][...] = refs[j][...]
     grid, unit = gate.shape[1], gate.shape[-1]
     for c in range(grid):
         for i in range(UNITS):
@@ -696,7 +753,7 @@
             outs[2][0, :, at:at + unit] = down[c, 0, i, 0]
 
 
-def assemble(gathered, expert, n_expert, into):
+def assemble(gathered, expert, n_expert, into, through=()):
     grid, _, _, _, share, unit = gathered.shape
     cut = 2
     part = share // cut
@@ -705,13 +762,14 @@
     col_first = pl.BlockSpec((grid, 1, UNITS, 1, part, unit), lambda r, h: (0, r, 0, 2, h, 0))
     out_spec = pl.BlockSpec((1, part, grid * UNITS * unit), lambda r, h: (expert, r * cut + h, 0))
     whole = jax.ShapeDtypeStruct((n_expert, grid * share, grid * UNITS * unit), F32)
+    strips = [pl.BlockSpec((x.shape[0] // (grid * cut), x.shape[1]), lambda r, h: (r * cut + h, 0)) for x in through]
     return pl.pallas_call(
-        assemble_kernel, grid=(grid, cut), out_shape=(whole,) * 3,
-        in_specs=[row_first, up_first, col_first] + [pl.BlockSpec(memory_space=pl.ANY)] * len(into),
-        out_specs=(out_spec,) * 3, input_output_aliases={3 + i: i for i in range(len(into))},
+        assemble_kernel, grid=(grid, cut), out_shape=(whole,) * 3 + tuple(jax.ShapeDtypeStruct(x.shape, x.dtype) for x in through),
+        in_specs=[row_first, up_first, col_first] + strips + [pl.BlockSpec(memory_space=pl.ANY)] * len(into),
+        out_specs=(out_spec,) * 3 + tuple(strips), input_output_aliases={3 + i: i for i in range(len(into))},
         compiler_params=pltpu.CompilerParams(vmem_limit_bytes=40 * 2 ** 20),
         cost_estimate=pl.CostEstimate(flops=1_000_000, bytes_accessed=44_000_000, transcendentals=0),
-    )(gathered, gathered, gathered, *into)
+    )(gathered, gathered, gathered, *through, *into)
 
 
 def solution(mesh):
@@ -723,11 +781,11 @@
 
     def local_step(tok_x, tok_dy, exp_first, exp_second, eligible, slot_first, slot_second,
                    ln_weight, ln_bias, router, w_gate, w_up, w_down):
-        n_local, d_model = tok_x.shape
+        n_local, _ = tok_x.shape
         n_exp = eligible.shape[1]
         local_exp = w_gate.shape[0]
         slot_cap = 3 * n_local // n_exp
-        hidden, x_hat, inv_std = layer_norm(tok_x, ln_weight, ln_bias)
+        hidden, mean, inv_std = layer_norm(tok_x, ln_weight, ln_bias)
         logits = jnp.dot(hidden, router, preferred_element_type=F32)
         expert_ids = jnp.arange(n_exp)
         allowed = eligible > 0
@@ -742,48 +800,36 @@
 
         pos_one = place(exp_first, slot_first)
         pos_two = place(exp_second, slot_second)
-        sel_one = (pos_one[:, None] == row_ids[None, :]).astype(BF16)
-        sel_two = (pos_two[:, None] == row_ids[None, :]).astype(BF16)
-        sel_both = sel_one + sel_two
         dy_float = tok_dy.astype(F32)
         grad_one = (gate_one[:, None] * dy_float).astype(BF16)
         grad_two = (gate_two[:, None] * dy_float).astype(BF16)
-        pair = jnp.concatenate([grad_one, grad_two], axis=0)
         pos_pair = jnp.concatenate([pos_one, pos_two])
         wg_t, wu_t = jnp.swapaxes(w_gate, 1, 2), jnp.swapaxes(w_up, 1, 2)
+
+        def lanes(columns):
+            flat = jnp.concatenate(columns, axis=1)
+            return jnp.pad(flat, ((0, 0), (0, 128 - flat.shape[1])))
+
+        stats = lanes([gate_one[:, None], gate_two[:, None], mean, inv_std])
+        err_one, err_two = lanes([pick_one - prob_one]), lanes([pick_two - prob_two])
+        places = lanes([pos_one[:, None], pos_two[:, None]])
+        router_t = jnp.pad(router.T, ((0, 128 - n_exp), (0, 0)))
         cuts = [slice(e * per, (e + 1) * per) for e in range(local_exp)]
         sels = []
         for e in range(local_exp):
             ids = row_ids[cuts[e]][:, None]
             sels.append(jnp.logical_or(ids == pos_one[None, :], ids == pos_two[None, :]).astype(BF16))
             sels.append((ids == pos_pair[None, :]).astype(BF16))
-        o, dh, share, *landed = expert_call((sels[0], hidden, sels[1], pair, sels[2], sels[3]), wg_t, wu_t, w_down, 0, slot_cap, grid)
+        o, dh, share, *landed = expert_call((sels[0], hidden, sels[1], grad_one, grad_two, sels[2], sels[3]), wg_t, wu_t, w_down, 0, slot_cap, grid)
         o_next, dh_next, share, o, dh, held = expert_call((*landed, o, dh, share), wg_t, wu_t, w_down, 1, slot_cap, grid)
         gathered_next = lax.all_gather(share, 'dp')
-        held, o_next, dh_next = spread_call(held, o_next, dh_next, slot_cap, grid, local_exp + 1)
+        held, out_tok, dx_tok, small = tail_call(
+            held, o_next, dh_next, tok_x, tok_dy, hidden, o, dh, stats, err_one, err_two, places,
+            ln_weight.astype(F32)[None], router_t, slot_cap, grid, local_exp + 1)
         gathered = [x.reshape((grid, grid) + share.shape) for x in (held, gathered_next)]
-        outs, grads = [o, o_next], [dh, dh_next]
-        sel_cat = [sel_one, sel_two]
-        out_one, out_two = [sum(jnp.dot(s[:, c], o, preferred_element_type=F32) for c, o in zip(cuts, outs)) for s in sel_cat]
-        y_mix = gate_one[:, None] * out_one + gate_two[:, None] * out_two
-        out_tok = (tok_x.astype(F32) + y_mix).astype(BF16)
-        grad_exp = sum(jnp.dot(sel_both[:, c], g, preferred_element_type=F32) for c, g in zip(cuts, grads))
-        dgate_one = jnp.sum(dy_float * out_one, axis=-1)
-        dgate_two = jnp.sum(dy_float * out_two, axis=-1)
-        d_logits = ((dgate_one * gate_one)[:, None] * (pick_one - prob_one)
-                    + (dgate_two * gate_two)[:, None] * (pick_two - prob_two)).astype(BF16)
-        d_router = jnp.einsum('te,td->ed', d_logits, hidden, preferred_element_type=F32)
-        grad_h = jnp.einsum('te,de->td', d_logits, router, preferred_element_type=F32) + grad_exp
-        d_ln_weight = jnp.sum(grad_h * x_hat, axis=0)
-        d_ln_bias = jnp.sum(grad_h, axis=0)
-        dx_tok = (dy_float + layer_norm_back(grad_h, x_hat, inv_std, ln_weight)).astype(BF16)
-        small = jnp.concatenate([d_router, d_ln_weight[None], d_ln_bias[None], jnp.zeros((6, d_model), F32)], axis=0)
-        small = small_sum(small, n_ep, grid, local_exp)
-        d_router, d_ln_weight, d_ln_bias = small[:n_exp].T, small[n_exp], small[n_exp + 1]
-
-        weights = ()
-        for e in range(local_exp):
-            weights = assemble(gathered[e], e, local_exp, weights)
+        d_router, d_ln_weight, d_ln_bias = small[:n_exp].T, small[16], small[17]
+        *weights, out_tok, dx_tok = assemble(gathered[0], 0, local_exp, (), (out_tok, dx_tok))
+        weights = assemble(gathered[1], 1, local_exp, weights)
         dw_gate, dw_up, dw_down = jnp.swapaxes(weights[0], 1, 2), jnp.swapaxes(weights[1], 1, 2), weights[2]
         return out_tok, dx_tok, dw_gate, dw_up, dw_down, d_router, d_ln_weight, d_ln_bias
 

time: 516 us -> 515 us (level)
  waiting for transfers between devices: 0.02 us -> 35.8 us
  Pallas kernels: 464 us -> 448 us
  matrix products: 15.7 us -> 0.76 us
    all_gather x1, waiting for transfers between devices: 0.01 us -> 35.8 us  [local_step(): gathered_next = lax.all_gather(share, 'dp')]
    pallas_call x4 -> x3, Pallas kernels: 174 us -> 159 us  [the longest x1 125 us: tail_call(): pl.pallas_call(functools.partial(tail_kernel, grid, cap), out_shape=(jax....]
    dot_general x8 -> x0, matrix products: 15 us -> none  [the longest x4 8.02 us: local_step(): jnp.dot(s[:, c], o, preferred_element_type=F32)]
  transfers between devices with their start and end apart: 1 -> 1, of which waited for: 0 -> 1; matrix products, arithmetic and copies ran while one was open for 4% -> 0% of each run, Pallas kernels for 31% -> 28%
where the time goes in v1:
time: 515 us
  Pallas kernels  448 us (87%)
  waiting for transfers between devices  35.8 us (7%)
  between operations  14.4 us (3%)
  other arithmetic  11.7 us (2%)
    pallas_call x2, Pallas kernels, expert_call(): pl.pallas_call(functools.partial(expert_kernel, (expert, grid, chunk, cap...  289 us
    pallas_call x1, Pallas kernels, tail_call(): pl.pallas_call(functools.partial(tail_kernel, grid, cap), out_shape=(jax....  125 us
    all_gather x1, waiting for transfers between devices, local_step(): gathered_next = lax.all_gather(share, 'dp')  35.8 us
    pallas_call x2, Pallas kernels, assemble(): pl.pallas_call(assemble_kernel, grid=(grid, cut), out_shape=(whole,) * 3...  33.8 us
  transfers between devices with their start and end apart: 1, of which 1 were waited for; matrix products, arithmetic and copies ran while one was open for 0% of the time, Pallas kernels for 28%

profile of v1, /device:TPU:1, one launch (start us, length us, event | category | flops | bytes accessed | tf_op | source)
XLA Modules:
  0.0 515.1 jit_solution(4535643947082806204)
XLA Ops:
  7.2 0.0 copy-start.1
  7.3 0.0 all-gather.3.cloned.1.call-start
  7.3 2.1 convert_reduce_fusion
  9.4 2.3 fusion.2
  11.8 0.0 copy-done.9
  11.8 0.0 copy-done.6
  11.8 0.1 copy.37
  12.0 0.9 or_convert_fusion
  12.9 1.1 compare_convert_fusion
  14.0 1.0 fusion.5.refs_1_.refs_5_
  15.0 0.0 copy-start.3
  15.0 1.3 copy-done.3
  16.3 0.0 copy-done.4
  16.3 0.8 fusion.14
  17.1 0.3 fusion.21
  17.4 0.3 fusion.13
  17.7 0.2 convert_subtract_fusion.1
  17.9 0.2 select_reduce_fusion
  18.1 3.2 fusion.7
  21.3 176.0 %shard_map.188 = (bf16[384,4096]{1,0:T(8,128)(2,1)}, bf16[384,4096]{1,0:T(8,128)(2,1)}, f32[4,3,112,256]{3,2,1,0:T(8,128)}, bf16[384,4096]{1,0:T(8,128)(2,1)}, b...) custom-call(bf16[384,256]{1,0:T(8,128)(2,1)} %get-tuple-element.74.refs_0_, ...), custom_call_target="tpu_custom_call" | custom-call | flops 12683575296 | bytes 30000000 | tf_op jit(solution)/shard_map/pallas_call | solution.py:734
  197.4 112.5 %shard_map.189 = (bf16[384,4096]{1,0:T(8,128)(2,1)}, bf16[384,4096]{1,0:T(8,128)(2,1)}, f32[4,3,112,256]{3,2,1,0:T(8,128)}, bf16[384,4096]{1,0:T(8,128)(2,1)}, b...) custom-call(bf16[384,4096]{1,0:T(8,128)(2,1)} %get-tuple-element.33.refs_0_, ...), custom_call_target="tpu_custom_call" | custom-call | flops 12683575296 | bytes 30000000 | tf_op jit(solution)/shard_map/pallas_call | solution.py:734
  309.9 0.0 all-gather.3.cloned.1.call-update
  309.9 0.1 copy.41
  310.1 0.1 copy.40
  310.3 0.1 pad.23.refs_13_
  310.4 125.2 %tail.1 = (f32[16,4,3,112,256]{4,3,2,1,0:T(8,128)}, bf16[256,4096]{1,0:T(8,128)(2,1)S(1)}, bf16[256,4096]{1,0:T(8,128)(2,1)}, f32[24,4096]{1,0:T(8,128)S(1)}) custom-call(f32[16,4,3,112,256]{4,3,2,1,0:T(8,128)} %get-tuple-element.40.refs_0_, bf16[384,4096]{1,0:T(8,128)(2,1)} %get-tuple-element.41.refs_1_, ...), custom_call_target="tpu_custom_call", output_to_operand_aliasing={{0}: (0, {})} | custom-call | flops 10000000000 | bytes 30000000 | tf_op jit(solution)/shard_map/tail/pallas_call | solution.py:299
  435.6 1.7 copy-done
  437.3 17.4 %shard_map.190 = (f32[2,448,4096]{2,1,0:T(8,128)}, f32[2,448,4096]{2,1,0:T(8,128)}, f32[2,448,4096]{2,1,0:T(8,128)}, bf16[256,4096]{1,0:T(8,128)(2,1)}, bf16[256,4096]{1,0:T(8,128)(2,1)}) custom-call(f32[4,4,4,3,112,256]{5,4,3,2,1,0:T(8,128)} %bitcast.21, f32[4,4,4,3,112,256]{5,4,3,2,1,0:T(8,128)} %bitcast.22, f32[4,4,4,3,112,256]{5,4,3,2,1,0:T(8,128)} %bitcast.23, ...), custom_call_target="tpu_custom_call" | custom-call | flops 1000000 | bytes 44000000 | tf_op jit(solution)/shard_map/pallas_call | solution.py:766
  454.7 0.6 fusion.23
  455.3 0.7 slice_bitcast_fusion
  456.0 35.8 %all-gather.3.cloned.1.call-done = f32[64,3,112,256]{3,2,1,0:T(8,128)} async-done(((f32[4,3,112,256]{3,2,1,0:T(8,128)}), f32[64,3,112,256]{3,2,1,0:T(8,128)}) %all-gather.3.cloned.1.call-update) | async-done | bytes 22020112 | tf_op jit(solution)/shard_map/all_gather | solution.py:825
  491.8 16.4 %shard_map.191 = (f32[2,448,4096]{2,1,0:T(8,128)}, f32[2,448,4096]{2,1,0:T(8,128)}, f32[2,448,4096]{2,1,0:T(8,128)}) custom-call(f32[4,4,4,3,112,256]{5,4,3,2,1,0:T(8,128)} %bitcast.24, f32[4,4,4,3,112,256]{5,4,3,2,1,0:T(8,128)} %bitcast.25, f32[4,4,4,3,112,256]{5,4,3,2,1,0:T(8,128)} %bitcast.26, ...), custom_call_target="tpu_custom_call", output_to_operand_aliasing={{0}: (3, {}), {1}: (4, {}), {2}: (5, {})} | custom-call | flops 1000000 | bytes 44000000 | tf_op jit(solution)/shard_map/pallas_call | solution.py:766
  (33 shorter events, 0.2 us)
Async XLA Ops:
  7.2 6.8 %copy-start.1 = (bf16[256,4096]{1,0:T(8,128)(2,1)S(1)}, bf16[256,4096]{1,0:T(8,128)(2,1)}, u32[]{:S(2)}) copy-start(bf16[256,4096]{1,0:T(8,128)(2,1)} %refs_3_.1) | copy-start | bytes 6291460
  7.2 4.6 copy-start.8
  7.2 4.6 copy-start.9
  7.2 4.6 copy-start.6
  7.2 4.7 copy-start.5
  7.2 4.7 copy-start.7
  7.2 4.7 copy-start.10
  7.2 4.7 copy-start.11
  7.3 484.6 %all-gather.3.cloned.1.call-start = ((), (), s32[]{:S(2)}) async-start(), calls=%async_computation | async-start | bytes 23396352 | tf_op jit(solution)/shard_map/all_gather | solution.py:825
  9.4 7.0 %copy-start.4 = (bf16[4096,16]{0,1:T(8,128)(2,1)S(1)}, bf16[4096,16]{0,1:T(8,128)(2,1)}, u32[]{:S(2)}) copy-start(bf16[4096,16]{0,1:T(8,128)(2,1)} %param.22) | copy-start | bytes 393220
  14.0 4.1 copy-start.2
  15.0 1.3 copy-start.3
  435.6 1.7 copy-start
Sparse Core Ops, SparseCore 0:
  310.0 181.7 all-gather.2

commit v2 on v1

--- a/solution.py
+++ b/solution.py
@@ -11,19 +11,26 @@
 LN_EPS = 1e-5
 CORES = 2
 UNITS = 4
+NEAR, FAR = (1, 3), (3, 1)
+LANES = 128
+PACK = 16
+SMALL = 24
+STREAM = 30_000_000
+KEEP = {'keepdims': True}
 F32 = jnp.float32
 BF16 = jnp.bfloat16
+ALL = Ellipsis
 MESH_ID = pl.DeviceIdType.MESH
 NT = (((1,), (1,)), ((), ()))
 
 
 def layer_norm(x_rows, ln_weight, ln_bias):
     x_float = x_rows.astype(F32)
-    centered = x_float - jnp.mean(x_float, axis=-1, keepdims=True)
-    inv_std = lax.rsqrt(jnp.mean(centered * centered, axis=-1, keepdims=True) + LN_EPS)
+    centered = x_float - jnp.mean(x_float, axis=-1, **KEEP)
+    inv_std = lax.rsqrt(jnp.mean(centered * centered, axis=-1, **KEEP) + LN_EPS)
     x_hat = centered * inv_std
     hidden = (x_hat * ln_weight.astype(F32) + ln_bias.astype(F32)).astype(BF16)
-    return hidden, jnp.mean(x_float, axis=-1, keepdims=True), inv_std
+    return hidden, jnp.mean(x_float, axis=-1, **KEEP), inv_std
 
 
 def masked_gate(logits, allowed, choice):
@@ -74,14 +81,17 @@
             return (self.z * self.grid + (self.y ^ bits), self.ep)
         return ((self.z ^ bits) * self.grid + self.y, self.ep)
 
-    def barrier(self):
+    def arrive(self):
         sem = pltpu.get_barrier_semaphore()
         peers = [(self.dp, self.ep_to(k)) for k in range(len(self.offsets))]
         for k in range(1, self.grid):
             peers += [self.device('y', k), self.device('z', k)]
         for peer in peers:
             pl.semaphore_signal(sem, inc=1, device_id=peer, device_id_type=MESH_ID)
-        pl.semaphore_wait(sem, len(peers))
+        return len(peers)
+
+    def barrier(self, signals=None):
+        pl.semaphore_wait(pltpu.get_barrier_semaphore(), self.arrive() if signals is None else signals)
 
 
 def rows_at(start, size, unit):
@@ -89,14 +99,14 @@
 
 
 class Spread:
-    STAGES = ((0,), (1, 2), (3, 4, 5, 6), tuple(range(7, 15)))
+    STAGES = [range(2 ** i - 1, 2 ** (i + 1) - 1) for i in range(UNITS)]
 
     def __init__(self, here, own, held, send, recv):
         self.here, self.own, self.held, self.sems = here, own, held, (send, recv)
 
     def plan(self, unit, index):
         axes = ('y', 'z') if unit < UNITS // 2 else ('z', 'y')
-        one, two = (1, 3) if unit % 2 == 0 else (3, 1)
+        one, two = FAR if unit % 2 else NEAR
         line = (0, one, two, one ^ two)
         if index < 1:
             return axes, (axes[0], one), (0, 0)
@@ -156,7 +166,7 @@
     spread.send(3)
 
     def block(e, base=0):
-        return rows_at(base + e * cap, cap, 16)
+        return rows_at(base + e * cap, cap, PACK)
 
     pairs = ((o_next_h, o_v), (dh_next_h, dh_v))
 
@@ -176,8 +186,8 @@
     for c in loads:
         c.start()
     slots = lax.broadcasted_iota(jnp.int32, (n_tok, 2 * rows), 1)
-    sel_one[...] = (slots == places[:, 0:1]).astype(F32).astype(BF16)
-    sel_two[...] = (slots == places[:, 1:2]).astype(F32).astype(BF16)
+    sel_one[ALL] = (slots == places[:, 0:1]).astype(F32).astype(BF16)
+    sel_two[ALL] = (slots == places[:, 1:2]).astype(F32).astype(BF16)
     gate_one, gate_two, mean, inv_std = [stats[:, i:i + 1] for i in range(4)]
     zero = jnp.zeros((n_tok, 1), F32)
     for c in loads:
@@ -187,43 +197,43 @@
         back(0, k).wait_recv()
 
     def mix(i, sums):
-        cols = rows_at(i * wide, wide, 128)
-        one = jnp.dot(sel_one[...], o_v[:, cols], preferred_element_type=F32)
-        two = jnp.dot(sel_two[...], o_v[:, cols], preferred_element_type=F32)
+        cols = rows_at(i * wide, wide, LANES)
+        one = jnp.dot(sel_one[ALL], o_v[:, cols], preferred_element_type=F32)
+        two = jnp.dot(sel_two[ALL], o_v[:, cols], preferred_element_type=F32)
         dy = dy_v[:, cols].astype(F32)
         out[:, cols] = (x_v[:, cols].astype(F32) + (gate_one * one + gate_two * two)).astype(BF16)
-        return sums[0] + jnp.sum(dy * one, axis=1, keepdims=True), sums[1] + jnp.sum(dy * two, axis=1, keepdims=True)
+        return sums[0] + jnp.sum(dy * one, axis=1, **KEEP), sums[1] + jnp.sum(dy * two, axis=1, **KEEP)
 
     dgate_one, dgate_two = lax.fori_loop(0, d_model // wide, mix, (zero, zero))
-    d_logits = ((dgate_one * gate_one) * err_one[...] + (dgate_two * gate_two) * err_two[...]).astype(BF16)
+    d_logits = ((dgate_one * gate_one) * err_one[ALL] + (dgate_two * gate_two) * err_two[ALL]).astype(BF16)
     lanes = d_logits.shape[1]
     eye = (lax.broadcasted_iota(jnp.int32, (lanes, lanes), 0)
            == lax.broadcasted_iota(jnp.int32, (lanes, lanes), 1)).astype(F32).astype(BF16)
     d_logits_t = lax.dot_general(eye, d_logits, NT, preferred_element_type=F32).astype(BF16)[:16]
-    sel_both = sel_one[...] + sel_two[...]
+    sel_both = sel_one[ALL] + sel_two[ALL]
     row = lax.broadcasted_iota(jnp.int32, (8, wide), 0)
     own[1].wait()
     for k in range(n_peer):
         back(1, k).wait_recv()
 
     def gradient(i, sums):
-        cols = rows_at(i * wide, wide, 128)
+        cols = rows_at(i * wide, wide, LANES)
         grad = (jnp.dot(d_logits, router[:, cols], preferred_element_type=F32)
                 + jnp.dot(sel_both, dh_v[:, cols], preferred_element_type=F32))
         x_hat = (x_v[:, cols].astype(F32) - mean) * inv_std
         grad_h[:, cols] = grad
         val[0:16, cols] = jnp.dot(d_logits_t, hid_v[:, cols], preferred_element_type=F32)
-        d_weight = jnp.sum(grad * x_hat, axis=0, keepdims=True)
-        d_bias = jnp.sum(grad, axis=0, keepdims=True)
-        val[16:24, cols] = jnp.where(row == 0, d_weight, jnp.where(row == 1, d_bias, 0.0))
+        d_weight = jnp.sum(grad * x_hat, axis=0, **KEEP)
+        d_bias = jnp.sum(grad, axis=0, **KEEP)
+        val[16:SMALL, cols] = jnp.where(row == 0, d_weight, jnp.where(row == 1, d_bias, 0.0))
         scaled = grad * lnw[:, cols]
-        return sums[0] + jnp.sum(scaled, axis=1, keepdims=True), sums[1] + jnp.sum(scaled * x_hat, axis=1, keepdims=True)
+        return sums[0] + jnp.sum(scaled, axis=1, **KEEP), sums[1] + jnp.sum(scaled * x_hat, axis=1, **KEEP)
 
     mean_one, mean_two = lax.fori_loop(0, d_model // wide, gradient, (zero, zero))
     mean_one, mean_two = mean_one / d_model, mean_two / d_model
 
     def part(e):
-        return rows_at(e * width, width, 128)
+        return rows_at(e * width, width, LANES)
 
     def scatter(k):
         to = here.ep_to(k)
@@ -250,29 +260,29 @@
 
     @pl.loop(0, d_model // wide)
     def _(i):
-        cols = rows_at(i * wide, wide, 128)
+        cols = rows_at(i * wide, wide, LANES)
         x_hat = (x_v[:, cols].astype(F32) - mean) * inv_std
         step = inv_std * (grad_h[:, cols] * lnw[:, cols] - mean_one - x_hat * mean_two)
         dx[:, cols] = (dy_v[:, cols].astype(F32) + step).astype(BF16)
 
     for k in range(n_peer):
         scatter(k).wait_recv()
-    c_one[...] = add_up(first, n_ep)
-    second[here.y] = c_one[...]
+    c_one[ALL] = add_up(first, n_ep)
+    second[here.y] = c_one[ALL]
     for k in range(1, grid):
         along('y', c_one, second, s_two, r_two, k).start()
     for k in range(1, grid):
         along('y', c_one, second, s_two, r_two, k).wait_recv()
-    c_two[...] = add_up(second, grid)
-    third[here.z] = c_two[...]
+    c_two[ALL] = add_up(second, grid)
+    third[here.z] = c_two[ALL]
     for k in range(1, grid):
         along('z', c_two, third, s_three, r_three, k).start()
     for k in range(1, grid):
         along('z', c_two, third, s_three, r_three, k).wait_recv()
-    c_three[...] = add_up(third, grid)
+    c_three[ALL] = add_up(third, grid)
     for k in range(n_peer):
         gather(k).start()
-    small[:, part(ep)] = c_three[...]
+    small[:, part(ep)] = c_three[ALL]
     for k in range(n_peer):
         gather(k).wait_recv()
     for k in range(n_peer):
@@ -298,15 +308,15 @@
     peers, ring = dma((n_peer,)), dma((grid,))
     return pl.pallas_call(
         functools.partial(tail_kernel, grid, cap),
-        out_shape=(jax.ShapeDtypeStruct(held.shape, F32), tokens, tokens, jax.ShapeDtypeStruct((24, d_model), F32)),
+        out_shape=(jax.ShapeDtypeStruct(held.shape, F32), tokens, tokens, jax.ShapeDtypeStruct((SMALL, d_model), F32)),
         in_specs=[hbm] * 8 + [on_chip] * 6, out_specs=(hbm, on_chip, on_chip, on_chip), input_output_aliases={0: 0},
         scratch_shapes=[vmem((n_tok, d_model), BF16)] * 3 + [vmem((2 * rows, d_model), BF16)] * 2
-        + [vmem((n_tok, 2 * rows), BF16)] * 2 + [vmem((n_tok, d_model), F32), vmem((24, d_model), F32)]
-        + [vmem((n_ep, 24, width), F32), vmem((grid, 24, width), F32), vmem((grid, 24, width), F32)] + [vmem((24, width), F32)] * 3
+        + [vmem((n_tok, 2 * rows), BF16)] * 2 + [vmem((n_tok, d_model), F32), vmem((SMALL, d_model), F32)]
+        + [vmem((n_ep, SMALL, width), F32), vmem((grid, SMALL, width), F32), vmem((grid, SMALL, width), F32)] + [vmem((SMALL, width), F32)] * 3
         + [dma((7,)), dma((UNITS, 15)), dma((UNITS, 15)), dma((2, n_peer)), dma((2, n_peer)),
            peers, peers, ring, ring, ring, ring, peers, peers],
         compiler_params=pltpu.CompilerParams(collective_id=collective_id, has_side_effects=True, vmem_limit_bytes=50 * 2 ** 20),
-        cost_estimate=pl.CostEstimate(flops=10_000_000_000, bytes_accessed=30_000_000, transcendentals=0),
+        cost_estimate=pl.CostEstimate(flops=10_000_000_000, bytes_accessed=STREAM, transcendentals=0),
         name='tail',
     )(held, o_next, dh_next, tok_x, tok_dy, hidden, o, dh, stats, err_one, err_two, places, lnw, router)
 
@@ -346,7 +356,7 @@
         return here.y if axis == 'y' else here.z
 
     def block(e):
-        return rows_at(e * cap, cap, 16)
+        return rows_at(e * cap, cap, PACK)
 
     weights = [pltpu.make_async_copy(src.at[expert], dst, loc.at[i]) for i, (src, dst) in enumerate(((wg_h, wg), (wu_h, wu), (wd_h, wd)))]
 
@@ -355,8 +365,8 @@
                       send_sem=send.at[k], recv_sem=recv.at[k], device_id=(here.dp, here.ep_to(k)))
 
     def slice_copy(axis, buf, sl, send, recv, src_ep, k):
-        return remote(src_ref=buf.at[block(src_ep), rows_at(here.step(axis, k) * quarter, quarter, 128)],
-                      dst_ref=sl.at[rows_at(spot(axis) * rows + src_ep * cap, cap, 16), :],
+        return remote(src_ref=buf.at[block(src_ep), rows_at(here.step(axis, k) * quarter, quarter, LANES)],
+                      dst_ref=sl.at[rows_at(spot(axis) * rows + src_ep * cap, cap, PACK), :],
                       send_sem=send.at[k], recv_sem=recv.at[k], device_id=here.device(axis, k))
 
     def slices(axis, buf, sl, send, recv, k):
@@ -364,14 +374,14 @@
                       send_sem=send.at[k], recv_sem=recv.at[k], device_id=here.device(axis, k))
 
     half = ff // 2
-    gathers = [(u_all, pl.ds(0, half), 'z', 1, 3), (u_all, pl.ds(half, half), 'z', 3, 1),
-               (da_all, pl.ds(0, ff), 'y', 1, 3), (db_all, pl.ds(0, ff), 'y', 3, 1)]
+    gathers = [(u_all, pl.ds(0, half), 'z', *NEAR), (u_all, pl.ds(half, half), 'z', *FAR),
+               (da_all, pl.ds(0, ff), 'y', *NEAR), (db_all, pl.ds(0, ff), 'y', *FAR)]
 
     def share_t(g, j):
         ref, part, axis, one, two = gathers[g]
         flip = two if j else one
         owner = spot(axis) ^ (one if j == 2 else 0)
-        view = ref.at[part, rows_at(owner * rows, rows, 128)]
+        view = ref.at[part, rows_at(owner * rows, rows, LANES)]
         return remote(src_ref=view, dst_ref=view, send_sem=ga_s.at[g, j], recv_sem=ga_r.at[g, j], device_id=here.flip(axis, flip))
 
     def share_on(units):
@@ -385,8 +395,8 @@
             for j in (1, 2):
                 share_t(g, j).wait_recv()
 
-    reduces = [(0, pl.ds(0, quarter), 'z', 1, 3), (1, pl.ds(0, quarter), 'z', 3, 1),
-               (2, pl.ds(0, quarter // 2), 'y', 1, 3), (2, pl.ds(quarter // 2, quarter // 2), 'y', 3, 1)]
+    reduces = [(0, pl.ds(0, quarter), 'z', *NEAR), (1, pl.ds(0, quarter), 'z', *FAR),
+               (2, pl.ds(0, quarter // 2), 'y', *NEAR), (2, pl.ds(quarter // 2, quarter // 2), 'y', *FAR)]
 
     def part_at(i):
         return rows_at(i * share, share, 8)
@@ -425,39 +435,39 @@
         return outs
 
     def own_slice(axis, buf, sl):
-        sl[rows_at(spot(axis) * rows, rows, 16), :] = buf[:, rows_at(spot(axis) * quarter, quarter, 128)]
+        sl[rows_at(spot(axis) * rows, rows, PACK), :] = buf[:, rows_at(spot(axis) * quarter, quarter, LANES)]
 
     strip = ff // 7
-    u_cols = rows_at(here.z * rows, rows, 128)
-    g_cols = rows_at(here.y * rows, rows, 128)
+    u_cols = rows_at(here.z * rows, rows, LANES)
+    g_cols = rows_at(here.y * rows, rows, LANES)
 
     def forward_pass():
-        a_t[...] = jnp.zeros_like(a_t)
-        b_t[...] = jnp.zeros_like(b_t)
+        a_t[ALL] = jnp.zeros_like(a_t)
+        b_t[ALL] = jnp.zeros_like(b_t)
 
         @pl.loop(0, d_model // chunk)
         def _(i):
-            cols = rows_at(i * chunk, chunk, 128)
-            a_t[...] += lax.dot_general(wg[:, cols], h_recv[:, cols], NT, preferred_element_type=F32)
-            b_t[...] += lax.dot_general(wu[:, cols], h_recv[:, cols], NT, preferred_element_type=F32)
+            cols = rows_at(i * chunk, chunk, LANES)
+            a_t[ALL] += lax.dot_general(wg[:, cols], h_recv[:, cols], NT, preferred_element_type=F32)
+            b_t[ALL] += lax.dot_general(wu[:, cols], h_recv[:, cols], NT, preferred_element_type=F32)
 
         @pl.loop(0, 7)
         def _(i):
-            r = rows_at(i * strip, strip, 16)
+            r = rows_at(i * strip, strip, PACK)
             a = a_t[r, :]
             u_all[r, u_cols] = (a * jax.nn.sigmoid(a) * b_t[r, :]).astype(BF16)
 
     def backward_pass():
-        d_t[...] = jnp.zeros_like(d_t)
+        d_t[ALL] = jnp.zeros_like(d_t)
 
         @pl.loop(0, d_model // chunk)
         def _(i):
-            cols = rows_at(i * chunk, chunk, 128)
-            d_t[...] += lax.dot_general(wd[:, cols], q_recv[:, cols], NT, preferred_element_type=F32)
+            cols = rows_at(i * chunk, chunk, LANES)
+            d_t[ALL] += lax.dot_general(wd[:, cols], q_recv[:, cols], NT, preferred_element_type=F32)
 
         @pl.loop(0, 7)
         def _(i):
-            r = rows_at(i * strip, strip, 16)
+            r = rows_at(i * strip, strip, PACK)
             a, b, du = a_t[r, :], b_t[r, :], d_t[r, :]
             sig = jax.nn.sigmoid(a)
             silu = a * sig
@@ -465,29 +475,42 @@
             db_all[r, g_cols] = (du * silu).astype(BF16)
 
     def untranspose(out, ref, cols):
-        out[...] = lax.dot_general(eye[...], ref[:, cols], NT, preferred_element_type=F32).astype(BF16)
+        out[ALL] = lax.dot_general(eye[ALL], ref[:, cols], NT, preferred_element_type=F32).astype(BF16)
 
     def o_pass():
         @pl.loop(0, d_model // wide)
         def _(i):
-            cols = rows_at(i * wide, wide, 128)
-            o_v[:, cols] = jnp.dot(act[...], wd[:, cols], preferred_element_type=F32).astype(BF16)
+            cols = rows_at(i * wide, wide, LANES)
+            o_v[:, cols] = jnp.dot(act[ALL], wd[:, cols], preferred_element_type=F32).astype(BF16)
 
     def dh_pass():
         @pl.loop(0, d_model // wide)
         def _(i):
-            cols = rows_at(i * wide, wide, 128)
-            dh_v[:, cols] = (jnp.dot(act[...], wg[:, cols], preferred_element_type=F32)
-                             + jnp.dot(act_b[...], wu[:, cols], preferred_element_type=F32)).astype(BF16)
+            cols = rows_at(i * wide, wide, LANES)
+            dh_v[:, cols] = (jnp.dot(act[ALL], wg[:, cols], preferred_element_type=F32)
+                             + jnp.dot(act_b[ALL], wu[:, cols], preferred_element_type=F32)).astype(BF16)
 
     def weight_grad(t, left, right):
         @pl.loop(0, quarter // wide)
         def _(i):
-            cols = rows_at(i * wide, wide, 128)
-            dw[t, :, cols] = jnp.dot(left[...], right[:, cols], preferred_element_type=F32)
+            cols = rows_at(i * wide, wide, LANES)
+            dw[t, :, cols] = jnp.dot(left[ALL], right[:, cols], preferred_element_type=F32)
+
+    def forward_part():
+        weights[0].wait()
+        weights[1].wait()
+        forward_pass()
+        share_t(0, 0).start()
+        share_t(1, 0).start()
+        untranspose(act, u_all, u_cols)
+        weights[2].wait()
+        o_pass()
+        o_out = pltpu.make_async_copy(o_v, o_h, loc.at[3])
+        o_out.start()
+        return o_out
 
     def make_eye():
-        eye[...] = (lax.broadcasted_iota(jnp.int32, (rows, rows), 0)
+        eye[ALL] = (lax.broadcasted_iota(jnp.int32, (rows, rows), 0)
                     == lax.broadcasted_iota(jnp.int32, (rows, rows), 1)).astype(F32).astype(BF16)
 
     if first:
@@ -495,14 +518,14 @@
                   for i, (src, dst) in enumerate(zip(sel_in, (sel_h, hidden, sel_q, grad_one, grad_two, sel_h_next, sel_q_next)))]
         for c in inputs:
             c.start()
-        here.barrier()
+        signals = here.arrive()
         for c in inputs:
             c.wait()
 
         def gather(sel, source, out, e):
             @pl.loop(0, d_model // chunk)
             def _(i):
-                cols = rows_at(i * chunk, chunk, 128)
+                cols = rows_at(i * chunk, chunk, LANES)
                 total = jnp.dot(sel[block(e), :n_tok], source[0][:, cols], preferred_element_type=F32)
                 for j in range(1, len(source)):
                     total += jnp.dot(sel[block(e), j * n_tok:(j + 1) * n_tok], source[j][:, cols], preferred_element_type=F32)
@@ -517,23 +540,48 @@
             _, _, out, recv_buf, send, recv = what
             return x_copy(out, recv_buf, send, recv, k)
 
-        pending = []
-
-        def dispatch(what, k):
-            gather(what[0], what[1], what[2], here.ep_to(k))
-            pending.append(copy_of(what, k))
-            if len(pending) > 1:
-                pending.pop(0).start()
-
-        for k in range(n_peer):
-            for what in now:
-                dispatch(what, k)
+        others = range(1, n_peer)
+        pairs = list(zip(others[::2], others[1::2]))
+        steps = [(group, i, ks) for group, order in ((now, (0, 1)), (later, (1, 0))) for i in order for ks in pairs]
+        ahead = 2 * len(pairs)
+
+        def gather_step(n):
+            if n < len(steps):
+                group, i, ks = steps[n]
+                for k in ks:
+                    gather(group[i][0], group[i][1], group[i][2], here.ep_to(k))
+
+        def send_step(n):
+            if n < len(steps):
+                group, i, ks = steps[n]
+                for k in ks:
+                    copy_of(group[i], k).start()
+
+        def sent_step(n):
+            if n < len(steps):
+                group, i, ks = steps[n]
+                for k in ks:
+                    copy_of(group[i], k).wait_send()
+
+        def partner(group):
+            for what in group:
+                gather(what[0], what[1], what[2], here.ep_to(0))
+
+        def partner_send(group):
+            for what in group:
+                copy_of(what, 0).start()
+
+        gather_step(0)
+        here.barrier(signals)
+        send_step(0)
+        gather_step(1)
+        send_step(1)
+        partner(now)
+        partner_send(now)
+        for c in weights:
+            c.start()
         for what in now:
             gather(what[0], what[1], what[3], ep)
-        while pending:
-            pending.pop(0).start()
-        for c in weights:
-            c.start()
         make_eye()
 
         spread = (('y', h_recv, h_sl, hs_s, hs_r), ('z', q_recv, q_sl, qs_s, qs_r))
@@ -544,44 +592,58 @@
                 for k in range(1, grid):
                     slice_copy(axis, buf, sl, send, recv, ep, k).start()
 
-        def forward(group, spread, p):
-            for what, (axis, buf, sl, send, recv) in zip(group, spread):
-                copy_of(what, p).wait_recv()
-                for k in range(1, grid):
-                    slice_copy(axis, buf, sl, send, recv, here.ep_from(p), k).start()
+        def forward(group, spread, i, p):
+            axis, buf, sl, send, recv = spread[i]
+            copy_of(group[i], p).wait_recv()
+            for k in range(1, grid):
+                slice_copy(axis, buf, sl, send, recv, here.ep_from(p), k).start()
+
+        def forward_step(n):
+            if n < len(steps):
+                group, i, ks = steps[n]
+                for k in ks:
+                    forward(group, spread if group is now else spread_next, i, k)
 
         forward_own(spread, (h_recv, q_recv))
+        for i in range(2):
+            forward(now, spread, i, 0)
         for what in later:
             gather(what[0], what[1], what[2], ep)
         own_next = [pltpu.make_async_copy(what[2].at[block(ep), :], what[3].at[block(ep), :], lin.at[7 + i]) for i, what in enumerate(later)]
-        for p in range(n_peer):
-            forward(now, spread, p)
-            for what in later:
-                dispatch(what, p)
-            if p == min(3, n_peer - 1):
-                while pending:
-                    pending.pop(0).start()
+        partner(later)
+        partner_send(later)
+        middle, last = max(len(pairs) - 1, 0), max(ahead - 1, 0)
+        for n in range(last + 1):
+            gather_step(n + 2)
+            sent_step(n)
+            send_step(n + 2)
+            forward_step(n)
+            if n == middle:
+                own_slice('y', h_recv, h_sl)
+                copy_of(now[0], 0).wait_send()
+                o_out = forward_part()
+            if n == min(middle + 2, last):
+                share_on((0, 1))
+            if n >= 2:
+                gather_step(n + ahead)
+            if n == min(1, last):
                 forward_own(spread_next, (h_send_next, q_send_next))
-                forward(later, spread_next, 0)
-        while pending:
-            pending.pop(0).start()
+                for i in range(2):
+                    forward(later, spread_next, i, 0)
+        send_step(ahead + 2)
+        send_step(ahead + 3)
         for c in own_next:
             c.start()
-        own_slice('y', h_recv, h_sl)
         own_slice('z', q_recv, q_sl)
-        for c in weights:
-            c.wait()
-        for k in range(n_peer):
-            for what in now:
-                copy_of(what, k).wait_send()
+        copy_of(now[1], 0).wait_send()
     else:
-        loads = [pltpu.make_async_copy(h_next, h_recv, lin.at[0]), weights[0], weights[1],
-                 pltpu.make_async_copy(q_next, q_recv, lin.at[1]), weights[2]]
+        load_h, load_q = [pltpu.make_async_copy(src, dst, lin.at[2 + i * grid]) for i, (src, dst) in enumerate(((h_next, h_recv), (q_next, q_recv)))]
+        load_slices = []
         for i, (axis, src, dst) in enumerate((('z', qsl_next, q_sl), ('y', hsl_next, h_sl))):
             for k in range(1, grid):
-                part = rows_at(here.step(axis, k) * rows, rows, 16)
-                loads.append(pltpu.make_async_copy(src.at[part, :], dst.at[part, :], lin.at[2 + i * grid + k]))
-        for c in loads:
+                part = rows_at(here.step(axis, k) * rows, rows, PACK)
+                load_slices.append(pltpu.make_async_copy(src.at[part, :], dst.at[part, :], lin.at[2 + i * grid + k]))
+        for c in [load_h] + weights + [load_q] + load_slices:
             c.start()
         here.barrier()
         back = list(zip(carry, carry_out))
@@ -606,26 +668,23 @@
         for j in range(len(carry)):
             send_back(j)
         make_eye()
-        for c in loads:
-            c.wait()
-        own_unit.start()
+        load_h.wait()
+        o_out = forward_part()
+        spread_unit.receive(0)
+        spread_unit.send(1)
+        load_q.wait()
         own_slice('y', h_recv, h_sl)
         own_slice('z', q_recv, q_sl)
-
-    forward_pass()
-    share_t(0, 0).start()
-    share_t(1, 0).start()
-    if not first:
-        spread_unit.receive(0)
-        spread_unit.send(1)
+        own_unit.start()
+
     backward_pass()
     share_t(2, 0).start()
     share_t(3, 0).start()
-    untranspose(act, u_all, u_cols)
-    share_on((0, 1))
-    o_pass()
-    o_out = pltpu.make_async_copy(o_v, o_h, loc.at[3])
-    o_out.start()
+    if first:
+        sent_step(ahead)
+        send_step(ahead + 4)
+    else:
+        share_on((0, 1))
     untranspose(act, da_all, g_cols)
     untranspose(act_b, db_all, g_cols)
     share_on((2, 3))
@@ -633,11 +692,17 @@
     dh_out = pltpu.make_async_copy(dh_v, dh_h, loc.at[4])
     dh_out.start()
     if first:
+        sent_step(ahead + 1)
+        send_step(ahead + 5)
+        forward_step(ahead)
+        forward_step(ahead + 1)
         for k in range(1, grid):
             slices('z', q_recv, q_sl, qs_s, qs_r, k).wait_recv()
     else:
         spread_unit.receive(1)
         spread_unit.send(2, (0,))
+        for c in load_slices:
+            c.wait()
     share_done((0, 1))
     weight_grad(2, u_all, q_sl)
     reduce_start((2, 3))
@@ -651,36 +716,34 @@
     weight_grad(1, db_all, h_sl)
     reduce_start((1,))
     if first:
-        for p in range(1, (n_peer + 1) // 2):
-            forward(later, spread_next, p)
+        forward_step(ahead + 2)
+        forward_step(ahead + 3)
     else:
         spread_unit.send(2, (1,))
     reduce_on((2, 3))
     if first:
-        for p in range((n_peer + 1) // 2, n_peer - 2):
-            forward(later, spread_next, p)
+        forward_step(ahead + 4)
     reduce_on((0, 1))
-    if not first:
+    if first:
+        forward_step(ahead + 5)
+    else:
         spread_unit.send(2, (2, 3))
-    if first:
-        for p in range(max((n_peer + 1) // 2, n_peer - 2), n_peer):
-            forward(later, spread_next, p)
     ends = reduce_end(2) + reduce_end(0) + reduce_end(1)
 
     for j in range(3):
         for g in range(4):
             share_t(g, j).wait_send()
-        for r in range(4):
-            reduce_copy(r, j).wait_send()
+            reduce_copy(g, j).wait_send()
     if first:
         for k in range(1, grid):
             for axis, buf, sl, send, recv in spread:
                 slices(axis, buf, sl, send, recv, k).wait_send()
             for axis, buf, sl, send, recv in spread_next:
                 slices(axis, buf, sl, send, recv, k).wait()
-        for k in range(n_peer):
-            for what in later:
-                copy_of(what, k).wait_send()
+        for what in later:
+            copy_of(what, 0).wait_send()
+        for n in range(2, 6):
+            sent_step(ahead + n)
         for c in own_next:
             c.wait()
     else:
@@ -735,7 +798,7 @@
         functools.partial(expert_kernel, (expert, grid, chunk, cap, first)),
         out_shape=tuple(outs), in_specs=[hbm] * len(operands), out_specs=(hbm,) * len(outs), scratch_shapes=scratch,
         compiler_params=pltpu.CompilerParams(collective_id=expert, has_side_effects=True, vmem_limit_bytes=63 * 2 ** 20),
-        cost_estimate=pl.CostEstimate(flops=2 * rows * d_model * ff * 9, bytes_accessed=30_000_000, transcendentals=0),
+        cost_estimate=pl.CostEstimate(flops=2 * rows * d_model * ff * 9, bytes_accessed=STREAM, transcendentals=0),
     )(*operands)
 
 
@@ -743,7 +806,7 @@
     n_pass = (len(refs) - 3) // 2 if len(refs) > 6 else 0
     outs = refs[-3 - n_pass:][:3]
     for j in range(n_pass):
-        refs[-n_pass + j][...] = refs[j][...]
+        refs[-n_pass + j][ALL] = refs[j][ALL]
     grid, unit = gate.shape[1], gate.shape[-1]
     for c in range(grid):
         for i in range(UNITS):
@@ -808,12 +871,12 @@
 
         def lanes(columns):
             flat = jnp.concatenate(columns, axis=1)
-            return jnp.pad(flat, ((0, 0), (0, 128 - flat.shape[1])))
+            return jnp.pad(flat, ((0, 0), (0, LANES - flat.shape[1])))
 
         stats = lanes([gate_one[:, None], gate_two[:, None], mean, inv_std])
         err_one, err_two = lanes([pick_one - prob_one]), lanes([pick_two - prob_two])
         places = lanes([pos_one[:, None], pos_two[:, None]])
-        router_t = jnp.pad(router.T, ((0, 128 - n_exp), (0, 0)))
+        router_t = jnp.pad(router.T, ((0, LANES - n_exp), (0, 0)))
         cuts = [slice(e * per, (e + 1) * per) for e in range(local_exp)]
         sels = []
         for e in range(local_exp):

time: 515 us -> 494 us (0.959)
  Pallas kernels: 448 us -> 427 us
    pallas_call x2, Pallas kernels: 289 us -> 265 us  [expert_call(): pl.pallas_call(functools.partial(expert_kernel, (expert, grid, chunk, cap...]
  transfers between devices with their start and end apart: 1 -> 1, of which waited for: 1 -> 1; matrix products, arithmetic and copies ran while one was open for 0% -> 0% of each run, Pallas kernels for 28% -> 29%
where the time goes in v2:
time: 494 us
  Pallas kernels  427 us (86%)
  waiting for transfers between devices  35.2 us (7%)
  between operations  14.4 us (3%)
  other arithmetic  11.7 us (2%)
    pallas_call x2, Pallas kernels, expert_call(): pl.pallas_call(functools.partial(expert_kernel, (expert, grid, chunk, cap...  265 us
    pallas_call x1, Pallas kernels, tail_call(): pl.pallas_call(functools.partial(tail_kernel, grid, cap), out_shape=(jax....  128 us
    all_gather x1, waiting for transfers between devices, local_step(): gathered_next = lax.all_gather(share, 'dp')  35.2 us
    pallas_call x2, Pallas kernels, assemble(): pl.pallas_call(assemble_kernel, grid=(grid, cut), out_shape=(whole,) * 3...  33.8 us
  transfers between devices with their start and end apart: 1, of which 1 were waited for; matrix products, arithmetic and copies ran while one was open for 0% of the time, Pallas kernels for 29%

profile of v2, /device:TPU:1, one launch (start us, length us, event | category | flops | bytes accessed | tf_op | source)
XLA Modules:
  0.0 493.8 jit_solution(7561624963532218966)
XLA Ops:
  7.2 0.0 copy-start.1
  7.3 0.0 all-gather.3.cloned.1.call-start
  7.3 2.1 convert_reduce_fusion
  9.4 2.3 fusion.2
  11.8 0.0 copy-done.9
  11.8 0.0 copy-done.6
  11.8 0.1 copy.37
  12.0 0.9 or_convert_fusion
  12.9 1.1 compare_convert_fusion
  14.0 1.0 fusion.5.refs_1_.refs_5_
  15.0 0.0 copy-start.3
  15.0 1.3 copy-done.3
  16.3 0.0 copy-done.4
  16.3 0.8 fusion.14
  17.1 0.3 fusion.21
  17.4 0.3 fusion.13
  17.7 0.2 convert_subtract_fusion.1
  17.9 0.2 select_reduce_fusion
  18.1 3.2 fusion.7
  21.3 158.6 %shard_map.188 = (bf16[384,4096]{1,0:T(8,128)(2,1)}, bf16[384,4096]{1,0:T(8,128)(2,1)}, f32[4,3,112,256]{3,2,1,0:T(8,128)}, bf16[384,4096]{1,0:T(8,128)(2,1)}, b...) custom-call(bf16[384,256]{1,0:T(8,128)(2,1)} %get-tuple-element.74.refs_0_, ...), custom_call_target="tpu_custom_call" | custom-call | flops 12683575296 | bytes 30000000 | tf_op jit(solution)/shard_map/pallas_call | solution.py:797
  180.0 106.5 %shard_map.189 = (bf16[384,4096]{1,0:T(8,128)(2,1)}, bf16[384,4096]{1,0:T(8,128)(2,1)}, f32[4,3,112,256]{3,2,1,0:T(8,128)}, bf16[384,4096]{1,0:T(8,128)(2,1)}, b...) custom-call(bf16[384,4096]{1,0:T(8,128)(2,1)} %get-tuple-element.33.refs_0_, ...), custom_call_target="tpu_custom_call" | custom-call | flops 12683575296 | bytes 30000000 | tf_op jit(solution)/shard_map/pallas_call | solution.py:797
  286.5 0.0 all-gather.3.cloned.1.call-update
  286.5 0.1 copy.41
  286.7 0.1 copy.40
  286.9 0.1 pad.23.refs_13_
  287.0 128.0 %tail.1 = (f32[16,4,3,112,256]{4,3,2,1,0:T(8,128)}, bf16[256,4096]{1,0:T(8,128)(2,1)S(1)}, bf16[256,4096]{1,0:T(8,128)(2,1)}, f32[24,4096]{1,0:T(8,128)S(1)}) custom-call(f32[16,4,3,112,256]{4,3,2,1,0:T(8,128)} %get-tuple-element.40.refs_0_, bf16[384,4096]{1,0:T(8,128)(2,1)} %get-tuple-element.41.refs_1_, ...), custom_call_target="tpu_custom_call", output_to_operand_aliasing={{0}: (0, {})} | custom-call | flops 10000000000 | bytes 30000000 | tf_op jit(solution)/shard_map/tail/pallas_call | solution.py:309
  415.0 1.6 copy-done
  416.6 17.4 %shard_map.190 = (f32[2,448,4096]{2,1,0:T(8,128)}, f32[2,448,4096]{2,1,0:T(8,128)}, f32[2,448,4096]{2,1,0:T(8,128)}, bf16[256,4096]{1,0:T(8,128)(2,1)}, bf16[256,4096]{1,0:T(8,128)(2,1)}) custom-call(f32[4,4,4,3,112,256]{5,4,3,2,1,0:T(8,128)} %bitcast.21, f32[4,4,4,3,112,256]{5,4,3,2,1,0:T(8,128)} %bitcast.22, f32[4,4,4,3,112,256]{5,4,3,2,1,0:T(8,128)} %bitcast.23, ...), custom_call_target="tpu_custom_call" | custom-call | flops 1000000 | bytes 44000000 | tf_op jit(solution)/shard_map/pallas_call | solution.py:829
  434.0 0.6 fusion.23
  434.6 0.7 slice_bitcast_fusion
  435.3 35.2 %all-gather.3.cloned.1.call-done = f32[64,3,112,256]{3,2,1,0:T(8,128)} async-done(((f32[4,3,112,256]{3,2,1,0:T(8,128)}), f32[64,3,112,256]{3,2,1,0:T(8,128)}) %all-gather.3.cloned.1.call-update) | async-done | bytes 22020112 | tf_op jit(solution)/shard_map/all_gather | solution.py:888
  470.5 16.4 %shard_map.191 = (f32[2,448,4096]{2,1,0:T(8,128)}, f32[2,448,4096]{2,1,0:T(8,128)}, f32[2,448,4096]{2,1,0:T(8,128)}) custom-call(f32[4,4,4,3,112,256]{5,4,3,2,1,0:T(8,128)} %bitcast.24, f32[4,4,4,3,112,256]{5,4,3,2,1,0:T(8,128)} %bitcast.25, f32[4,4,4,3,112,256]{5,4,3,2,1,0:T(8,128)} %bitcast.26, ...), custom_call_target="tpu_custom_call", output_to_operand_aliasing={{0}: (3, {}), {1}: (4, {}), {2}: (5, {})} | custom-call | flops 1000000 | bytes 44000000 | tf_op jit(solution)/shard_map/pallas_call | solution.py:829
  (33 shorter events, 0.2 us)
Async XLA Ops:
  7.2 6.8 %copy-start.1 = (bf16[256,4096]{1,0:T(8,128)(2,1)S(1)}, bf16[256,4096]{1,0:T(8,128)(2,1)}, u32[]{:S(2)}) copy-start(bf16[256,4096]{1,0:T(8,128)(2,1)} %refs_3_.1) | copy-start | bytes 6291460
  7.2 4.6 copy-start.8
  7.2 4.6 copy-start.9
  7.2 4.6 copy-start.6
  7.2 4.7 copy-start.5
  7.2 4.7 copy-start.7
  7.2 4.7 copy-start.10
  7.2 4.7 copy-start.11
  7.3 463.3 %all-gather.3.cloned.1.call-start = ((), (), s32[]{:S(2)}) async-start(), calls=%async_computation | async-start | bytes 23396352 | tf_op jit(solution)/shard_map/all_gather | solution.py:888
  9.4 7.0 %copy-start.4 = (bf16[4096,16]{0,1:T(8,128)(2,1)S(1)}, bf16[4096,16]{0,1:T(8,128)(2,1)}, u32[]{:S(2)}) copy-start(bf16[4096,16]{0,1:T(8,128)(2,1)} %param.22) | copy-start | bytes 393220
  14.0 4.1 copy-start.2
  15.0 1.3 copy-start.3
  415.0 1.6 copy-start
Sparse Core Ops, SparseCore 0:
  286.6 183.8 all-gather.2

commit v3 on v2

--- a/solution.py
+++ b/solution.py
@@ -374,8 +374,8 @@
                       send_sem=send.at[k], recv_sem=recv.at[k], device_id=here.device(axis, k))
 
     half = ff // 2
-    gathers = [(u_all, pl.ds(0, half), 'z', *NEAR), (u_all, pl.ds(half, half), 'z', *FAR),
-               (da_all, pl.ds(0, ff), 'y', *NEAR), (db_all, pl.ds(0, ff), 'y', *FAR)]
+    halves = ((pl.ds(0, half), NEAR), (pl.ds(half, half), FAR))
+    gathers = [(ref, part, axis, *order) for ref, axis in ((u_all, 'z'), (da_all, 'y'), (db_all, 'y')) for part, order in halves]
 
     def share_t(g, j):
         ref, part, axis, one, two = gathers[g]
@@ -384,19 +384,24 @@
         view = ref.at[part, rows_at(owner * rows, rows, LANES)]
         return remote(src_ref=view, dst_ref=view, send_sem=ga_s.at[g, j], recv_sem=ga_r.at[g, j], device_id=here.flip(axis, flip))
 
-    def share_on(units):
-        for g in units:
+    def share_start(t):
+        for g in (2 * t, 2 * t + 1):
+            share_t(g, 0).start()
+
+    def share_on(t):
+        for g in (2 * t, 2 * t + 1):
             share_t(g, 0).wait_recv()
             for j in (1, 2):
                 share_t(g, j).start()
 
-    def share_done(units):
-        for g in units:
+    def share_done(t):
+        for g in (2 * t, 2 * t + 1):
             for j in (1, 2):
                 share_t(g, j).wait_recv()
 
-    reduces = [(0, pl.ds(0, quarter), 'z', *NEAR), (1, pl.ds(0, quarter), 'z', *FAR),
-               (2, pl.ds(0, quarter // 2), 'y', *NEAR), (2, pl.ds(quarter // 2, quarter // 2), 'y', *FAR)]
+    wing = quarter // 2
+    wings = ((pl.ds(0, wing), NEAR), (pl.ds(wing, wing), FAR))
+    reduces = [(t, cols, axis, *order) for t, axis in enumerate('zzy') for cols, order in wings]
 
     def part_at(i):
         return rows_at(i * share, share, 8)
@@ -408,14 +413,14 @@
         return remote(src_ref=dw.at[t, part_at(chunk_at), cols], dst_ref=rsb.at[t, j, :, cols],
                       send_sem=rs_s.at[r, j], recv_sem=rs_r.at[r, j], device_id=here.flip(axis, flip))
 
-    def reduce_start(units):
-        for r in units:
+    def reduce_start(t):
+        for r in (2 * t, 2 * t + 1):
             for j in (0, 1):
                 reduce_copy(r, j).start()
 
-    def reduce_on(units):
-        for r in units:
-            t, cols, axis, _, two = reduces[r]
+    def reduce_on(t):
+        for r in (2 * t, 2 * t + 1):
+            _, cols, axis, _, two = reduces[r]
             reduce_copy(r, 0).wait_recv()
             reduce_copy(r, 1).wait_recv()
             on = part_at(spot(axis) ^ two)
@@ -423,9 +428,8 @@
             reduce_copy(r, 2).start()
 
     def reduce_end(t):
-        units = [r for r in range(len(reduces)) if reduces[r][0] == t]
-        axis = reduces[units[0]][2]
-        for r in units:
+        axis = 'zzy'[t]
+        for r in (2 * t, 2 * t + 1):
             reduce_copy(r, 2).wait_recv()
         rsb[t, 0] = dw[t, part_at(spot(axis)), :] + rsb[t, 0] + rsb[t, 2]
         unit = quarter // UNITS
@@ -500,8 +504,7 @@
         weights[0].wait()
         weights[1].wait()
         forward_pass()
-        share_t(0, 0).start()
-        share_t(1, 0).start()
+        share_start(0)
         untranspose(act, u_all, u_cols)
         weights[2].wait()
         o_pass()
@@ -623,7 +626,7 @@
                 copy_of(now[0], 0).wait_send()
                 o_out = forward_part()
             if n == min(middle + 2, last):
-                share_on((0, 1))
+                share_on(0)
             if n >= 2:
                 gather_step(n + ahead)
             if n == min(1, last):
@@ -650,6 +653,7 @@
         spread_unit = Spread(here, done_h, all_h, sp_s, sp_r)
         own_unit = pltpu.make_async_copy(done_h, all_h.at[here.dp], lin.at[1])
         spread_unit.send(0)
+        spread_unit.send(1, (0,))
 
         def back_copy(j, k):
             src, dst = back[j]
@@ -670,24 +674,26 @@
         make_eye()
         load_h.wait()
         o_out = forward_part()
-        spread_unit.receive(0)
-        spread_unit.send(1)
         load_q.wait()
         own_slice('y', h_recv, h_sl)
         own_slice('z', q_recv, q_sl)
         own_unit.start()
 
     backward_pass()
-    share_t(2, 0).start()
-    share_t(3, 0).start()
+    share_start(1)
+    share_start(2)
     if first:
         sent_step(ahead)
         send_step(ahead + 4)
     else:
-        share_on((0, 1))
+        share_on(0)
     untranspose(act, da_all, g_cols)
     untranspose(act_b, db_all, g_cols)
-    share_on((2, 3))
+    share_on(1)
+    share_on(2)
+    if not first:
+        spread_unit.receive(0)
+        spread_unit.send(1, (1,))
     dh_pass()
     dh_out = pltpu.make_async_copy(dh_v, dh_h, loc.at[4])
     dh_out.start()
@@ -695,43 +701,43 @@
         sent_step(ahead + 1)
         send_step(ahead + 5)
         forward_step(ahead)
-        forward_step(ahead + 1)
         for k in range(1, grid):
             slices('z', q_recv, q_sl, qs_s, qs_r, k).wait_recv()
+            slices('y', h_recv, h_sl, hs_s, hs_r, k).wait_recv()
+    else:
+        for c in load_slices:
+            c.wait()
+    share_done(1)
+    weight_grad(0, da_all, h_sl)
+    reduce_start(0)
+    if not first:
+        spread_unit.send(2, (0,))
+    share_done(0)
+    weight_grad(2, u_all, q_sl)
+    share_done(2)
+    weight_grad(1, db_all, h_sl)
+    reduce_start(1)
+    reduce_start(2)
+    if first:
+        forward_step(ahead + 1)
     else:
         spread_unit.receive(1)
-        spread_unit.send(2, (0,))
-        for c in load_slices:
-            c.wait()
-    share_done((0, 1))
-    weight_grad(2, u_all, q_sl)
-    reduce_start((2, 3))
+    reduce_on(0)
+    if not first:
+        spread_unit.send(2, (1,))
+    reduce_on(1)
+    reduce_on(2)
     if first:
-        for k in range(1, grid):
-            slices('y', h_recv, h_sl, hs_s, hs_r, k).wait_recv()
-    share_done((2,))
-    weight_grad(0, da_all, h_sl)
-    reduce_start((0,))
-    share_done((3,))
-    weight_grad(1, db_all, h_sl)
-    reduce_start((1,))
-    if first:
-        forward_step(ahead + 2)
-        forward_step(ahead + 3)
+        for n in range(2, 5):
+            forward_step(ahead + n)
     else:
-        spread_unit.send(2, (1,))
-    reduce_on((2, 3))
-    if first:
-        forward_step(ahead + 4)
-    reduce_on((0, 1))
+        spread_unit.send(2, (2, 3))
+    ends = reduce_end(0) + reduce_end(1) + reduce_end(2)
     if first:
         forward_step(ahead + 5)
-    else:
-        spread_unit.send(2, (2, 3))
-    ends = reduce_end(2) + reduce_end(0) + reduce_end(1)
 
     for j in range(3):
-        for g in range(4):
+        for g in range(len(gathers)):
             share_t(g, j).wait_send()
             reduce_copy(g, j).wait_send()
     if first:
@@ -778,7 +784,7 @@
         vmem(slice_block, BF16), vmem(slice_block, BF16),
         vmem((3, ff, quarter), F32), vmem((3, 3, share, quarter), F32),
         vmem((rows, ff), BF16), vmem((rows, ff), BF16), vmem((rows, rows), BF16), dma((5 + 3 * UNITS,)),
-    ] + [dma((grid,))] * 4 + [dma((4, 3))] * 4
+    ] + [dma((grid,))] * 4 + [dma((6, 3))] * 4
     out = lambda shape, dtype=BF16: jax.ShapeDtypeStruct(shape, dtype)
     share_block = (UNITS, 3, share, quarter // UNITS)
     outs = [out(row_block), out(row_block), out(share_block, F32)]

time: 494 us -> 487 us (0.986)
  Pallas kernels: 427 us -> 419 us
    pallas_call x2, Pallas kernels: 265 us -> 260 us  [expert_call(): pl.pallas_call(functools.partial(expert_kernel, (expert, grid, chunk, cap...]
where the time goes in v3:
time: 487 us; the launch traced here: 486 us
  Pallas kernels  419 us (86%)
  waiting for transfers between devices  35.8 us (7%)
  between operations  14.4 us (3%)
  other arithmetic  11.7 us (2%)
    pallas_call x2, Pallas kernels, expert_call(): pl.pallas_call(functools.partial(expert_kernel, (expert, grid, chunk, cap...  260 us
    pallas_call x1, Pallas kernels, tail_call(): pl.pallas_call(functools.partial(tail_kernel, grid, cap), out_shape=(jax....  125 us
    all_gather x1, waiting for transfers between devices, local_step(): gathered_next = lax.all_gather(share, 'dp')  35.7 us
    pallas_call x2, Pallas kernels, assemble(): pl.pallas_call(assemble_kernel, grid=(grid, cut), out_shape=(whole,) * 3...  33.8 us
  transfers between devices with their start and end apart: 1, of which 1 were waited for; matrix products, arithmetic and copies ran while one was open for 0% of the time, Pallas kernels for 29%

profile of v3, /device:TPU:1, one launch (start us, length us, event | category | flops | bytes accessed | tf_op | source)
XLA Modules:
  0.0 486.3 jit_solution(734181219561332696)
XLA Ops:
  7.2 0.0 copy-start.1
  7.3 0.0 all-gather.3.cloned.1.call-start
  7.3 2.1 convert_reduce_fusion
  9.4 2.3 fusion.2
  11.8 0.0 copy-done.9
  11.8 0.0 copy-done.6
  11.8 0.1 copy.37
  12.0 0.9 or_convert_fusion
  12.9 1.1 compare_convert_fusion
  14.0 1.0 fusion.5.refs_1_.refs_5_
  15.0 0.0 copy-start.3
  15.0 1.3 copy-done.3
  16.3 0.0 copy-done.4
  16.3 0.8 fusion.14
  17.1 0.3 fusion.21
  17.4 0.3 fusion.13
  17.7 0.2 convert_subtract_fusion.1
  17.9 0.2 select_reduce_fusion
  18.1 3.2 fusion.7
  21.3 160.5 %shard_map.188 = (bf16[384,4096]{1,0:T(8,128)(2,1)}, bf16[384,4096]{1,0:T(8,128)(2,1)}, f32[4,3,112,256]{3,2,1,0:T(8,128)}, bf16[384,4096]{1,0:T(8,128)(2,1)}, b...) custom-call(bf16[384,256]{1,0:T(8,128)(2,1)} %get-tuple-element.74.refs_0_, ...), custom_call_target="tpu_custom_call" | custom-call | flops 12683575296 | bytes 30000000 | tf_op jit(solution)/shard_map/pallas_call | solution.py:803
  181.9 99.4 %shard_map.189 = (bf16[384,4096]{1,0:T(8,128)(2,1)}, bf16[384,4096]{1,0:T(8,128)(2,1)}, f32[4,3,112,256]{3,2,1,0:T(8,128)}, bf16[384,4096]{1,0:T(8,128)(2,1)}, b...) custom-call(bf16[384,4096]{1,0:T(8,128)(2,1)} %get-tuple-element.33.refs_0_, ...), custom_call_target="tpu_custom_call" | custom-call | flops 12683575296 | bytes 30000000 | tf_op jit(solution)/shard_map/pallas_call | solution.py:803
  281.3 0.0 all-gather.3.cloned.1.call-update
  281.3 0.1 copy.41
  281.5 0.1 copy.40
  281.7 0.1 pad.23.refs_13_
  281.8 125.1 %tail.1 = (f32[16,4,3,112,256]{4,3,2,1,0:T(8,128)}, bf16[256,4096]{1,0:T(8,128)(2,1)S(1)}, bf16[256,4096]{1,0:T(8,128)(2,1)}, f32[24,4096]{1,0:T(8,128)S(1)}) custom-call(f32[16,4,3,112,256]{4,3,2,1,0:T(8,128)} %get-tuple-element.40.refs_0_, bf16[384,4096]{1,0:T(8,128)(2,1)} %get-tuple-element.41.refs_1_, ...), custom_call_target="tpu_custom_call", output_to_operand_aliasing={{0}: (0, {})} | custom-call | flops 10000000000 | bytes 30000000 | tf_op jit(solution)/shard_map/tail/pallas_call | solution.py:309
  406.9 1.6 copy-done
  408.6 17.4 %shard_map.190 = (f32[2,448,4096]{2,1,0:T(8,128)}, f32[2,448,4096]{2,1,0:T(8,128)}, f32[2,448,4096]{2,1,0:T(8,128)}, bf16[256,4096]{1,0:T(8,128)(2,1)}, bf16[256,4096]{1,0:T(8,128)(2,1)}) custom-call(f32[4,4,4,3,112,256]{5,4,3,2,1,0:T(8,128)} %bitcast.21, f32[4,4,4,3,112,256]{5,4,3,2,1,0:T(8,128)} %bitcast.22, f32[4,4,4,3,112,256]{5,4,3,2,1,0:T(8,128)} %bitcast.23, ...), custom_call_target="tpu_custom_call" | custom-call | flops 1000000 | bytes 44000000 | tf_op jit(solution)/shard_map/pallas_call | solution.py:835
  425.9 0.6 fusion.23
  426.6 0.7 slice_bitcast_fusion
  427.3 35.7 %all-gather.3.cloned.1.call-done = f32[64,3,112,256]{3,2,1,0:T(8,128)} async-done(((f32[4,3,112,256]{3,2,1,0:T(8,128)}), f32[64,3,112,256]{3,2,1,0:T(8,128)}) %all-gather.3.cloned.1.call-update) | async-done | bytes 22020112 | tf_op jit(solution)/shard_map/all_gather | solution.py:894
  463.0 16.4 %shard_map.191 = (f32[2,448,4096]{2,1,0:T(8,128)}, f32[2,448,4096]{2,1,0:T(8,128)}, f32[2,448,4096]{2,1,0:T(8,128)}) custom-call(f32[4,4,4,3,112,256]{5,4,3,2,1,0:T(8,128)} %bitcast.24, f32[4,4,4,3,112,256]{5,4,3,2,1,0:T(8,128)} %bitcast.25, f32[4,4,4,3,112,256]{5,4,3,2,1,0:T(8,128)} %bitcast.26, ...), custom_call_target="tpu_custom_call", output_to_operand_aliasing={{0}: (3, {}), {1}: (4, {}), {2}: (5, {})} | custom-call | flops 1000000 | bytes 44000000 | tf_op jit(solution)/shard_map/pallas_call | solution.py:835
  (33 shorter events, 0.2 us)
Async XLA Ops:
  7.2 6.8 %copy-start.1 = (bf16[256,4096]{1,0:T(8,128)(2,1)S(1)}, bf16[256,4096]{1,0:T(8,128)(2,1)}, u32[]{:S(2)}) copy-start(bf16[256,4096]{1,0:T(8,128)(2,1)} %refs_3_.1) | copy-start | bytes 6291460
  7.2 4.6 copy-start.8
  7.2 4.6 copy-start.9
  7.2 4.6 copy-start.6
  7.2 4.7 copy-start.5
  7.2 4.7 copy-start.7
  7.2 4.7 copy-start.10
  7.2 4.7 copy-start.11
  7.3 455.8 %all-gather.3.cloned.1.call-start = ((), (), s32[]{:S(2)}) async-start(), calls=%async_computation | async-start | bytes 23396352 | tf_op jit(solution)/shard_map/all_gather | solution.py:894
  9.4 7.0 %copy-start.4 = (bf16[4096,16]{0,1:T(8,128)(2,1)S(1)}, bf16[4096,16]{0,1:T(8,128)(2,1)}, u32[]{:S(2)}) copy-start(bf16[4096,16]{0,1:T(8,128)(2,1)} %param.22) | copy-start | bytes 393220
  14.0 4.1 copy-start.2
  15.0 1.3 copy-start.3
  406.9 1.6 copy-start
Sparse Core Ops, SparseCore 0:
  281.5 181.5 all-gather.2

commit v4 on v3

--- a/solution.py
+++ b/solution.py
@@ -14,6 +14,7 @@
 NEAR, FAR = (1, 3), (3, 1)
 LANES = 128
 PACK = 16
+STRIPS = 7
 SMALL = 24
 STREAM = 30_000_000
 KEEP = {'keepdims': True}
@@ -22,22 +23,6 @@
 ALL = Ellipsis
 MESH_ID = pl.DeviceIdType.MESH
 NT = (((1,), (1,)), ((), ()))
-
-
-def layer_norm(x_rows, ln_weight, ln_bias):
-    x_float = x_rows.astype(F32)
-    centered = x_float - jnp.mean(x_float, axis=-1, **KEEP)
-    inv_std = lax.rsqrt(jnp.mean(centered * centered, axis=-1, **KEEP) + LN_EPS)
-    x_hat = centered * inv_std
-    hidden = (x_hat * ln_weight.astype(F32) + ln_bias.astype(F32)).astype(BF16)
-    return hidden, jnp.mean(x_float, axis=-1, **KEEP), inv_std
-
-
-def masked_gate(logits, allowed, choice):
-    expert_ids = jnp.arange(logits.shape[-1])
-    prob_all = jax.nn.softmax(jnp.where(allowed, logits, -1e30), axis=-1)
-    picked = (choice[:, None] == expert_ids[None, :]).astype(F32)
-    return jnp.sum(prob_all * picked, axis=-1), prob_all, picked
 
 
 def ring_offsets(n_x):
@@ -92,6 +77,10 @@
 
     def barrier(self, signals=None):
         pl.semaphore_wait(pltpu.get_barrier_semaphore(), self.arrive() if signals is None else signals)
+
+
+def cost(flops, size):
+    return pl.CostEstimate(flops=flops, bytes_accessed=size, transcendentals=0)
 
 
 def rows_at(start, size, unit):
@@ -148,7 +137,7 @@
 def tail_kernel(grid, cap, *refs):
     refs = list(refs)
     take = lambda n: [refs.pop(0) for _ in range(n)]
-    _, o_next_h, dh_next_h, x_h, dy_h, hid_h, o_h, dh_h, stats, err_one, err_two, places, lnw, router = take(14)
+    _, o_next_h, dh_next_h, x_h, dy_h, hid_h, o_h, dh_h, stats, err_one, err_two, lnw, router = take(13)
     held, out, dx, small = take(4)
     x_v, dy_v, hid_v, o_v, dh_v, sel_one, sel_two, grad_h, val = take(9)
     first, second, third, c_one, c_two, c_three = take(6)
@@ -186,8 +175,8 @@
     for c in loads:
         c.start()
     slots = lax.broadcasted_iota(jnp.int32, (n_tok, 2 * rows), 1)
-    sel_one[ALL] = (slots == places[:, 0:1]).astype(F32).astype(BF16)
-    sel_two[ALL] = (slots == places[:, 1:2]).astype(F32).astype(BF16)
+    sel_one[ALL] = (slots == stats[:, 4:5].astype(jnp.int32)).astype(F32).astype(BF16)
+    sel_two[ALL] = (slots == stats[:, 5:6].astype(jnp.int32)).astype(F32).astype(BF16)
     gate_one, gate_two, mean, inv_std = [stats[:, i:i + 1] for i in range(4)]
     zero = jnp.zeros((n_tok, 1), F32)
     for c in loads:
@@ -209,7 +198,7 @@
     lanes = d_logits.shape[1]
     eye = (lax.broadcasted_iota(jnp.int32, (lanes, lanes), 0)
            == lax.broadcasted_iota(jnp.int32, (lanes, lanes), 1)).astype(F32).astype(BF16)
-    d_logits_t = lax.dot_general(eye, d_logits, NT, preferred_element_type=F32).astype(BF16)[:16]
+    d_logits_t = lax.dot_general(eye, d_logits, NT, preferred_element_type=F32).astype(BF16)[:PACK]
     sel_both = sel_one[ALL] + sel_two[ALL]
     row = lax.broadcasted_iota(jnp.int32, (8, wide), 0)
     own[1].wait()
@@ -222,11 +211,11 @@
                 + jnp.dot(sel_both, dh_v[:, cols], preferred_element_type=F32))
         x_hat = (x_v[:, cols].astype(F32) - mean) * inv_std
         grad_h[:, cols] = grad
-        val[0:16, cols] = jnp.dot(d_logits_t, hid_v[:, cols], preferred_element_type=F32)
+        val[:PACK, cols] = jnp.dot(d_logits_t, hid_v[:, cols], preferred_element_type=F32)
         d_weight = jnp.sum(grad * x_hat, axis=0, **KEEP)
         d_bias = jnp.sum(grad, axis=0, **KEEP)
-        val[16:SMALL, cols] = jnp.where(row == 0, d_weight, jnp.where(row == 1, d_bias, 0.0))
-        scaled = grad * lnw[:, cols]
+        val[PACK:SMALL, cols] = jnp.where(row == 0, d_weight, jnp.where(row == 1, d_bias, 0.0))
+        scaled = grad * lnw[0:1, cols]
         return sums[0] + jnp.sum(scaled, axis=1, **KEEP), sums[1] + jnp.sum(scaled * x_hat, axis=1, **KEEP)
 
     mean_one, mean_two = lax.fori_loop(0, d_model // wide, gradient, (zero, zero))
@@ -262,7 +251,7 @@
     def _(i):
         cols = rows_at(i * wide, wide, LANES)
         x_hat = (x_v[:, cols].astype(F32) - mean) * inv_std
-        step = inv_std * (grad_h[:, cols] * lnw[:, cols] - mean_one - x_hat * mean_two)
+        step = inv_std * (grad_h[:, cols] * lnw[0:1, cols] - mean_one - x_hat * mean_two)
         dx[:, cols] = (dy_v[:, cols].astype(F32) + step).astype(BF16)
 
     for k in range(n_peer):
@@ -297,7 +286,7 @@
     spread.sent(3)
 
 
-def tail_call(held, o_next, dh_next, tok_x, tok_dy, hidden, o, dh, stats, err_one, err_two, places, lnw, router, cap, grid, collective_id):
+def tail_call(held, o_next, dh_next, tok_x, tok_dy, hidden, o, dh, stats, err_one, err_two, lnw, router, cap, grid, collective_id):
     vmem, dma = pltpu.VMEM, pltpu.SemaphoreType.DMA
     n_tok, d_model = tok_x.shape
     rows = o.shape[0]
@@ -306,19 +295,20 @@
     hbm, on_chip = pl.BlockSpec(memory_space=pl.ANY), pl.BlockSpec(memory_space=pltpu.VMEM)
     tokens = jax.ShapeDtypeStruct((n_tok, d_model), BF16)
     peers, ring = dma((n_peer,)), dma((grid,))
+    deep, both = dma((UNITS, 15)), dma((2, n_peer))
     return pl.pallas_call(
         functools.partial(tail_kernel, grid, cap),
         out_shape=(jax.ShapeDtypeStruct(held.shape, F32), tokens, tokens, jax.ShapeDtypeStruct((SMALL, d_model), F32)),
-        in_specs=[hbm] * 8 + [on_chip] * 6, out_specs=(hbm, on_chip, on_chip, on_chip), input_output_aliases={0: 0},
+        in_specs=[hbm] * 8 + [on_chip] * 5, out_specs=(hbm, on_chip, on_chip, on_chip), input_output_aliases={0: 0},
         scratch_shapes=[vmem((n_tok, d_model), BF16)] * 3 + [vmem((2 * rows, d_model), BF16)] * 2
         + [vmem((n_tok, 2 * rows), BF16)] * 2 + [vmem((n_tok, d_model), F32), vmem((SMALL, d_model), F32)]
         + [vmem((n_ep, SMALL, width), F32), vmem((grid, SMALL, width), F32), vmem((grid, SMALL, width), F32)] + [vmem((SMALL, width), F32)] * 3
-        + [dma((7,)), dma((UNITS, 15)), dma((UNITS, 15)), dma((2, n_peer)), dma((2, n_peer)),
+        + [dma((7,)), deep, deep, both, both,
            peers, peers, ring, ring, ring, ring, peers, peers],
         compiler_params=pltpu.CompilerParams(collective_id=collective_id, has_side_effects=True, vmem_limit_bytes=50 * 2 ** 20),
-        cost_estimate=pl.CostEstimate(flops=10_000_000_000, bytes_accessed=STREAM, transcendentals=0),
+        cost_estimate=cost(10_000_000_000, STREAM),
         name='tail',
-    )(held, o_next, dh_next, tok_x, tok_dy, hidden, o, dh, stats, err_one, err_two, places, lnw, router)
+    )(held, o_next, dh_next, tok_x, tok_dy, hidden, o, dh, stats, err_one, err_two, lnw, router)
 
 
 def expert_kernel(dims, *refs):
@@ -326,8 +316,8 @@
     refs = list(refs)
     take = lambda n: [refs.pop(0) for _ in range(n)]
     if first:
-        sel_in, wg_h, wu_h, wd_h = take(7), *take(3)
-        o_h, dh_h, sh_h, h_next, q_next, hsl_next, qsl_next = take(7)
+        marks, columns, picks, norm, router, x_h, dy_h, wg_h, wu_h, wd_h = take(10)
+        o_h, dh_h, sh_h, h_next, q_next, hsl_next, qsl_next, hid_h, stats, err_one, err_two = take(11)
     else:
         h_next, q_next, hsl_next, qsl_next, wg_h, wu_h, wd_h, *carry = take(9)
         done_h, = take(1)
@@ -441,7 +431,7 @@
     def own_slice(axis, buf, sl):
         sl[rows_at(spot(axis) * rows, rows, PACK), :] = buf[:, rows_at(spot(axis) * quarter, quarter, LANES)]
 
-    strip = ff // 7
+    strip = ff // STRIPS
     u_cols = rows_at(here.z * rows, rows, LANES)
     g_cols = rows_at(here.y * rows, rows, LANES)
 
@@ -455,7 +445,7 @@
             a_t[ALL] += lax.dot_general(wg[:, cols], h_recv[:, cols], NT, preferred_element_type=F32)
             b_t[ALL] += lax.dot_general(wu[:, cols], h_recv[:, cols], NT, preferred_element_type=F32)
 
-        @pl.loop(0, 7)
+        @pl.loop(0, STRIPS)
         def _(i):
             r = rows_at(i * strip, strip, PACK)
             a = a_t[r, :]
@@ -469,7 +459,7 @@
             cols = rows_at(i * chunk, chunk, LANES)
             d_t[ALL] += lax.dot_general(wd[:, cols], q_recv[:, cols], NT, preferred_element_type=F32)
 
-        @pl.loop(0, 7)
+        @pl.loop(0, STRIPS)
         def _(i):
             r = rows_at(i * strip, strip, PACK)
             a, b, du = a_t[r, :], b_t[r, :], d_t[r, :]
@@ -517,13 +507,68 @@
                     == lax.broadcasted_iota(jnp.int32, (rows, rows), 1)).astype(F32).astype(BF16)
 
     if first:
-        inputs = [pltpu.make_async_copy(src, dst, lin.at[i])
-                  for i, (src, dst) in enumerate(zip(sel_in, (sel_h, hidden, sel_q, grad_one, grad_two, sel_h_next, sel_q_next)))]
+        inputs = [pltpu.make_async_copy(src, dst, lin.at[i]) for i, (src, dst) in enumerate(((x_h, hidden), (dy_h, grad_two)))]
+        n_tok = hidden.shape[0]
+        lane = lax.broadcasted_iota(jnp.int32, stats.shape, 1)
         for c in inputs:
             c.start()
         signals = here.arrive()
-        for c in inputs:
-            c.wait()
+
+        def place(table, i):
+            ids, slots = [table[j:j + 1, :] if table is picks else table[:, j:j + 1] for j in (i, i + 2)]
+            local = jnp.bitwise_and(ids, 1)
+            return jnp.where(slots >= 0, local * rows + jnp.right_shift(ids, 1) * cap + slots, -1)
+
+        for e, (one, two) in enumerate(((sel_h, sel_q), (sel_h_next, sel_q_next))):
+            slot = lax.broadcasted_iota(jnp.int32, one.shape, 0) + e * rows
+            hits = [(slot == place(picks, i)).astype(F32).astype(BF16) for i in range(2)]
+            one[ALL] = hits[0] + hits[1]
+            for i in range(2):
+                two[:, i * n_tok:(i + 1) * n_tok] = hits[i]
+        inputs[0].wait()
+        strip_rows = 2 * PACK
+
+        @pl.loop(0, n_tok // strip_rows)
+        def _(i):
+            r = rows_at(i * strip_rows, strip_rows, PACK)
+            x = hidden[r, :].astype(F32)
+            mean = jnp.mean(x, axis=1, **KEEP)
+            centered = x - mean
+            inv_std = lax.rsqrt(jnp.mean(centered * centered, axis=1, **KEEP) + LN_EPS)
+            hidden[r, :] = (centered * inv_std * norm[0:1, :] + norm[1:, :]).astype(BF16)
+            at = lane[:strip_rows]
+            stats[r, :] = jnp.where(at == 2, mean, jnp.where(at == 3, inv_std, 0.0))
+
+        hid_out = pltpu.make_async_copy(hidden, hid_h, lin.at[2])
+        hid_out.start()
+
+        def gates():
+            logits = lax.dot_general(hidden[ALL], router[ALL], NT, preferred_element_type=F32)
+            choices = [columns[:, i:i + 1] for i in range(2)]
+            err_one[ALL] = jnp.zeros_like(err_one)
+            err_one[:, :marks.shape[1]] = marks[ALL].astype(F32)
+            allowed = err_one[ALL] > 0
+            found = [place(columns, i).astype(F32) for i in range(2)]
+            for choice, err in zip(choices, (err_one, err_two)):
+                masked = jnp.where(allowed, logits, -1e30)
+                weight = jnp.exp(masked - jnp.max(masked, axis=1, **KEEP))
+                prob = weight / jnp.sum(weight, axis=1, **KEEP)
+                pick = (lane == choice).astype(F32)
+                found.append(jnp.sum(prob * pick, axis=1, **KEEP))
+                err[ALL] = pick - prob
+                allowed = jnp.logical_and(allowed, lane != choice)
+            total = stats[ALL]
+            for i, value in zip((4, 5, 0, 1), found):
+                total = jnp.where(lane == i, value, total)
+            stats[ALL] = total
+            inputs[1].wait()
+
+            @pl.loop(0, d_model // wide)
+            def _(i):
+                cols = rows_at(i * wide, wide, LANES)
+                dy = grad_two[:, cols].astype(F32)
+                grad_one[:, cols] = (stats[:, 0:1] * dy).astype(BF16)
+                grad_two[:, cols] = (stats[:, 1:2] * dy).astype(BF16)
 
         def gather(sel, source, out, e):
             @pl.loop(0, d_model // chunk)
@@ -534,7 +579,6 @@
                     total += jnp.dot(sel[block(e), j * n_tok:(j + 1) * n_tok], source[j][:, cols], preferred_element_type=F32)
                 out[block(e), cols] = total.astype(BF16)
 
-        n_tok = hidden.shape[0]
         rows_h, rows_q = (hidden,), (grad_one, grad_two)
         now = ((sel_h, rows_h, h_send, h_recv, xh_s, xh_r), (sel_q, rows_q, q_send, q_recv, xq_s, xq_r))
         later = ((sel_h_next, rows_h, h_send_next, h_next, nh_s, nh_r), (sel_q_next, rows_q, q_send_next, q_next, nq_s, nq_r))
@@ -566,25 +610,22 @@
                 for k in ks:
                     copy_of(group[i], k).wait_send()
 
-        def partner(group):
-            for what in group:
-                gather(what[0], what[1], what[2], here.ep_to(0))
-
-        def partner_send(group):
-            for what in group:
-                copy_of(what, 0).start()
+        def partner(what):
+            gather(what[0], what[1], what[2], here.ep_to(0))
+            copy_of(what, 0).start()
 
         gather_step(0)
         here.barrier(signals)
         send_step(0)
         gather_step(1)
         send_step(1)
-        partner(now)
-        partner_send(now)
         for c in weights:
             c.start()
-        for what in now:
+        for i, what in enumerate(now):
+            partner(what)
             gather(what[0], what[1], what[3], ep)
+            if not i:
+                gates()
         make_eye()
 
         spread = (('y', h_recv, h_sl, hs_s, hs_r), ('z', q_recv, q_sl, qs_s, qs_r))
@@ -613,8 +654,8 @@
         for what in later:
             gather(what[0], what[1], what[2], ep)
         own_next = [pltpu.make_async_copy(what[2].at[block(ep), :], what[3].at[block(ep), :], lin.at[7 + i]) for i, what in enumerate(later)]
-        partner(later)
-        partner_send(later)
+        for what in later:
+            partner(what)
         middle, last = max(len(pairs) - 1, 0), max(ahead - 1, 0)
         for n in range(last + 1):
             gather_step(n + 2)
@@ -750,7 +791,7 @@
             copy_of(what, 0).wait_send()
         for n in range(2, 6):
             sent_step(ahead + n)
-        for c in own_next:
+        for c in own_next + [hid_out]:
             c.wait()
     else:
         for j in range(len(back)):
@@ -765,16 +806,17 @@
         c.wait()
 
 
-def expert_call(inputs, w_gate, w_up, w_down, expert, cap, grid):
+def expert_call(inputs, w_gate, w_up, w_down, expert, cap, grid, mesh_ep):
     first = expert == 0
     d_model = w_gate.shape[2]
     ff = w_gate.shape[1]
-    rows = inputs[0].shape[0]
+    rows = (mesh_ep if first else inputs[0].shape[0] // cap) * cap
     quarter, share = d_model // grid, ff // grid
     n_peer = rows // cap - 1
     chunk = min(1024, d_model)
     vmem, dma = pltpu.VMEM, pltpu.SemaphoreType.DMA
     hbm = pl.BlockSpec(memory_space=pl.ANY)
+    on_chip = pl.BlockSpec(memory_space=pltpu.VMEM)
     row_block, slice_block = (rows, d_model), (grid * rows, quarter)
     scratch = [
         vmem(row_block, BF16), vmem(row_block, BF16),
@@ -789,22 +831,25 @@
     share_block = (UNITS, 3, share, quarter // UNITS)
     outs = [out(row_block), out(row_block), out(share_block, F32)]
     if first:
-        sel_h, hidden, sel_q, grad_one, grad_two, sel_h_next, sel_q_next = inputs
-        scratch += [vmem(x.shape, BF16) for x in (sel_h, sel_q, sel_h_next, sel_q_next, hidden, grad_one, grad_two)]
+        tokens = inputs[-1].shape
+        n_tok = tokens[0]
+        scratch += [vmem((rows, i * n_tok), BF16) for i in (1, 2, 1, 2)] + [vmem(tokens, BF16)] * 3
         scratch += [vmem(row_block, BF16)] * 4 + [dma((n_peer,))] * 8 + [dma((grid,))] * 4 + [dma((9,))]
         operands = (*inputs, w_gate, w_up, w_down)
-        outs += [out(row_block), out(row_block), out(slice_block), out(slice_block)]
+        outs += [out(row_block), out(row_block), out(slice_block), out(slice_block), out(tokens)] + [out((n_tok, LANES), F32)] * 3
+        in_specs, out_specs = [on_chip] * 5 + [hbm] * 5, [hbm] * 8 + [on_chip] * 3
     else:
         h_next, q_next, hsl_next, qsl_next, *carry, done = inputs
-        scratch += [vmem(row_block, BF16)] * 2 + [dma((2, n_peer)), dma((2, n_peer)), dma((2,)), dma((2 + 2 * grid,))]
-        scratch += [dma((UNITS, 15)), dma((UNITS, 15))]
+        scratch += [vmem(row_block, BF16)] * 2 + [dma((2, n_peer))] * 2 + [dma((2,)), dma((2 + 2 * grid,))]
+        scratch += [dma((UNITS, 15))] * 2
         operands = (h_next, q_next, hsl_next, qsl_next, w_gate, w_up, w_down, *carry, done)
         outs += [out(row_block), out(row_block), out((grid * grid,) + share_block, F32)]
+        in_specs, out_specs = [hbm] * len(operands), [hbm] * len(outs)
     return pl.pallas_call(
         functools.partial(expert_kernel, (expert, grid, chunk, cap, first)),
-        out_shape=tuple(outs), in_specs=[hbm] * len(operands), out_specs=(hbm,) * len(outs), scratch_shapes=scratch,
+        out_shape=tuple(outs), in_specs=in_specs, out_specs=tuple(out_specs), scratch_shapes=scratch,
         compiler_params=pltpu.CompilerParams(collective_id=expert, has_side_effects=True, vmem_limit_bytes=63 * 2 ** 20),
-        cost_estimate=pl.CostEstimate(flops=2 * rows * d_model * ff * 9, bytes_accessed=STREAM, transcendentals=0),
+        cost_estimate=cost(2 * rows * d_model * ff * 9, STREAM),
     )(*operands)
 
 
@@ -837,7 +882,7 @@
         in_specs=[row_first, up_first, col_first] + strips + [pl.BlockSpec(memory_space=pl.ANY)] * len(into),
         out_specs=(out_spec,) * 3 + tuple(strips), input_output_aliases={3 + i: i for i in range(len(into))},
         compiler_params=pltpu.CompilerParams(vmem_limit_bytes=40 * 2 ** 20),
-        cost_estimate=pl.CostEstimate(flops=1_000_000, bytes_accessed=44_000_000, transcendentals=0),
+        cost_estimate=cost(1_000_000, 44_000_000),
     )(gathered, gathered, gathered, *through, *into)
 
 
@@ -854,49 +899,21 @@
         n_exp = eligible.shape[1]
         local_exp = w_gate.shape[0]
         slot_cap = 3 * n_local // n_exp
-        hidden, mean, inv_std = layer_norm(tok_x, ln_weight, ln_bias)
-        logits = jnp.dot(hidden, router, preferred_element_type=F32)
-        expert_ids = jnp.arange(n_exp)
-        allowed = eligible > 0
-        gate_one, prob_one, pick_one = masked_gate(logits, allowed, exp_first)
-        gate_two, prob_two, pick_two = masked_gate(logits, allowed & (expert_ids[None, :] != exp_first[:, None]), exp_second)
-        per = n_ep * slot_cap
-        row_ids = jnp.arange(n_exp * slot_cap)
-
-        def place(expert, slot):
-            pos = (expert % local_exp) * per + (expert // local_exp) * slot_cap + slot
-            return jnp.where(slot >= 0, pos, -1)
-
-        pos_one = place(exp_first, slot_first)
-        pos_two = place(exp_second, slot_second)
-        dy_float = tok_dy.astype(F32)
-        grad_one = (gate_one[:, None] * dy_float).astype(BF16)
-        grad_two = (gate_two[:, None] * dy_float).astype(BF16)
-        pos_pair = jnp.concatenate([pos_one, pos_two])
         wg_t, wu_t = jnp.swapaxes(w_gate, 1, 2), jnp.swapaxes(w_up, 1, 2)
 
-        def lanes(columns):
-            flat = jnp.concatenate(columns, axis=1)
-            return jnp.pad(flat, ((0, 0), (0, LANES - flat.shape[1])))
-
-        stats = lanes([gate_one[:, None], gate_two[:, None], mean, inv_std])
-        err_one, err_two = lanes([pick_one - prob_one]), lanes([pick_two - prob_two])
-        places = lanes([pos_one[:, None], pos_two[:, None]])
+        columns = jnp.stack([exp_first, exp_second, slot_first, slot_second], axis=1)
+        picks = jnp.stack([exp_first, exp_second, slot_first, slot_second])
+        norm = jnp.stack([ln_weight, ln_bias]).astype(F32)
         router_t = jnp.pad(router.T, ((0, LANES - n_exp), (0, 0)))
-        cuts = [slice(e * per, (e + 1) * per) for e in range(local_exp)]
-        sels = []
-        for e in range(local_exp):
-            ids = row_ids[cuts[e]][:, None]
-            sels.append(jnp.logical_or(ids == pos_one[None, :], ids == pos_two[None, :]).astype(BF16))
-            sels.append((ids == pos_pair[None, :]).astype(BF16))
-        o, dh, share, *landed = expert_call((sels[0], hidden, sels[1], grad_one, grad_two, sels[2], sels[3]), wg_t, wu_t, w_down, 0, slot_cap, grid)
-        o_next, dh_next, share, o, dh, held = expert_call((*landed, o, dh, share), wg_t, wu_t, w_down, 1, slot_cap, grid)
+        o, dh, share, *landed, hidden, stats, err_one, err_two = expert_call(
+            (eligible, columns, picks, norm, router_t, tok_x, tok_dy), wg_t, wu_t, w_down, 0, slot_cap, grid, n_ep)
+        o_next, dh_next, share, o, dh, held = expert_call((*landed, o, dh, share), wg_t, wu_t, w_down, 1, slot_cap, grid, n_ep)
         gathered_next = lax.all_gather(share, 'dp')
         held, out_tok, dx_tok, small = tail_call(
-            held, o_next, dh_next, tok_x, tok_dy, hidden, o, dh, stats, err_one, err_two, places,
-            ln_weight.astype(F32)[None], router_t, slot_cap, grid, local_exp + 1)
+            held, o_next, dh_next, tok_x, tok_dy, hidden, o, dh, stats, err_one, err_two,
+            norm, router_t, slot_cap, grid, local_exp + 1)
         gathered = [x.reshape((grid, grid) + share.shape) for x in (held, gathered_next)]
-        d_router, d_ln_weight, d_ln_bias = small[:n_exp].T, small[16], small[17]
+        d_router, d_ln_weight, d_ln_bias = small[:n_exp].T, small[PACK], small[PACK + 1]
         *weights, out_tok, dx_tok = assemble(gathered[0], 0, local_exp, (), (out_tok, dx_tok))
         weights = assemble(gathered[1], 1, local_exp, weights)
         dw_gate, dw_up, dw_down = jnp.swapaxes(weights[0], 1, 2), jnp.swapaxes(weights[1], 1, 2), weights[2]

time: 487 us -> 487 us (level)
  other arithmetic: 11.7 us -> 2.73 us
  Pallas kernels: 419 us -> 425 us
  local copies, waits for them, and re-layouts: 4.86 us -> 9.83 us
    pallas_call x2, Pallas kernels: 260 us -> 268 us  [expert_call(): pl.pallas_call(functools.partial(expert_kernel, (expert, grid, chunk, cap...]
    convert_element_type x6 -> x1, other arithmetic: 6.24 us -> 0.66 us  [local_step(): norm = jnp.stack([ln_weight, ln_bias]).astype(F32)]
    reduce_sum x4 -> x0, other arithmetic: 4.9 us -> none  [the longest x1 2.31 us: layer_norm(): inv_std = lax.rsqrt(jnp.mean(centered * centered, axis=-1, **KEEP) + LN_EPS)]
where the time goes in v4:
time: 487 us
  Pallas kernels  425 us (87%)
  waiting for transfers between devices  34.3 us (7%)
  between operations  14.1 us (3%)
  local copies, waits for them, and re-layouts  9.83 us (2%)
    pallas_call x2, Pallas kernels, expert_call(): pl.pallas_call(functools.partial(expert_kernel, (expert, grid, chunk, cap...  268 us
    pallas_call x1, Pallas kernels, tail_call(): pl.pallas_call(functools.partial(tail_kernel, grid, cap), out_shape=(jax....  124 us
    all_gather x1, waiting for transfers between devices, local_step(): gathered_next = lax.all_gather(share, 'dp')  34.3 us
    pallas_call x2, Pallas kernels, assemble(): pl.pallas_call(assemble_kernel, grid=(grid, cut), out_shape=(whole,) * 3...  33.8 us
  transfers between devices with their start and end apart: 1, of which 1 were waited for; matrix products, arithmetic and copies ran while one was open for 0% of the time, Pallas kernels for 29%

profile of v4, /device:TPU:1, one launch (start us, length us, event | category | flops | bytes accessed | tf_op | source)
XLA Modules:
  0.0 486.5 jit_solution(5587582071839313469)
XLA Ops:
  7.2 0.0 all-gather.3.cloned.1.call-start
  7.2 0.7 stack.49
  7.9 0.7 stack.50
  8.6 0.7 pad_add_fusion
  9.4 0.8 copy.32.refs_1_
  10.2 1.5 copy.31.refs_0_
  11.7 0.7 maximum_convert_fusion.refs_3_.refs_11_
  12.3 2.0 pad.4.refs_4_.refs_12_
  14.3 1.3 pad_add_fusion.1.refs_2_
  15.6 163.9 %shard_map.188 = (bf16[384,4096]{1,0:T(8,128)(2,1)}, bf16[384,4096]{1,0:T(8,128)(2,1)}, f32[4,3,112,256]{3,2,1,0:T(8,128)}, bf16[384,4096]{1,0:T(8,128)(2,1)}, b...) custom-call(s32[256,16]{1,0:T(8,128)} %copy.31.refs_0_, ...), custom_call_target="tpu_custom_call" | custom-call | flops 12683575296 | bytes 30000000 | tf_op jit(solution)/shard_map/pallas_call | solution.py:848
  179.5 0.0 copy-start.2
  179.5 0.0 copy-start.3
  179.5 0.0 copy-start.4
  179.5 0.0 copy-start.5
  179.6 103.8 %shard_map.189 = (bf16[384,4096]{1,0:T(8,128)(2,1)}, bf16[384,4096]{1,0:T(8,128)(2,1)}, f32[4,3,112,256]{3,2,1,0:T(8,128)}, bf16[384,4096]{1,0:T(8,128)(2,1)}, b...) custom-call(bf16[384,4096]{1,0:T(8,128)(2,1)} %get-tuple-element.37.refs_0_, ...), custom_call_target="tpu_custom_call" | custom-call | flops 12683575296 | bytes 30000000 | tf_op jit(solution)/shard_map/pallas_call | solution.py:848
  283.3 0.0 all-gather.3.cloned.1.call-update
  283.4 0.0 copy-done.2
  283.4 0.0 copy-done.3
  283.4 0.0 copy-done.4
  283.4 0.0 copy-done.5
  283.4 0.0 copy-start
  283.4 1.2 copy-done
  284.6 124.0 %tail.1 = (f32[16,4,3,112,256]{4,3,2,1,0:T(8,128)}, bf16[256,4096]{1,0:T(8,128)(2,1)S(1)}, bf16[256,4096]{1,0:T(8,128)(2,1)}, f32[24,4096]{1,0:T(8,128)S(1)}) custom-call(f32[16,4,3,112,256]{4,3,2,1,0:T(8,128)} %get-tuple-element.44.refs_0_, bf16[384,4096]{1,0:T(8,128)(2,1)} %get-tuple-element.45.refs_1_, ...), custom_call_target="tpu_custom_call", output_to_operand_aliasing={{0}: (0, {})} | custom-call | flops 10000000000 | bytes 30000000 | tf_op jit(solution)/shard_map/tail/pallas_call | solution.py:299
  408.6 0.0 copy-start.1
  408.6 1.6 copy-done.1
  410.2 17.4 %shard_map.190 = (f32[2,448,4096]{2,1,0:T(8,128)}, f32[2,448,4096]{2,1,0:T(8,128)}, f32[2,448,4096]{2,1,0:T(8,128)}, bf16[256,4096]{1,0:T(8,128)(2,1)}, bf16[256,4096]{1,0:T(8,128)(2,1)}) custom-call(f32[4,4,4,3,112,256]{5,4,3,2,1,0:T(8,128)} %bitcast.19, f32[4,4,4,3,112,256]{5,4,3,2,1,0:T(8,128)} %bitcast.20, f32[4,4,4,3,112,256]{5,4,3,2,1,0:T(8,128)} %bitcast.21, ...), custom_call_target="tpu_custom_call" | custom-call | flops 1000000 | bytes 44000000 | tf_op jit(solution)/shard_map/pallas_call | solution.py:880
  427.6 0.6 fusion
  428.2 0.7 slice_bitcast_fusion
  428.9 34.3 %all-gather.3.cloned.1.call-done = f32[64,3,112,256]{3,2,1,0:T(8,128)} async-done(((f32[4,3,112,256]{3,2,1,0:T(8,128)}), f32[64,3,112,256]{3,2,1,0:T(8,128)}) %all-gather.3.cloned.1.call-update) | async-done | bytes 22020112 | tf_op jit(solution)/shard_map/all_gather | solution.py:911
  463.3 16.4 %shard_map.191 = (f32[2,448,4096]{2,1,0:T(8,128)}, f32[2,448,4096]{2,1,0:T(8,128)}, f32[2,448,4096]{2,1,0:T(8,128)}) custom-call(f32[4,4,4,3,112,256]{5,4,3,2,1,0:T(8,128)} %bitcast.22, f32[4,4,4,3,112,256]{5,4,3,2,1,0:T(8,128)} %bitcast.23, f32[4,4,4,3,112,256]{5,4,3,2,1,0:T(8,128)} %bitcast.24, ...), custom_call_target="tpu_custom_call", output_to_operand_aliasing={{0}: (3, {}), {1}: (4, {}), {2}: (5, {})} | custom-call | flops 1000000 | bytes 44000000 | tf_op jit(solution)/shard_map/pallas_call | solution.py:880
Async XLA Ops:
  7.2 456.1 %all-gather.3.cloned.1.call-start = ((), (), s32[]{:S(2)}) async-start(), calls=%async_computation | async-start | bytes 23396352 | tf_op jit(solution)/shard_map/all_gather | solution.py:911
  179.5 103.8 %copy-start.2 = (f32[256,128]{1,0:T(8,128)S(1)}, f32[256,128]{1,0:T(8,128)}, u32[]{:S(2)}) copy-start(f32[256,128]{1,0:T(8,128)} %get-tuple-element.50.refs_8_) | copy-start | bytes 393220
  179.5 103.8 %copy-start.3 = (f32[256,128]{1,0:T(8,128)S(1)}, f32[256,128]{1,0:T(8,128)}, u32[]{:S(2)}) copy-start(f32[256,128]{1,0:T(8,128)} %get-tuple-element.51.refs_9_) | copy-start | bytes 393220
  179.5 103.8 %copy-start.4 = (f32[256,128]{1,0:T(8,128)S(1)}, f32[256,128]{1,0:T(8,128)}, u32[]{:S(2)}) copy-start(f32[256,128]{1,0:T(8,128)} %get-tuple-element.52.refs_10_) | copy-start | bytes 393220
  179.5 103.8 %copy-start.5 = (f32[2,4096]{1,0:T(2,128)S(1)}, f32[2,4096]{1,0:T(2,128)}, u32[]{:S(2)}) copy-start(f32[2,4096]{1,0:T(2,128)} %maximum_convert_fusion.refs_3_.refs_11_) | copy-start | bytes 98308
  283.4 1.2 copy-start
  408.6 1.6 copy-start.1
Sparse Core Ops, SparseCore 0:
  283.5 179.7 all-gather.2

commit v5 on v4

--- a/solution.py
+++ b/solution.py
@@ -79,6 +79,11 @@
         pl.semaphore_wait(pltpu.get_barrier_semaphore(), self.arrive() if signals is None else signals)
 
 
+def widen(out, rows):
+    out[ALL] = jnp.zeros_like(out)
+    out[:rows.shape[0], :] = rows
+
+
 def cost(flops, size):
     return pl.CostEstimate(flops=flops, bytes_accessed=size, transcendentals=0)
 
@@ -121,25 +126,25 @@
             for unit in range(UNITS):
                 yield self.copy(unit, index)
 
-    def send(self, stage, picks=None):
-        for c in self.each(stage, picks):
+    def send(self, *what):
+        for c in self.each(*what):
             c.start()
 
-    def receive(self, stage):
-        for c in self.each(stage):
+    def receive(self, *what):
+        for c in self.each(*what):
             c.wait_recv()
 
-    def sent(self, stage):
-        for c in self.each(stage):
+    def sent(self, *what):
+        for c in self.each(*what):
             c.wait_send()
 
 
 def tail_kernel(grid, cap, *refs):
     refs = list(refs)
     take = lambda n: [refs.pop(0) for _ in range(n)]
-    _, o_next_h, dh_next_h, x_h, dy_h, hid_h, o_h, dh_h, stats, err_one, err_two, lnw, router = take(13)
+    _, o_next_h, dh_next_h, x_h, dy_h, hid_h, o_h, dh_h, stats, err_one, err_two, lnw, router_in = take(13)
     held, out, dx, small = take(4)
-    x_v, dy_v, hid_v, o_v, dh_v, sel_one, sel_two, grad_h, val = take(9)
+    x_v, dy_v, hid_v, o_v, dh_v, sel_one, sel_two, grad_h, val, router = take(10)
     first, second, third, c_one, c_two, c_three = take(6)
     loc, sp_s, sp_r, ba_s, ba_r, s_one, r_one, s_two, r_two, s_three, r_three, s_four, r_four = take(13)
     n_tok, d_model = x_v.shape
@@ -174,6 +179,7 @@
         (x_h, x_v), (dy_h, dy_v), (hid_h, hid_v), (o_h, o_v.at[home, :]), (dh_h, dh_v.at[home, :])))]
     for c in loads:
         c.start()
+    widen(router, router_in[ALL])
     slots = lax.broadcasted_iota(jnp.int32, (n_tok, 2 * rows), 1)
     sel_one[ALL] = (slots == stats[:, 4:5].astype(jnp.int32)).astype(F32).astype(BF16)
     sel_two[ALL] = (slots == stats[:, 5:6].astype(jnp.int32)).astype(F32).astype(BF16)
@@ -215,7 +221,7 @@
         d_weight = jnp.sum(grad * x_hat, axis=0, **KEEP)
         d_bias = jnp.sum(grad, axis=0, **KEEP)
         val[PACK:SMALL, cols] = jnp.where(row == 0, d_weight, jnp.where(row == 1, d_bias, 0.0))
-        scaled = grad * lnw[0:1, cols]
+        scaled = grad * lnw[:, cols]
         return sums[0] + jnp.sum(scaled, axis=1, **KEEP), sums[1] + jnp.sum(scaled * x_hat, axis=1, **KEEP)
 
     mean_one, mean_two = lax.fori_loop(0, d_model // wide, gradient, (zero, zero))
@@ -251,7 +257,7 @@
     def _(i):
         cols = rows_at(i * wide, wide, LANES)
         x_hat = (x_v[:, cols].astype(F32) - mean) * inv_std
-        step = inv_std * (grad_h[:, cols] * lnw[0:1, cols] - mean_one - x_hat * mean_two)
+        step = inv_std * (grad_h[:, cols] * lnw[:, cols] - mean_one - x_hat * mean_two)
         dx[:, cols] = (dy_v[:, cols].astype(F32) + step).astype(BF16)
 
     for k in range(n_peer):
@@ -301,7 +307,7 @@
         out_shape=(jax.ShapeDtypeStruct(held.shape, F32), tokens, tokens, jax.ShapeDtypeStruct((SMALL, d_model), F32)),
         in_specs=[hbm] * 8 + [on_chip] * 5, out_specs=(hbm, on_chip, on_chip, on_chip), input_output_aliases={0: 0},
         scratch_shapes=[vmem((n_tok, d_model), BF16)] * 3 + [vmem((2 * rows, d_model), BF16)] * 2
-        + [vmem((n_tok, 2 * rows), BF16)] * 2 + [vmem((n_tok, d_model), F32), vmem((SMALL, d_model), F32)]
+        + [vmem((n_tok, 2 * rows), BF16)] * 2 + [vmem((n_tok, d_model), F32), vmem((SMALL, d_model), F32), vmem((LANES, d_model), BF16)]
         + [vmem((n_ep, SMALL, width), F32), vmem((grid, SMALL, width), F32), vmem((grid, SMALL, width), F32)] + [vmem((SMALL, width), F32)] * 3
         + [dma((7,)), deep, deep, both, both,
            peers, peers, ring, ring, ring, ring, peers, peers],
@@ -316,18 +322,19 @@
     refs = list(refs)
     take = lambda n: [refs.pop(0) for _ in range(n)]
     if first:
-        marks, columns, picks, norm, router, x_h, dy_h, wg_h, wu_h, wd_h = take(10)
-        o_h, dh_h, sh_h, h_next, q_next, hsl_next, qsl_next, hid_h, stats, err_one, err_two = take(11)
+        marks, *lines = take(1 + UNITS)
+        lnw, lnb, router_in, x_h, dy_h, wg_h, wu_h, wd_h = take(8)
+        o_h, dh_h, sh_h, h_next, q_next, hsl_next, qsl_next, hid_h, all_h, stats, err_one, err_two = take(12)
     else:
         h_next, q_next, hsl_next, qsl_next, wg_h, wu_h, wd_h, *carry = take(9)
-        done_h, = take(1)
+        done_h, _ = take(2)
         o_h, dh_h, sh_h, *carry_out = take(5)
         all_h, = take(1)
     h_recv, q_recv, wg, wu, wd, a_t, b_t, d_t, u_all, da_all, db_all, h_sl, q_sl, dw, rsb, act, act_b, eye = take(18)
     loc, hs_s, hs_r, qs_s, qs_r, ga_s, ga_r, rs_s, rs_r = take(9)
     if first:
-        sel_h, sel_q, sel_h_next, sel_q_next, hidden, grad_one, grad_two, h_send, q_send, h_send_next, q_send_next = take(11)
-        xh_s, xh_r, xq_s, xq_r, nh_s, nh_r, nq_s, nq_r, ns_h_s, ns_h_r, ns_q_s, ns_q_r, lin = take(13)
+        sel_h, sel_q, sel_h_next, sel_q_next, hidden, grad_one, grad_two, h_send, q_send, h_send_next, q_send_next, router, wide_table = take(13)
+        xh_s, xh_r, xq_s, xq_r, nh_s, nh_r, nq_s, nq_r, ns_h_s, ns_h_r, ns_q_s, ns_q_r, lin, sp_s, sp_r = take(15)
         o_v, dh_v = h_send, q_send
     else:
         o_v, dh_v = take(2)
@@ -510,18 +517,19 @@
         inputs = [pltpu.make_async_copy(src, dst, lin.at[i]) for i, (src, dst) in enumerate(((x_h, hidden), (dy_h, grad_two)))]
         n_tok = hidden.shape[0]
         lane = lax.broadcasted_iota(jnp.int32, stats.shape, 1)
+        n_exp = router_in.shape[0]
         for c in inputs:
             c.start()
         signals = here.arrive()
-
-        def place(table, i):
-            ids, slots = [table[j:j + 1, :] if table is picks else table[:, j:j + 1] for j in (i, i + 2)]
+        make_eye()
+
+        def place(ids, slots):
             local = jnp.bitwise_and(ids, 1)
             return jnp.where(slots >= 0, local * rows + jnp.right_shift(ids, 1) * cap + slots, -1)
 
         for e, (one, two) in enumerate(((sel_h, sel_q), (sel_h_next, sel_q_next))):
             slot = lax.broadcasted_iota(jnp.int32, one.shape, 0) + e * rows
-            hits = [(slot == place(picks, i)).astype(F32).astype(BF16) for i in range(2)]
+            hits = [(slot == place(lines[i][ALL], lines[i + 2][ALL])).astype(F32).astype(BF16) for i in range(2)]
             one[ALL] = hits[0] + hits[1]
             for i in range(2):
                 two[:, i * n_tok:(i + 1) * n_tok] = hits[i]
@@ -535,7 +543,7 @@
             mean = jnp.mean(x, axis=1, **KEEP)
             centered = x - mean
             inv_std = lax.rsqrt(jnp.mean(centered * centered, axis=1, **KEEP) + LN_EPS)
-            hidden[r, :] = (centered * inv_std * norm[0:1, :] + norm[1:, :]).astype(BF16)
+            hidden[r, :] = (centered * inv_std * lnw[ALL] + lnb[ALL]).astype(BF16)
             at = lane[:strip_rows]
             stats[r, :] = jnp.where(at == 2, mean, jnp.where(at == 3, inv_std, 0.0))
 
@@ -543,12 +551,16 @@
         hid_out.start()
 
         def gates():
+            widen(router, router_in[ALL])
+            row = lax.broadcasted_iota(jnp.int32, marks.shape, 0)
+            index_rows = sum(jnp.where(row == i, lines[i][ALL], 0) for i in range(UNITS))
+            widen(wide_table, jnp.concatenate([marks[ALL], index_rows]).astype(F32).astype(BF16))
+            columns = lax.dot_general(eye[:n_tok, :n_tok], wide_table[ALL], NT, preferred_element_type=F32)
             logits = lax.dot_general(hidden[ALL], router[ALL], NT, preferred_element_type=F32)
-            choices = [columns[:, i:i + 1] for i in range(2)]
-            err_one[ALL] = jnp.zeros_like(err_one)
-            err_one[:, :marks.shape[1]] = marks[ALL].astype(F32)
-            allowed = err_one[ALL] > 0
-            found = [place(columns, i).astype(F32) for i in range(2)]
+            ints = [columns[:, n_exp + i:n_exp + i + 1].astype(jnp.int32) for i in range(UNITS)]
+            choices, allowed = ints[:2], jnp.logical_and(columns > 0, lane < n_exp)
+            found = [place(*ints[i::2]) for i in range(2)]
+            found = [value.astype(F32) for value in found]
             for choice, err in zip(choices, (err_one, err_two)):
                 masked = jnp.where(allowed, logits, -1e30)
                 weight = jnp.exp(masked - jnp.max(masked, axis=1, **KEEP))
@@ -626,8 +638,6 @@
             gather(what[0], what[1], what[3], ep)
             if not i:
                 gates()
-        make_eye()
-
         spread = (('y', h_recv, h_sl, hs_s, hs_r), ('z', q_recv, q_sl, qs_s, qs_r))
         spread_next = (('y', h_next, hsl_next, ns_h_s, ns_h_r), ('z', q_next, qsl_next, ns_q_s, ns_q_r))
 
@@ -693,8 +703,8 @@
         back = list(zip(carry, carry_out))
         spread_unit = Spread(here, done_h, all_h, sp_s, sp_r)
         own_unit = pltpu.make_async_copy(done_h, all_h.at[here.dp], lin.at[1])
-        spread_unit.send(0)
-        spread_unit.send(1, (0,))
+        spread_unit.send(1, (1,))
+        spread_unit.send(2, (0,))
 
         def back_copy(j, k):
             src, dst = back[j]
@@ -732,9 +742,6 @@
     untranspose(act_b, db_all, g_cols)
     share_on(1)
     share_on(2)
-    if not first:
-        spread_unit.receive(0)
-        spread_unit.send(1, (1,))
     dh_pass()
     dh_out = pltpu.make_async_copy(dh_v, dh_h, loc.at[4])
     dh_out.start()
@@ -751,8 +758,6 @@
     share_done(1)
     weight_grad(0, da_all, h_sl)
     reduce_start(0)
-    if not first:
-        spread_unit.send(2, (0,))
     share_done(0)
     weight_grad(2, u_all, q_sl)
     share_done(2)
@@ -762,7 +767,7 @@
     if first:
         forward_step(ahead + 1)
     else:
-        spread_unit.receive(1)
+        spread_unit.receive(1, (1,))
     reduce_on(0)
     if not first:
         spread_unit.send(2, (1,))
@@ -775,6 +780,12 @@
         spread_unit.send(2, (2, 3))
     ends = reduce_end(0) + reduce_end(1) + reduce_end(2)
     if first:
+        for c in ends:
+            c.wait()
+        ends = []
+        spread_unit = Spread(here, sh_h, all_h, sp_s, sp_r)
+        spread_unit.send(0)
+        spread_unit.send(1, (0,))
         forward_step(ahead + 5)
 
     for j in range(3):
@@ -793,14 +804,17 @@
             sent_step(ahead + n)
         for c in own_next + [hid_out]:
             c.wait()
+        for stage, picks in enumerate((None, (0,))):
+            spread_unit.receive(stage, picks)
+            spread_unit.sent(stage, picks)
     else:
         for j in range(len(back)):
             for k in range(n_peer):
                 back_copy(j, k).wait()
             back_own(j).wait()
         spread_unit.receive(2)
-        for stage in range(3):
-            spread_unit.sent(stage)
+        spread_unit.sent(1, (1,))
+        spread_unit.sent(2)
         own_unit.wait()
     for c in ends + [o_out, dh_out]:
         c.wait()
@@ -834,20 +848,23 @@
         tokens = inputs[-1].shape
         n_tok = tokens[0]
         scratch += [vmem((rows, i * n_tok), BF16) for i in (1, 2, 1, 2)] + [vmem(tokens, BF16)] * 3
-        scratch += [vmem(row_block, BF16)] * 4 + [dma((n_peer,))] * 8 + [dma((grid,))] * 4 + [dma((9,))]
+        scratch += [vmem(row_block, BF16)] * 4 + [vmem((LANES, d_model), BF16), vmem((LANES, n_tok), BF16)] + [dma((n_peer,))] * 8 + [dma((grid,))] * 4 + [dma((9,))] + [dma((UNITS, 15))] * 2
         operands = (*inputs, w_gate, w_up, w_down)
-        outs += [out(row_block), out(row_block), out(slice_block), out(slice_block), out(tokens)] + [out((n_tok, LANES), F32)] * 3
-        in_specs, out_specs = [on_chip] * 5 + [hbm] * 5, [hbm] * 8 + [on_chip] * 3
+        outs += [out(row_block), out(row_block), out(slice_block), out(slice_block), out(tokens)]
+        outs += [out((grid * grid,) + share_block, F32)] + [out((n_tok, LANES), F32)] * 3
+        aliases = {}
+        in_specs, out_specs = [on_chip] * 8 + [hbm] * 5, [hbm] * 9 + [on_chip] * 3
     else:
-        h_next, q_next, hsl_next, qsl_next, *carry, done = inputs
+        h_next, q_next, hsl_next, qsl_next, *carry, done, held = inputs
         scratch += [vmem(row_block, BF16)] * 2 + [dma((2, n_peer))] * 2 + [dma((2,)), dma((2 + 2 * grid,))]
         scratch += [dma((UNITS, 15))] * 2
-        operands = (h_next, q_next, hsl_next, qsl_next, w_gate, w_up, w_down, *carry, done)
+        operands = (h_next, q_next, hsl_next, qsl_next, w_gate, w_up, w_down, *carry, done, held)
         outs += [out(row_block), out(row_block), out((grid * grid,) + share_block, F32)]
         in_specs, out_specs = [hbm] * len(operands), [hbm] * len(outs)
+        aliases = {len(operands) - 1: len(outs) - 1}
     return pl.pallas_call(
         functools.partial(expert_kernel, (expert, grid, chunk, cap, first)),
-        out_shape=tuple(outs), in_specs=in_specs, out_specs=tuple(out_specs), scratch_shapes=scratch,
+        out_shape=tuple(outs), in_specs=in_specs, out_specs=tuple(out_specs), scratch_shapes=scratch, input_output_aliases=aliases,
         compiler_params=pltpu.CompilerParams(collective_id=expert, has_side_effects=True, vmem_limit_bytes=63 * 2 ** 20),
         cost_estimate=cost(2 * rows * d_model * ff * 9, STREAM),
     )(*operands)
@@ -901,17 +918,16 @@
         slot_cap = 3 * n_local // n_exp
         wg_t, wu_t = jnp.swapaxes(w_gate, 1, 2), jnp.swapaxes(w_up, 1, 2)
 
-        columns = jnp.stack([exp_first, exp_second, slot_first, slot_second], axis=1)
-        picks = jnp.stack([exp_first, exp_second, slot_first, slot_second])
-        norm = jnp.stack([ln_weight, ln_bias]).astype(F32)
-        router_t = jnp.pad(router.T, ((0, LANES - n_exp), (0, 0)))
-        o, dh, share, *landed, hidden, stats, err_one, err_two = expert_call(
-            (eligible, columns, picks, norm, router_t, tok_x, tok_dy), wg_t, wu_t, w_down, 0, slot_cap, grid, n_ep)
-        o_next, dh_next, share, o, dh, held = expert_call((*landed, o, dh, share), wg_t, wu_t, w_down, 1, slot_cap, grid, n_ep)
+        lines = [x[None] for x in (exp_first, exp_second, slot_first, slot_second)]
+        lnw, lnb = ln_weight.astype(F32)[None], ln_bias.astype(F32)[None]
+        router_t = router.T
+        o, dh, share, *landed, hidden, held, stats, err_one, err_two = expert_call(
+            (eligible.T, *lines, lnw, lnb, router_t, tok_x, tok_dy), wg_t, wu_t, w_down, 0, slot_cap, grid, n_ep)
+        o_next, dh_next, share, o, dh, held = expert_call((*landed, o, dh, share, held), wg_t, wu_t, w_down, 1, slot_cap, grid, n_ep)
         gathered_next = lax.all_gather(share, 'dp')
         held, out_tok, dx_tok, small = tail_call(
             held, o_next, dh_next, tok_x, tok_dy, hidden, o, dh, stats, err_one, err_two,
-            norm, router_t, slot_cap, grid, local_exp + 1)
+            lnw, router_t, slot_cap, grid, local_exp + 1)
         gathered = [x.reshape((grid, grid) + share.shape) for x in (held, gathered_next)]
         d_router, d_ln_weight, d_ln_bias = small[:n_exp].T, small[PACK], small[PACK + 1]
         *weights, out_tok, dx_tok = assemble(gathered[0], 0, local_exp, (), (out_tok, dx_tok))

time: 487 us -> 487 us (level)
  local copies, waits for them, and re-layouts: 9.83 us -> 3.05 us
  Pallas kernels: 425 us -> 431 us
where the time goes in v5:
time: 487 us
  Pallas kernels  431 us (89%)
  waiting for transfers between devices  36.6 us (8%)
  between operations  14.1 us (3%)
    pallas_call x2, Pallas kernels, expert_call(): pl.pallas_call(functools.partial(expert_kernel, (expert, grid, chunk, cap...  272 us
    pallas_call x1, Pallas kernels, tail_call(): pl.pallas_call(functools.partial(tail_kernel, grid, cap), out_shape=(jax....  124 us
    all_gather x1, waiting for transfers between devices, local_step(): gathered_next = lax.all_gather(share, 'dp')  36.6 us
    pallas_call x2, Pallas kernels, assemble(): pl.pallas_call(assemble_kernel, grid=(grid, cut), out_shape=(whole,) * 3...  33.8 us
  transfers between devices with their start and end apart: 1, of which 1 were waited for; matrix products, arithmetic and copies ran while one was open for 0% of the time, Pallas kernels for 29%

profile of v5, /device:TPU:1, one launch (start us, length us, event | category | flops | bytes accessed | tf_op | source)
XLA Modules:
  0.0 486.9 jit_solution(15453777912676534562)
XLA Ops:
  7.2 0.0 all-gather.3.cloned.1.call-start
  7.2 1.3 broadcast_in_dim.30
  8.5 1.3 broadcast_in_dim.31
  9.8 180.6 %shard_map.188 = (bf16[384,4096]{1,0:T(8,128)(2,1)}, bf16[384,4096]{1,0:T(8,128)(2,1)}, f32[4,3,112,256]{3,2,1,0:T(8,128)}, bf16[384,4096]{1,0:T(8,128)(2,1)}, b...) custom-call(s32[16,256]{1,0:T(8,128)} %bitcast.37, ...), custom_call_target="tpu_custom_call" | custom-call | flops 12683575296 | bytes 30000000 | tf_op jit(solution)/shard_map/pallas_call | solution.py:865
  190.4 0.0 copy-start.1
  190.4 0.0 copy-start.2
  190.4 0.0 copy-start.3
  190.5 0.0 copy-start.4
  190.5 0.0 copy-start.5
  190.5 91.8 %shard_map.189 = (bf16[384,4096]{1,0:T(8,128)(2,1)}, bf16[384,4096]{1,0:T(8,128)(2,1)}, f32[4,3,112,256]{3,2,1,0:T(8,128)}, bf16[384,4096]{1,0:T(8,128)(2,1)}, b...) custom-call(bf16[384,4096]{1,0:T(8,128)(2,1)} %get-tuple-element.38.refs_0_, ...), custom_call_target="tpu_custom_call", output_to_operand_aliasing={{5}: (10, {})} | custom-call | flops 12683575296 | bytes 30000000 | tf_op jit(solution)/shard_map/pallas_call | solution.py:865
  282.3 0.0 all-gather.3.cloned.1.call-update
  282.4 0.0 copy-done.1
  282.4 0.0 copy-done.2
  282.4 0.0 copy-done.3
  282.4 0.0 copy-done.4
  282.4 0.0 copy-done.5
  282.4 124.3 %tail.1 = (f32[16,4,3,112,256]{4,3,2,1,0:T(8,128)}, bf16[256,4096]{1,0:T(8,128)(2,1)S(1)}, bf16[256,4096]{1,0:T(8,128)(2,1)}, f32[24,4096]{1,0:T(8,128)S(1)}) custom-call(f32[16,4,3,112,256]{4,3,2,1,0:T(8,128)} %get-tuple-element.46.refs_0_, bf16[384,4096]{1,0:T(8,128)(2,1)} %get-tuple-element.47.refs_1_, ...), custom_call_target="tpu_custom_call", output_to_operand_aliasing={{0}: (0, {})} | custom-call | flops 10000000000 | bytes 30000000 | tf_op jit(solution)/shard_map/tail/pallas_call | solution.py:305
  406.7 0.0 copy-start
  406.8 1.7 copy-done
  408.4 17.3 %shard_map.190 = (f32[2,448,4096]{2,1,0:T(8,128)}, f32[2,448,4096]{2,1,0:T(8,128)}, f32[2,448,4096]{2,1,0:T(8,128)}, bf16[256,4096]{1,0:T(8,128)(2,1)}, bf16[256,4096]{1,0:T(8,128)(2,1)}) custom-call(f32[4,4,4,3,112,256]{5,4,3,2,1,0:T(8,128)} %bitcast.22, f32[4,4,4,3,112,256]{5,4,3,2,1,0:T(8,128)} %bitcast.23, f32[4,4,4,3,112,256]{5,4,3,2,1,0:T(8,128)} %bitcast.24, ...), custom_call_target="tpu_custom_call" | custom-call | flops 1000000 | bytes 44000000 | tf_op jit(solution)/shard_map/pallas_call | solution.py:897
  425.8 0.6 fusion
  426.4 0.7 slice_bitcast_fusion
  427.1 36.6 %all-gather.3.cloned.1.call-done = f32[64,3,112,256]{3,2,1,0:T(8,128)} async-done(((f32[4,3,112,256]{3,2,1,0:T(8,128)}), f32[64,3,112,256]{3,2,1,0:T(8,128)}) %all-gather.3.cloned.1.call-update) | async-done | bytes 22020112 | tf_op jit(solution)/shard_map/all_gather | solution.py:927
  463.7 16.4 %shard_map.191 = (f32[2,448,4096]{2,1,0:T(8,128)}, f32[2,448,4096]{2,1,0:T(8,128)}, f32[2,448,4096]{2,1,0:T(8,128)}) custom-call(f32[4,4,4,3,112,256]{5,4,3,2,1,0:T(8,128)} %bitcast.25, f32[4,4,4,3,112,256]{5,4,3,2,1,0:T(8,128)} %bitcast.26, f32[4,4,4,3,112,256]{5,4,3,2,1,0:T(8,128)} %bitcast.27, ...), custom_call_target="tpu_custom_call", output_to_operand_aliasing={{0}: (3, {}), {1}: (4, {}), {2}: (5, {})} | custom-call | flops 1000000 | bytes 44000000 | tf_op jit(solution)/shard_map/pallas_call | solution.py:897
Async XLA Ops:
  7.2 456.5 %all-gather.3.cloned.1.call-start = ((), (), s32[]{:S(2)}) async-start(), calls=%async_computation | async-start | bytes 23396352 | tf_op jit(solution)/shard_map/all_gather | solution.py:927
  190.4 91.9 %copy-start.1 = (bf16[4096,16]{0,1:T(8,128)(2,1)S(1)}, bf16[4096,16]{0,1:T(8,128)(2,1)}, u32[]{:S(2)}) copy-start(bf16[4096,16]{0,1:T(8,128)(2,1)} %param.22) | copy-start | bytes 393220
  190.4 91.9 %copy-start.2 = (f32[256,128]{1,0:T(8,128)S(1)}, f32[256,128]{1,0:T(8,128)}, u32[]{:S(2)}) copy-start(f32[256,128]{1,0:T(8,128)} %get-tuple-element.52.refs_8_) | copy-start | bytes 393220
  190.4 91.9 %copy-start.3 = (f32[256,128]{1,0:T(8,128)S(1)}, f32[256,128]{1,0:T(8,128)}, u32[]{:S(2)}) copy-start(f32[256,128]{1,0:T(8,128)} %get-tuple-element.53.refs_9_) | copy-start | bytes 393220
  190.5 91.9 %copy-start.4 = (f32[256,128]{1,0:T(8,128)S(1)}, f32[256,128]{1,0:T(8,128)}, u32[]{:S(2)}) copy-start(f32[256,128]{1,0:T(8,128)} %get-tuple-element.54.refs_10_) | copy-start | bytes 393220
  190.5 91.9 %copy-start.5 = (f32[4096]{0:T(1024)S(1)}, f32[4096]{0:T(1024)}, u32[]{:S(2)}) copy-start(f32[4096]{0:T(1024)} %broadcast_in_dim.30) | copy-start | bytes 49156
  406.7 1.7 copy-start
Sparse Core Ops, SparseCore 0:
  282.5 181.1 all-gather.2

commit v6 on v4

--- a/solution.py
+++ b/solution.py
@@ -79,6 +79,11 @@
         pl.semaphore_wait(pltpu.get_barrier_semaphore(), self.arrive() if signals is None else signals)
 
 
+def widen(out, rows):
+    out[ALL] = jnp.zeros_like(out)
+    out[:rows.shape[0], :] = rows
+
+
 def cost(flops, size):
     return pl.CostEstimate(flops=flops, bytes_accessed=size, transcendentals=0)
 
@@ -137,9 +142,9 @@
 def tail_kernel(grid, cap, *refs):
     refs = list(refs)
     take = lambda n: [refs.pop(0) for _ in range(n)]
-    _, o_next_h, dh_next_h, x_h, dy_h, hid_h, o_h, dh_h, stats, err_one, err_two, lnw, router = take(13)
+    _, o_next_h, dh_next_h, x_h, dy_h, hid_h, o_h, dh_h, stats, err_one, err_two, lnw, router_in = take(13)
     held, out, dx, small = take(4)
-    x_v, dy_v, hid_v, o_v, dh_v, sel_one, sel_two, grad_h, val = take(9)
+    x_v, dy_v, hid_v, o_v, dh_v, sel_one, sel_two, grad_h, val, router = take(10)
     first, second, third, c_one, c_two, c_three = take(6)
     loc, sp_s, sp_r, ba_s, ba_r, s_one, r_one, s_two, r_two, s_three, r_three, s_four, r_four = take(13)
     n_tok, d_model = x_v.shape
@@ -174,6 +179,7 @@
         (x_h, x_v), (dy_h, dy_v), (hid_h, hid_v), (o_h, o_v.at[home, :]), (dh_h, dh_v.at[home, :])))]
     for c in loads:
         c.start()
+    widen(router, router_in[ALL])
     slots = lax.broadcasted_iota(jnp.int32, (n_tok, 2 * rows), 1)
     sel_one[ALL] = (slots == stats[:, 4:5].astype(jnp.int32)).astype(F32).astype(BF16)
     sel_two[ALL] = (slots == stats[:, 5:6].astype(jnp.int32)).astype(F32).astype(BF16)
@@ -215,7 +221,7 @@
         d_weight = jnp.sum(grad * x_hat, axis=0, **KEEP)
         d_bias = jnp.sum(grad, axis=0, **KEEP)
         val[PACK:SMALL, cols] = jnp.where(row == 0, d_weight, jnp.where(row == 1, d_bias, 0.0))
-        scaled = grad * lnw[0:1, cols]
+        scaled = grad * lnw[:, cols]
         return sums[0] + jnp.sum(scaled, axis=1, **KEEP), sums[1] + jnp.sum(scaled * x_hat, axis=1, **KEEP)
 
     mean_one, mean_two = lax.fori_loop(0, d_model // wide, gradient, (zero, zero))
@@ -251,7 +257,7 @@
     def _(i):
         cols = rows_at(i * wide, wide, LANES)
         x_hat = (x_v[:, cols].astype(F32) - mean) * inv_std
-        step = inv_std * (grad_h[:, cols] * lnw[0:1, cols] - mean_one - x_hat * mean_two)
+        step = inv_std * (grad_h[:, cols] * lnw[:, cols] - mean_one - x_hat * mean_two)
         dx[:, cols] = (dy_v[:, cols].astype(F32) + step).astype(BF16)
 
     for k in range(n_peer):
@@ -301,7 +307,7 @@
         out_shape=(jax.ShapeDtypeStruct(held.shape, F32), tokens, tokens, jax.ShapeDtypeStruct((SMALL, d_model), F32)),
         in_specs=[hbm] * 8 + [on_chip] * 5, out_specs=(hbm, on_chip, on_chip, on_chip), input_output_aliases={0: 0},
         scratch_shapes=[vmem((n_tok, d_model), BF16)] * 3 + [vmem((2 * rows, d_model), BF16)] * 2
-        + [vmem((n_tok, 2 * rows), BF16)] * 2 + [vmem((n_tok, d_model), F32), vmem((SMALL, d_model), F32)]
+        + [vmem((n_tok, 2 * rows), BF16)] * 2 + [vmem((n_tok, d_model), F32), vmem((SMALL, d_model), F32), vmem((LANES, d_model), BF16)]
         + [vmem((n_ep, SMALL, width), F32), vmem((grid, SMALL, width), F32), vmem((grid, SMALL, width), F32)] + [vmem((SMALL, width), F32)] * 3
         + [dma((7,)), deep, deep, both, both,
            peers, peers, ring, ring, ring, ring, peers, peers],
@@ -316,7 +322,8 @@
     refs = list(refs)
     take = lambda n: [refs.pop(0) for _ in range(n)]
     if first:
-        marks, columns, picks, norm, router, x_h, dy_h, wg_h, wu_h, wd_h = take(10)
+        marks, *lines = take(1 + UNITS)
+        lnw, lnb, router_in, x_h, dy_h, wg_h, wu_h, wd_h = take(8)
         o_h, dh_h, sh_h, h_next, q_next, hsl_next, qsl_next, hid_h, stats, err_one, err_two = take(11)
     else:
         h_next, q_next, hsl_next, qsl_next, wg_h, wu_h, wd_h, *carry = take(9)
@@ -326,7 +333,7 @@
     h_recv, q_recv, wg, wu, wd, a_t, b_t, d_t, u_all, da_all, db_all, h_sl, q_sl, dw, rsb, act, act_b, eye = take(18)
     loc, hs_s, hs_r, qs_s, qs_r, ga_s, ga_r, rs_s, rs_r = take(9)
     if first:
-        sel_h, sel_q, sel_h_next, sel_q_next, hidden, grad_one, grad_two, h_send, q_send, h_send_next, q_send_next = take(11)
+        sel_h, sel_q, sel_h_next, sel_q_next, hidden, grad_one, grad_two, h_send, q_send, h_send_next, q_send_next, router, wide_table = take(13)
         xh_s, xh_r, xq_s, xq_r, nh_s, nh_r, nq_s, nq_r, ns_h_s, ns_h_r, ns_q_s, ns_q_r, lin = take(13)
         o_v, dh_v = h_send, q_send
     else:
@@ -510,18 +517,19 @@
         inputs = [pltpu.make_async_copy(src, dst, lin.at[i]) for i, (src, dst) in enumerate(((x_h, hidden), (dy_h, grad_two)))]
         n_tok = hidden.shape[0]
         lane = lax.broadcasted_iota(jnp.int32, stats.shape, 1)
+        n_exp = router_in.shape[0]
         for c in inputs:
             c.start()
         signals = here.arrive()
-
-        def place(table, i):
-            ids, slots = [table[j:j + 1, :] if table is picks else table[:, j:j + 1] for j in (i, i + 2)]
+        make_eye()
+
+        def place(ids, slots):
             local = jnp.bitwise_and(ids, 1)
             return jnp.where(slots >= 0, local * rows + jnp.right_shift(ids, 1) * cap + slots, -1)
 
         for e, (one, two) in enumerate(((sel_h, sel_q), (sel_h_next, sel_q_next))):
             slot = lax.broadcasted_iota(jnp.int32, one.shape, 0) + e * rows
-            hits = [(slot == place(picks, i)).astype(F32).astype(BF16) for i in range(2)]
+            hits = [(slot == place(lines[i][ALL], lines[i + 2][ALL])).astype(F32).astype(BF16) for i in range(2)]
             one[ALL] = hits[0] + hits[1]
             for i in range(2):
                 two[:, i * n_tok:(i + 1) * n_tok] = hits[i]
@@ -535,7 +543,7 @@
             mean = jnp.mean(x, axis=1, **KEEP)
             centered = x - mean
             inv_std = lax.rsqrt(jnp.mean(centered * centered, axis=1, **KEEP) + LN_EPS)
-            hidden[r, :] = (centered * inv_std * norm[0:1, :] + norm[1:, :]).astype(BF16)
+            hidden[r, :] = (centered * inv_std * lnw[ALL] + lnb[ALL]).astype(BF16)
             at = lane[:strip_rows]
             stats[r, :] = jnp.where(at == 2, mean, jnp.where(at == 3, inv_std, 0.0))
 
@@ -543,12 +551,16 @@
         hid_out.start()
 
         def gates():
+            widen(router, router_in[ALL])
+            row = lax.broadcasted_iota(jnp.int32, marks.shape, 0)
+            index_rows = sum(jnp.where(row == i, lines[i][ALL], 0) for i in range(UNITS))
+            widen(wide_table, jnp.concatenate([marks[ALL], index_rows]).astype(F32).astype(BF16))
+            columns = lax.dot_general(eye[:n_tok, :n_tok], wide_table[ALL], NT, preferred_element_type=F32)
             logits = lax.dot_general(hidden[ALL], router[ALL], NT, preferred_element_type=F32)
-            choices = [columns[:, i:i + 1] for i in range(2)]
-            err_one[ALL] = jnp.zeros_like(err_one)
-            err_one[:, :marks.shape[1]] = marks[ALL].astype(F32)
-            allowed = err_one[ALL] > 0
-            found = [place(columns, i).astype(F32) for i in range(2)]
+            ints = [columns[:, n_exp + i:n_exp + i + 1].astype(jnp.int32) for i in range(UNITS)]
+            choices, allowed = ints[:2], jnp.logical_and(columns > 0, lane < n_exp)
+            found = [place(*ints[i::2]) for i in range(2)]
+            found = [value.astype(F32) for value in found]
             for choice, err in zip(choices, (err_one, err_two)):
                 masked = jnp.where(allowed, logits, -1e30)
                 weight = jnp.exp(masked - jnp.max(masked, axis=1, **KEEP))
@@ -626,8 +638,6 @@
             gather(what[0], what[1], what[3], ep)
             if not i:
                 gates()
-        make_eye()
-
         spread = (('y', h_recv, h_sl, hs_s, hs_r), ('z', q_recv, q_sl, qs_s, qs_r))
         spread_next = (('y', h_next, hsl_next, ns_h_s, ns_h_r), ('z', q_next, qsl_next, ns_q_s, ns_q_r))
 
@@ -834,10 +844,10 @@
         tokens = inputs[-1].shape
         n_tok = tokens[0]
         scratch += [vmem((rows, i * n_tok), BF16) for i in (1, 2, 1, 2)] + [vmem(tokens, BF16)] * 3
-        scratch += [vmem(row_block, BF16)] * 4 + [dma((n_peer,))] * 8 + [dma((grid,))] * 4 + [dma((9,))]
+        scratch += [vmem(row_block, BF16)] * 4 + [vmem((LANES, d_model), BF16), vmem((LANES, n_tok), BF16)] + [dma((n_peer,))] * 8 + [dma((grid,))] * 4 + [dma((9,))]
         operands = (*inputs, w_gate, w_up, w_down)
         outs += [out(row_block), out(row_block), out(slice_block), out(slice_block), out(tokens)] + [out((n_tok, LANES), F32)] * 3
-        in_specs, out_specs = [on_chip] * 5 + [hbm] * 5, [hbm] * 8 + [on_chip] * 3
+        in_specs, out_specs = [on_chip] * 8 + [hbm] * 5, [hbm] * 8 + [on_chip] * 3
     else:
         h_next, q_next, hsl_next, qsl_next, *carry, done = inputs
         scratch += [vmem(row_block, BF16)] * 2 + [dma((2, n_peer))] * 2 + [dma((2,)), dma((2 + 2 * grid,))]
@@ -901,17 +911,16 @@
         slot_cap = 3 * n_local // n_exp
         wg_t, wu_t = jnp.swapaxes(w_gate, 1, 2), jnp.swapaxes(w_up, 1, 2)
 
-        columns = jnp.stack([exp_first, exp_second, slot_first, slot_second], axis=1)
-        picks = jnp.stack([exp_first, exp_second, slot_first, slot_second])
-        norm = jnp.stack([ln_weight, ln_bias]).astype(F32)
-        router_t = jnp.pad(router.T, ((0, LANES - n_exp), (0, 0)))
+        lines = [x[None] for x in (exp_first, exp_second, slot_first, slot_second)]
+        lnw, lnb = ln_weight.astype(F32)[None], ln_bias.astype(F32)[None]
+        router_t = router.T
         o, dh, share, *landed, hidden, stats, err_one, err_two = expert_call(
-            (eligible, columns, picks, norm, router_t, tok_x, tok_dy), wg_t, wu_t, w_down, 0, slot_cap, grid, n_ep)
+            (eligible.T, *lines, lnw, lnb, router_t, tok_x, tok_dy), wg_t, wu_t, w_down, 0, slot_cap, grid, n_ep)
         o_next, dh_next, share, o, dh, held = expert_call((*landed, o, dh, share), wg_t, wu_t, w_down, 1, slot_cap, grid, n_ep)
         gathered_next = lax.all_gather(share, 'dp')
         held, out_tok, dx_tok, small = tail_call(
             held, o_next, dh_next, tok_x, tok_dy, hidden, o, dh, stats, err_one, err_two,
-            norm, router_t, slot_cap, grid, local_exp + 1)
+            lnw, router_t, slot_cap, grid, local_exp + 1)
         gathered = [x.reshape((grid, grid) + share.shape) for x in (held, gathered_next)]
         d_router, d_ln_weight, d_ln_bias = small[:n_exp].T, small[PACK], small[PACK + 1]
         *weights, out_tok, dx_tok = assemble(gathered[0], 0, local_exp, (), (out_tok, dx_tok))

time: 487 us -> 480 us (0.986)
  local copies, waits for them, and re-layouts: 9.83 us -> 2.99 us
where the time goes in v6:
time: 480 us; the launch traced here: 479 us
  Pallas kernels  424 us (88%)
  waiting for transfers between devices  35.5 us (7%)
  between operations  14.1 us (3%)
    pallas_call x2, Pallas kernels, expert_call(): pl.pallas_call(functools.partial(expert_kernel, (expert, grid, chunk, cap...  267 us
    pallas_call x1, Pallas kernels, tail_call(): pl.pallas_call(functools.partial(tail_kernel, grid, cap), out_shape=(jax....  123 us
    all_gather x1, waiting for transfers between devices, local_step(): gathered_next = lax.all_gather(share, 'dp')  35.5 us
    pallas_call x2, Pallas kernels, assemble(): pl.pallas_call(assemble_kernel, grid=(grid, cut), out_shape=(whole,) * 3...  33.8 us
  transfers between devices with their start and end apart: 1, of which 1 were waited for; matrix products, arithmetic and copies ran while one was open for 0% of the time, Pallas kernels for 29%

profile of v6, /device:TPU:1, one launch (start us, length us, event | category | flops | bytes accessed | tf_op | source)
XLA Modules:
  0.0 479.1 jit_solution(2927921484749064883)
XLA Ops:
  7.2 0.0 all-gather.3.cloned.1.call-start
  7.2 1.3 broadcast_in_dim.30
  8.5 1.3 broadcast_in_dim.31
  9.8 163.8 %shard_map.188 = (bf16[384,4096]{1,0:T(8,128)(2,1)}, bf16[384,4096]{1,0:T(8,128)(2,1)}, f32[4,3,112,256]{3,2,1,0:T(8,128)}, bf16[384,4096]{1,0:T(8,128)(2,1)}, b...) custom-call(s32[16,256]{1,0:T(8,128)} %bitcast.37, ...), custom_call_target="tpu_custom_call" | custom-call | flops 12683575296 | bytes 30000000 | tf_op jit(solution)/shard_map/pallas_call | solution.py:858
  173.6 0.0 copy-start.1
  173.6 0.0 copy-start.2
  173.6 0.0 copy-start.3
  173.7 0.0 copy-start.4
  173.7 0.0 copy-start.5
  173.7 103.3 %shard_map.189 = (bf16[384,4096]{1,0:T(8,128)(2,1)}, bf16[384,4096]{1,0:T(8,128)(2,1)}, f32[4,3,112,256]{3,2,1,0:T(8,128)}, bf16[384,4096]{1,0:T(8,128)(2,1)}, b...) custom-call(bf16[384,4096]{1,0:T(8,128)(2,1)} %get-tuple-element.37.refs_0_, ...), custom_call_target="tpu_custom_call" | custom-call | flops 12683575296 | bytes 30000000 | tf_op jit(solution)/shard_map/pallas_call | solution.py:858
  277.0 0.0 all-gather.3.cloned.1.call-update
  277.1 0.0 copy-done.1
  277.1 0.0 copy-done.2
  277.1 0.0 copy-done.3
  277.1 0.0 copy-done.4
  277.1 0.0 copy-done.5
  277.1 122.9 %tail.1 = (f32[16,4,3,112,256]{4,3,2,1,0:T(8,128)}, bf16[256,4096]{1,0:T(8,128)(2,1)S(1)}, bf16[256,4096]{1,0:T(8,128)(2,1)}, f32[24,4096]{1,0:T(8,128)S(1)}) custom-call(f32[16,4,3,112,256]{4,3,2,1,0:T(8,128)} %get-tuple-element.44.refs_0_, bf16[384,4096]{1,0:T(8,128)(2,1)} %get-tuple-element.45.refs_1_, ...), custom_call_target="tpu_custom_call", output_to_operand_aliasing={{0}: (0, {})} | custom-call | flops 10000000000 | bytes 30000000 | tf_op jit(solution)/shard_map/tail/pallas_call | solution.py:305
  400.0 0.0 copy-start
  400.0 1.6 copy-done
  401.6 17.4 %shard_map.190 = (f32[2,448,4096]{2,1,0:T(8,128)}, f32[2,448,4096]{2,1,0:T(8,128)}, f32[2,448,4096]{2,1,0:T(8,128)}, bf16[256,4096]{1,0:T(8,128)(2,1)}, bf16[256,4096]{1,0:T(8,128)(2,1)}) custom-call(f32[4,4,4,3,112,256]{5,4,3,2,1,0:T(8,128)} %bitcast.22, f32[4,4,4,3,112,256]{5,4,3,2,1,0:T(8,128)} %bitcast.23, f32[4,4,4,3,112,256]{5,4,3,2,1,0:T(8,128)} %bitcast.24, ...), custom_call_target="tpu_custom_call" | custom-call | flops 1000000 | bytes 44000000 | tf_op jit(solution)/shard_map/pallas_call | solution.py:890
  419.0 0.6 fusion
  419.7 0.7 slice_bitcast_fusion
  420.4 35.5 %all-gather.3.cloned.1.call-done = f32[64,3,112,256]{3,2,1,0:T(8,128)} async-done(((f32[4,3,112,256]{3,2,1,0:T(8,128)}), f32[64,3,112,256]{3,2,1,0:T(8,128)}) %all-gather.3.cloned.1.call-update) | async-done | bytes 22020112 | tf_op jit(solution)/shard_map/all_gather | solution.py:920
  455.8 16.4 %shard_map.191 = (f32[2,448,4096]{2,1,0:T(8,128)}, f32[2,448,4096]{2,1,0:T(8,128)}, f32[2,448,4096]{2,1,0:T(8,128)}) custom-call(f32[4,4,4,3,112,256]{5,4,3,2,1,0:T(8,128)} %bitcast.25, f32[4,4,4,3,112,256]{5,4,3,2,1,0:T(8,128)} %bitcast.26, f32[4,4,4,3,112,256]{5,4,3,2,1,0:T(8,128)} %bitcast.27, ...), custom_call_target="tpu_custom_call", output_to_operand_aliasing={{0}: (3, {}), {1}: (4, {}), {2}: (5, {})} | custom-call | flops 1000000 | bytes 44000000 | tf_op jit(solution)/shard_map/pallas_call | solution.py:890
Async XLA Ops:
  7.2 448.7 %all-gather.3.cloned.1.call-start = ((), (), s32[]{:S(2)}) async-start(), calls=%async_computation | async-start | bytes 23396352 | tf_op jit(solution)/shard_map/all_gather | solution.py:920
  173.6 103.4 %copy-start.1 = (bf16[4096,16]{0,1:T(8,128)(2,1)S(1)}, bf16[4096,16]{0,1:T(8,128)(2,1)}, u32[]{:S(2)}) copy-start(bf16[4096,16]{0,1:T(8,128)(2,1)} %param.22) | copy-start | bytes 393220
  173.6 103.4 %copy-start.2 = (f32[256,128]{1,0:T(8,128)S(1)}, f32[256,128]{1,0:T(8,128)}, u32[]{:S(2)}) copy-start(f32[256,128]{1,0:T(8,128)} %get-tuple-element.50.refs_8_) | copy-start | bytes 393220
  173.6 103.4 %copy-start.3 = (f32[256,128]{1,0:T(8,128)S(1)}, f32[256,128]{1,0:T(8,128)}, u32[]{:S(2)}) copy-start(f32[256,128]{1,0:T(8,128)} %get-tuple-element.51.refs_9_) | copy-start | bytes 393220
  173.7 103.4 %copy-start.4 = (f32[256,128]{1,0:T(8,128)S(1)}, f32[256,128]{1,0:T(8,128)}, u32[]{:S(2)}) copy-start(f32[256,128]{1,0:T(8,128)} %get-tuple-element.52.refs_10_) | copy-start | bytes 393220
  173.7 103.4 %copy-start.5 = (f32[4096]{0:T(1024)S(1)}, f32[4096]{0:T(1024)}, u32[]{:S(2)}) copy-start(f32[4096]{0:T(1024)} %broadcast_in_dim.30) | copy-start | bytes 49156
  400.0 1.6 copy-start
Sparse Core Ops, SparseCore 0:
  277.2 178.6 all-gather.2
